TPU v7x, 32 devices: a whole 2x2x4 slice. The times are simulated.
32 devices in a mesh: gx: 4 (over y, x), gy: 2 (over core), gz: 4 (over z).
Axes of the slice: x: 2, y: 2, z: 4, core: 2. Of those that a mesh axis runs over, the one named last changes fastest.
Arguments:
- right_side: float32 [8, 32, 64, 512], P(None, 'gx', 'gy', 'gz'), may hold values from -12 to 12
- shift: float32 [32, 64, 512], P('gx', 'gy', 'gz'), may hold values from 0.02 to 2
Outputs:
- solution_block: float32 [8, 32, 64, 512], P(None, 'gx', 'gy', 'gz')
- residual_norms: float32 [8], replicated
All inputs are finite; a program needn't handle non-finite values.
Results may differ from a plain program's by a relative error of at most 0.0003.
Values sent between devices are 32-bit elements; how exact they have to be, the bound alone decides.
No kernel may reach another device: no remote copies, remote signals or barrier semaphores. Data moves between devices by JAX's collectives and lax.ppermute only.
A program may use at most 128 MiB of HBM per device.

v0:
```python
import jax
import jax.numpy as jnp
from jax import lax
from jax.sharding import PartitionSpec as P

ITERS = 2


def padded_2(block, sides, width):
    for axis, dim in sides:
        count = lax.axis_size(axis)
        forward = [(i, i + 1) for i in range(count - 1)]
        backward = [(target, source) for source, target in forward]
        low = lax.ppermute(
            lax.slice_in_dim(block, block.shape[dim] - width, None, axis=dim), axis, forward
        )
        high = lax.ppermute(lax.slice_in_dim(block, 0, width, axis=dim), axis, backward)
        block = jnp.concatenate([low, block, high], axis=dim)
    return block


def operate(fields, shift):
    padded = padded_2(fields, (("gx", 1), ("gy", 2), ("gz", 3)), 1)
    beside = padded[:, 2:, 1:-1, 1:-1] + padded[:, :-2, 1:-1, 1:-1]
    beside = beside + padded[:, 1:-1, 2:, 1:-1] + padded[:, 1:-1, :-2, 1:-1]
    beside = beside + padded[:, 1:-1, 1:-1, 2:] + padded[:, 1:-1, 1:-1, :-2]
    return (6.0 + shift)[None] * fields - beside


def lower_inverse(lower):
    count = lower.shape[0]
    return jax.scipy.linalg.solve_triangular(lower, jnp.eye(count, dtype=lower.dtype), lower=True)


def small_dot(left, right):
    return jnp.dot(left, right, precision=lax.Precision.HIGHEST)


def body(right_side, shift):
    width = right_side.shape[0]
    shape = right_side.shape
    rows = right_side.reshape(width, -1)
    gram = lax.psum(small_dot(rows, rows.T), ("gx", "gy", "gz"))
    lower = jnp.linalg.cholesky(gram)
    start_coeff = lower.T
    basis = [small_dot(lower_inverse(lower), rows)]
    hessen = jnp.zeros(((ITERS + 1) * width, ITERS * width), jnp.float32)
    for step in range(ITERS):
        image = operate(basis[step].reshape(shape), shift).reshape(width, -1)
        stacked = jnp.concatenate(basis, axis=0)
        products = lax.psum(
            small_dot(jnp.concatenate([stacked, image], axis=0), image.T), ("gx", "gy", "gz")
        )
        coeffs = products[:-width]
        gram = products[-width:] - small_dot(coeffs.T, coeffs)
        projected = image - small_dot(coeffs.T, stacked)
        lower = jnp.linalg.cholesky(gram)
        hessen = hessen.at[: (step + 1) * width, step * width : (step + 1) * width].set(coeffs)
        hessen = hessen.at[
            (step + 1) * width : (step + 2) * width, step * width : (step + 1) * width
        ].set(lower.T)
        if step + 1 < ITERS:
            basis.append(small_dot(lower_inverse(lower), projected))
    target = jnp.zeros(((ITERS + 1) * width, width), jnp.float32).at[:width].set(start_coeff)
    normal = small_dot(hessen.T, hessen)
    factor = jnp.linalg.cholesky(normal)
    coeff_y = jax.scipy.linalg.cho_solve((factor, True), small_dot(hessen.T, target))
    solution = small_dot(coeff_y.T, jnp.concatenate(basis, axis=0)).reshape(shape)
    leftover = target - small_dot(hessen, coeff_y)
    norms = jnp.sqrt(jnp.sum(leftover * leftover, axis=0))
    return (solution, norms)


def solution(mesh):
    in_specs = (P(None, "gx", "gy", "gz"), P("gx", "gy", "gz"))
    out_specs = (P(None, "gx", "gy", "gz"), P())
    return jax.shard_map(body, mesh=mesh, in_specs=in_specs, out_specs=out_specs, check_vma=False)
```

profile of v0, /device:TPU:0, one launch (start us, length us, event | category | flops | bytes accessed | tf_op | source)
XLA Modules:
  0.0 228.1 jit_solution(12695287434098205644)
XLA Ops:
  0.6 4.9 %convolution_bitcast_fusion = f32[8,8]{0,1:T(8,128)S(1)} fusion(f32[8,8,32,128]{3,2,1,0:T(8,128)} %param.15), kind=kOutput, calls=%fused_computation.19 | convolution fusion | flops 25165824 | bytes 1048832 | tf_op jit(solution)/shard_map/dot_general | solution.py:36
  5.5 42.0 %psum.21 = f32[8,8]{0,1:T(8,128)S(1)} all-reduce(f32[8,8]{0,1:T(8,128)S(1)} %convolution_bitcast_fusion), channel_id=1, replica_groups=mesh['gx'=4,'gy'=2,'gz'=4] {'gx','gy','gz'}, use_global_device_ids=true, to_apply=%region_0.0 | all-reduce | flops 64 | bytes 512 | tf_op jit(solution)/shard_map/psum | solution.py:43
  47.5 0.7 cholesky.94
  50.4 1.5 fusion.12
  51.9 1.3 collective-permute-start
  53.2 4.8 %collective-permute-start.1 = (f32[8,1,32,128]{3,0,2,1:T(8,128)S(1)}, f32[8,1,32,128]{3,0,2,1:T(8,128)S(1)}, u32[]{:S(2)}, u32[]{:S(2)}) collective-permute-start(f32[8,1,32,128]{3,0,2,1:T(8,128)S(1)} %get-tuple-element.84), channel_id=1, source_target_pairs={{0,8},{8,16},{16,24},{1,9},{9,17},{17,25},{2,10},{10,18},{18,26},{... | collective-permute-start | bytes 393224 | tf_op jit(solution)/shard_map/ppermute | solution.py:14
  58.1 1.0 collective-permute-done
  59.1 1.5 collective-permute-done.1
  60.6 1.3 collective-permute-start.2
  61.9 3.0 %collective-permute-start.3 = (f32[8,10,1,128]{3,0,2,1:T(8,128)S(1)}, f32[8,10,1,128]{3,0,2,1:T(8,128)S(1)}, u32[]{:S(2)}, u32[]{:S(2)}) collective-permute-start(f32[8,10,1,128]{3,0,2,1:T(8,128)S(1)} %get-tuple-element.80), channel_id=1, source_target_pairs={{0,4},{1,5},{2,6},{3,7},{8,12},{9,13},{10,14},{11,15},{16,20},{17,... | collective-permute-start | bytes 122888 | tf_op jit(solution)/shard_map/ppermute | solution.py:14
  64.9 0.8 collective-permute-done.3
  66.4 1.5 fusion.56
  67.9 2.0 copy.130
  70.0 1.3 collective-permute-start.4
  71.2 0.7 copy.132
  71.9 4.5 %collective-permute-start.5 = (f32[8,10,34,1]{2,0,3,1:T(8,128)S(1)}, f32[8,10,34,1]{2,0,3,1:T(8,128)S(1)}, u32[]{:S(2)}, u32[]{:S(2)}) collective-permute-start(f32[8,10,34,1]{2,0,3,1:T(8,128)S(1)} %copy.132), channel_id=1, source_target_pairs={{0,1},{1,2},{2,3},{4,5},{5,6},{6,7},{8,9},{9,10},{10,11},{12,13},{... | collective-permute-start | bytes 32648 | tf_op jit(solution)/shard_map/ppermute | solution.py:14
  77.1 0.7 copy.131
  78.1 1.8 copy.133
  79.9 3.0 %fusion.22 = f32[8,8,32,128]{3,0,2,1:T(8,128)S(1)} fusion(f32[8,10,34,1]{3,0,2,1:T(8,128)} %copy.133, f32[8,10,1,128]{3,0,2,1:T(8,128)S(1)} %collective-permute-done.2, f32[8,10,1,128]{3,0,2,1:T(8,128)} %copy-done.6, f32[8,1,32,128]{3,0,2,1:T(8,128)} %copy-done.3, f32[8,8,32,128]{3,0,2,1:T(8,128)S(1)} %bitcast.73, f32[8,1,32,128]{3,0,2,1:T(8,128)} %copy-done.4, ...), kind=kLoop, calls=%fused_computation.50 | loop fusion | flops 6553600 | bytes 2594048 | tf_op jit(solution)/shard_map/sub | solution.py:27
  82.9 2.6 %fusion.6 = f32[16,8]{0,1:T(8,128)S(1)} fusion(f32[8,32768]{1,0:T(8,128)S(1)} %bitcast.78, f32[8,32768]{1,0:T(8,128)S(1)} %fusion.12), kind=kOutput, calls=%fused_computation.9 | convolution fusion | flops 50855936 | bytes 2097664 | tf_op jit(solution)/shard_map/dot_general | solution.py:36
  85.5 43.2 %psum.22 = f32[16,8]{0,1:T(8,128)S(1)} all-reduce(f32[16,8]{0,1:T(8,128)S(1)} %fusion.6), channel_id=1, replica_groups=mesh['gx'=4,'gy'=2,'gz'=4] {'gx','gy','gz'}, use_global_device_ids=true, to_apply=%region_3.0 | all-reduce | flops 128 | bytes 1024 | tf_op jit(solution)/shard_map/psum | solution.py:51
  128.6 1.0 convolution_subtract_fusion
  129.8 0.7 cholesky.105
  132.7 1.0 fusion.60
  133.7 1.3 collective-permute-start.6
  135.0 4.8 %collective-permute-start.7 = (f32[8,1,32,128]{3,0,2,1:T(8,128)S(1)}, f32[8,1,32,128]{3,0,2,1:T(8,128)S(1)}, u32[]{:S(2)}, u32[]{:S(2)}) collective-permute-start(f32[8,1,32,128]{3,0,2,1:T(8,128)S(1)} %get-tuple-element.82), channel_id=1, source_target_pairs={{0,8},{8,16},{16,24},{1,9},{9,17},{17,25},{2,10},{10,18},{18,26},{... | collective-permute-start | bytes 393224 | tf_op jit(solution)/shard_map/ppermute | solution.py:14
  139.9 1.2 collective-permute-done.6
  141.1 1.3 collective-permute-done.7
  142.4 1.3 collective-permute-start.8
  143.7 3.0 %collective-permute-start.9 = (f32[8,10,1,128]{3,0,2,1:T(8,128)S(1)}, f32[8,10,1,128]{3,0,2,1:T(8,128)S(1)}, u32[]{:S(2)}, u32[]{:S(2)}) collective-permute-start(f32[8,10,1,128]{3,0,2,1:T(8,128)S(1)} %get-tuple-element.78), channel_id=1, source_target_pairs={{0,4},{1,5},{2,6},{3,7},{8,12},{9,13},{10,14},{11,15},{16,20},{17,... | collective-permute-start | bytes 122888 | tf_op jit(solution)/shard_map/ppermute | solution.py:14
  146.7 0.8 collective-permute-done.9
  148.3 1.5 fusion.55
  149.8 2.6 %copy.137 = f32[8,10,34,1]{2,0,3,1:T(8,128)} copy(f32[8,10,34,1]{3,0,2,1:T(8,128)} %get-tuple-element.74) | data formatting | bytes 21760 | tf_op jit(solution)/shard_map/slice | solution.py:17
  152.4 1.3 collective-permute-start.10
  153.7 1.3 copy.139
  155.0 5.2 %collective-permute-start.11 = (f32[8,10,34,1]{2,0,3,1:T(8,128)}, f32[8,10,34,1]{2,0,3,1:T(8,128)}, u32[]{:S(2)}, u32[]{:S(2)}) collective-permute-start(f32[8,10,34,1]{2,0,3,1:T(8,128)} %copy.139), channel_id=1, source_target_pairs={{0,1},{1,2},{2,3},{4,5},{5,6},{6,7},{8,9},{9,10},{10,11},{12,13},{... | collective-permute-start | bytes 32648 | tf_op jit(solution)/shard_map/ppermute | solution.py:14
  161.8 1.5 copy.138
  163.3 2.6 %copy.140 = f32[8,10,34,1]{3,0,2,1:T(8,128)} copy(f32[8,10,34,1]{2,0,3,1:T(8,128)} %collective-permute-done.11) | data formatting | bytes 21760 | tf_op jit(solution)/shard_map/ppermute | solution.py:14
  165.8 3.0 %fusion.16 = f32[8,8,32,128]{3,0,2,1:T(8,128)S(1)} fusion(f32[8,10,34,1]{3,0,2,1:T(8,128)} %copy.140, f32[8,10,1,128]{3,0,2,1:T(8,128)S(1)} %collective-permute-done.8, f32[8,10,1,128]{3,0,2,1:T(8,128)} %copy-done.5, f32[8,1,32,128]{3,0,2,1:T(8,128)} %copy-done.1, f32[8,8,32,128]{3,0,2,1:T(8,128)S(1)} %bitcast.77, f32[8,1,32,128]{3,0,2,1:T(8,128)} %copy-done.2, ...), kind=kLoop, calls=%fused_computation.26 | loop fusion | flops 6553600 | bytes 2594048 | tf_op jit(solution)/shard_map/sub | solution.py:27
  168.9 3.0 %fusion = f32[24,8]{0,1:T(8,128)S(1)} fusion(f32[8,32768]{1,0:T(8,128)S(1)} %bitcast.82, f32[8,32768]{1,0:T(8,128)S(1)} %fusion.60, f32[8,32768]{1,0:T(8,128)S(1)} %fusion.12), kind=kOutput, calls=%fused_computation.1 | convolution fusion | flops 77070336 | bytes 3146496 | tf_op jit(solution)/shard_map/dot_general | solution.py:36
  171.9 42.0 %psum.23 = f32[24,8]{0,1:T(8,128)S(1)} all-reduce(f32[24,8]{0,1:T(8,128)S(1)} %fusion), channel_id=1, replica_groups=mesh['gx'=4,'gy'=2,'gz'=4] {'gx','gy','gz'}, use_global_device_ids=true, to_apply=%region_5.0 | all-reduce | flops 192 | bytes 1536 | tf_op jit(solution)/shard_map/psum | solution.py:51
  214.0 0.7 cholesky.116
  216.1 2.0 dynamic-slice_select_fusion
  218.1 1.7 scatter.20
  220.6 1.5 cholesky.41
  223.4 1.2 custom-call.15
  225.3 1.1 fusion.7
  227.0 1.2 copy.144
  (67 shorter events, 13.4 us)
Async XLA Ops:
  0.6 49.8 %copy-start = (f32[8,8,32,128]{3,2,1,0:T(8,128)S(1)}, f32[8,8,32,128]{3,2,1,0:T(8,128)}, u32[]{:S(2)}) copy-start(f32[8,8,32,128]{3,2,1,0:T(8,128)} %param.15) | copy-start | bytes 3145732
  51.9 7.1 %collective-permute-start = (f32[8,1,32,128]{3,0,2,1:T(8,128)S(1)}, f32[8,1,32,128]{3,0,2,1:T(8,128)S(1)}, u32[]{:S(2)}, u32[]{:S(2)}) collective-permute-start(f32[8,1,32,128]{3,0,2,1:T(8,128)S(1)} %get-tuple-element.85), channel_id=1, source_target_pairs={{8,0},{16,8},{24,16},{9,1},{17,9},{25,17},{10,2},{18,10},{26,18},{... | collective-permute-start | bytes 393224 | tf_op jit(solution)/shard_map/ppermute | solution.py:17
  53.2 7.3 %collective-permute-start.1 = (f32[8,1,32,128]{3,0,2,1:T(8,128)S(1)}, f32[8,1,32,128]{3,0,2,1:T(8,128)S(1)}, u32[]{:S(2)}, u32[]{:S(2)}) collective-permute-start(f32[8,1,32,128]{3,0,2,1:T(8,128)S(1)} %get-tuple-element.84), channel_id=1, source_target_pairs={{0,8},{8,16},{16,24},{1,9},{9,17},{17,25},{2,10},{10,18},{18,26},{... | collective-permute-start | bytes 393224 | tf_op jit(solution)/shard_map/ppermute | solution.py:14
  59.1 6.8 %copy-start.3 = (f32[8,1,32,128]{3,0,2,1:T(8,128)}, f32[8,1,32,128]{3,0,2,1:T(8,128)S(1)}, u32[]{:S(2)}) copy-start(f32[8,1,32,128]{3,0,2,1:T(8,128)S(1)} %collective-permute-done) | copy-start | bytes 393220
  60.6 5.3 %copy-start.4 = (f32[8,1,32,128]{3,0,2,1:T(8,128)}, f32[8,1,32,128]{3,0,2,1:T(8,128)S(1)}, u32[]{:S(2)}) copy-start(f32[8,1,32,128]{3,0,2,1:T(8,128)S(1)} %collective-permute-done.1) | copy-start | bytes 393220
  60.6 4.3 %collective-permute-start.2 = (f32[8,10,1,128]{3,0,2,1:T(8,128)S(1)}, f32[8,10,1,128]{3,0,2,1:T(8,128)S(1)}, u32[]{:S(2)}, u32[]{:S(2)}) collective-permute-start(f32[8,10,1,128]{3,0,2,1:T(8,128)S(1)} %get-tuple-element.81), channel_id=1, source_target_pairs={{4,0},{5,1},{6,2},{7,3},{12,8},{13,9},{14,10},{15,11},{20,16},{21,... | collective-permute-start | bytes 122888 | tf_op jit(solution)/shard_map/ppermute | solution.py:17
  61.9 3.9 %collective-permute-start.3 = (f32[8,10,1,128]{3,0,2,1:T(8,128)S(1)}, f32[8,10,1,128]{3,0,2,1:T(8,128)S(1)}, u32[]{:S(2)}, u32[]{:S(2)}) collective-permute-start(f32[8,10,1,128]{3,0,2,1:T(8,128)S(1)} %get-tuple-element.80), channel_id=1, source_target_pairs={{0,4},{1,5},{2,6},{3,7},{8,12},{9,13},{10,14},{11,15},{16,20},{17,... | collective-permute-start | bytes 122888 | tf_op jit(solution)/shard_map/ppermute | solution.py:14
  65.8 0.6 copy-start.6
  67.9 8.5 %copy-start.7 = (f32[8,32,128]{2,1,0:T(8,128)S(1)}, f32[8,32,128]{2,1,0:T(8,128)}, u32[]{:S(2)}) copy-start(f32[8,32,128]{2,1,0:T(8,128)} %param.16) | copy-start | bytes 393220
  70.0 7.2 %collective-permute-start.4 = (f32[8,10,34,1]{2,0,3,1:T(8,128)S(1)}, f32[8,10,34,1]{2,0,3,1:T(8,128)S(1)}, u32[]{:S(2)}, u32[]{:S(2)}) collective-permute-start(f32[8,10,34,1]{2,0,3,1:T(8,128)S(1)} %copy.130), channel_id=1, source_target_pairs={{1,0},{2,1},{3,2},{5,4},{6,5},{7,6},{9,8},{10,9},{11,10},{13,12},{... | collective-permute-start | bytes 32648 | tf_op jit(solution)/shard_map/ppermute | solution.py:17
  71.9 6.2 %collective-permute-start.5 = (f32[8,10,34,1]{2,0,3,1:T(8,128)S(1)}, f32[8,10,34,1]{2,0,3,1:T(8,128)S(1)}, u32[]{:S(2)}, u32[]{:S(2)}) collective-permute-start(f32[8,10,34,1]{2,0,3,1:T(8,128)S(1)} %copy.132), channel_id=1, source_target_pairs={{0,1},{1,2},{2,3},{4,5},{5,6},{6,7},{8,9},{9,10},{10,11},{12,13},{... | collective-permute-start | bytes 32648 | tf_op jit(solution)/shard_map/ppermute | solution.py:14
  133.7 7.3 %collective-permute-start.6 = (f32[8,1,32,128]{3,0,2,1:T(8,128)S(1)}, f32[8,1,32,128]{3,0,2,1:T(8,128)S(1)}, u32[]{:S(2)}, u32[]{:S(2)}) collective-permute-start(f32[8,1,32,128]{3,0,2,1:T(8,128)S(1)} %get-tuple-element.83), channel_id=1, source_target_pairs={{8,0},{16,8},{24,16},{9,1},{17,9},{25,17},{10,2},{18,10},{26,18},{... | collective-permute-start | bytes 393224 | tf_op jit(solution)/shard_map/ppermute | solution.py:17
  135.0 7.3 %collective-permute-start.7 = (f32[8,1,32,128]{3,0,2,1:T(8,128)S(1)}, f32[8,1,32,128]{3,0,2,1:T(8,128)S(1)}, u32[]{:S(2)}, u32[]{:S(2)}) collective-permute-start(f32[8,1,32,128]{3,0,2,1:T(8,128)S(1)} %get-tuple-element.82), channel_id=1, source_target_pairs={{0,8},{8,16},{16,24},{1,9},{9,17},{17,25},{2,10},{10,18},{18,26},{... | collective-permute-start | bytes 393224 | tf_op jit(solution)/shard_map/ppermute | solution.py:14
  141.1 6.5 %copy-start.1 = (f32[8,1,32,128]{3,0,2,1:T(8,128)}, f32[8,1,32,128]{3,0,2,1:T(8,128)S(1)}, u32[]{:S(2)}) copy-start(f32[8,1,32,128]{3,0,2,1:T(8,128)S(1)} %collective-permute-done.6) | copy-start | bytes 393220
  142.4 5.2 %copy-start.2 = (f32[8,1,32,128]{3,0,2,1:T(8,128)}, f32[8,1,32,128]{3,0,2,1:T(8,128)S(1)}, u32[]{:S(2)}) copy-start(f32[8,1,32,128]{3,0,2,1:T(8,128)S(1)} %collective-permute-done.7) | copy-start | bytes 393220
  142.4 4.4 %collective-permute-start.8 = (f32[8,10,1,128]{3,0,2,1:T(8,128)S(1)}, f32[8,10,1,128]{3,0,2,1:T(8,128)S(1)}, u32[]{:S(2)}, u32[]{:S(2)}) collective-permute-start(f32[8,10,1,128]{3,0,2,1:T(8,128)S(1)} %get-tuple-element.79), channel_id=1, source_target_pairs={{4,0},{5,1},{6,2},{7,3},{12,8},{13,9},{14,10},{15,11},{20,16},{21,... | collective-permute-start | bytes 122888 | tf_op jit(solution)/shard_map/ppermute | solution.py:17
  143.7 3.9 %collective-permute-start.9 = (f32[8,10,1,128]{3,0,2,1:T(8,128)S(1)}, f32[8,10,1,128]{3,0,2,1:T(8,128)S(1)}, u32[]{:S(2)}, u32[]{:S(2)}) collective-permute-start(f32[8,10,1,128]{3,0,2,1:T(8,128)S(1)} %get-tuple-element.78), channel_id=1, source_target_pairs={{0,4},{1,5},{2,6},{3,7},{8,12},{9,13},{10,14},{11,15},{16,20},{17,... | collective-permute-start | bytes 122888 | tf_op jit(solution)/shard_map/ppermute | solution.py:14
  147.6 0.6 copy-start.5
  152.4 9.4 %collective-permute-start.10 = (f32[8,10,34,1]{2,0,3,1:T(8,128)}, f32[8,10,34,1]{2,0,3,1:T(8,128)}, u32[]{:S(2)}, u32[]{:S(2)}) collective-permute-start(f32[8,10,34,1]{2,0,3,1:T(8,128)} %copy.137), channel_id=1, source_target_pairs={{1,0},{2,1},{3,2},{5,4},{6,5},{7,6},{9,8},{10,9},{11,10},{13,12},{... | collective-permute-start | bytes 32648 | tf_op jit(solution)/shard_map/ppermute | solution.py:17
  155.0 8.3 %collective-permute-start.11 = (f32[8,10,34,1]{2,0,3,1:T(8,128)}, f32[8,10,34,1]{2,0,3,1:T(8,128)}, u32[]{:S(2)}, u32[]{:S(2)}) collective-permute-start(f32[8,10,34,1]{2,0,3,1:T(8,128)} %copy.139), channel_id=1, source_target_pairs={{0,1},{1,2},{2,3},{4,5},{5,6},{6,7},{8,9},{9,10},{10,11},{12,13},{... | collective-permute-start | bytes 32648 | tf_op jit(solution)/shard_map/ppermute | solution.py:14
where the time goes:
time: 229 us; the launch traced here: 228 us
  blocking collectives  127 us (55%)
  starting transfers between devices  33.1 us (14%)
  local copies, waits for them, and re-layouts  22.6 us (10%)
  other arithmetic  21 us (9%)
  matrix products  16.4 us (7%)
  waiting for transfers between devices  6.95 us (3%)
    psum x2, blocking collectives, body(): lax.psum(small_dot(jnp.concatenate([stacked, image], axis=0), image.T), (...  85.1 us
    psum x1, blocking collectives, body(): gram = lax.psum(small_dot(rows, rows.T), ('gx', 'gy', 'gz'))  42 us
    ppermute x6, starting transfers between devices, padded_2(): lax.ppermute(lax.slice_in_dim(block, block.shape[dim] - width, None, axis...  25.4 us
    dot_general x12, matrix products, small_dot(): return jnp.dot(left, right, precision=lax.Precision.HIGHEST)  15.7 us
    ppermute x6, starting transfers between devices, padded_2(): lax.ppermute(lax.slice_in_dim(block, 0, width, axis=dim), axis, backward)  7.73 us
    slice x4, local copies, waits for them, and re-layouts, padded_2(): lax.slice_in_dim(block, 0, width, axis=dim)  7.72 us
    sub x2, other arithmetic, operate(): return (6.0 + shift)[None] * fields - beside  6.01 us
    ppermute x6, waiting for transfers between devices, padded_2(): lax.ppermute(lax.slice_in_dim(block, block.shape[dim] - width, None, axis...  4.75 us
  transfers between devices with their start and end apart: 12, of which 7 were waited for; matrix products, arithmetic and copies ran while one was open for 3% of the time, Pallas kernels for 0%

commit v1 on v0

v1 whole, which is shorter than its diff:
```python
import functools

import jax
import jax.numpy as jnp
from jax import lax
from jax.experimental import pallas as pl
from jax.experimental.pallas import tpu as pltpu
from jax.sharding import PartitionSpec as P

AXES = ("gx", "gy", "gz")
CENTRE = 7.0
LANES = 128
F32 = jnp.float32


def swap_pairs(count):
    first = [(i, j) for a in range(0, count - 1, 2) for i, j in ((a, a + 1), (a + 1, a))]
    second = [(i, j) for a in range(1, count - 1, 2) for i, j in ((a, a + 1), (a + 1, a))]
    return [pairs for pairs in (first, second) if pairs]


def rounds_of():
    return tuple(len(swap_pairs(lax.axis_size(axis))) for axis in AXES)


def parity(axis):
    return lax.rem(lax.axis_index(axis), 2) == 1


def write_xy_faces(v_ref, x_refs, y_refs):
    width, nx, ny, _ = v_ref.shape
    odd_x, odd_y = parity("gx"), parity("gy")
    for k, ref in enumerate(x_refs):
        high = jnp.logical_xor(odd_x, k == 0)
        ref[...] = v_ref[:, jnp.where(high, nx - 1, 0)]
    for k, ref in enumerate(y_refs):
        high = jnp.logical_xor(odd_y, k == 0)
        ref[...] = jnp.where(high, v_ref[:, :, ny - 1 : ny, :], v_ref[:, :, 0:1, :])


def packed_ends(tile, m, packed, lane):
    at = 2 * m
    hit = (lane == at) | (lane == lax.rem(at + LANES - 1, LANES))
    return jnp.where(hit, pltpu.roll(tile, at, 1), packed)


def pack_kernel(nx_r, ny_r, v_ref, *refs):
    width, nx, ny, _ = v_ref.shape
    x_refs, y_refs, z_ref = refs[:nx_r], refs[nx_r : nx_r + ny_r], refs[nx_r + ny_r]
    write_xy_faces(v_ref, x_refs, y_refs)
    lane = lax.broadcasted_iota(jnp.int32, (ny, LANES), 1)

    def field(f, packed):
        for x in range(nx):
            packed = packed_ends(v_ref[f, x], f * nx + x, packed, lane)
        return packed

    z_ref[...] = lax.fori_loop(0, width, field, jnp.zeros((ny, LANES), F32))


def pick(odd, refs, load):
    first = load(refs[0]) if refs else 0.0
    second = load(refs[1]) if len(refs) > 1 else jnp.zeros_like(first)
    return jnp.where(odd, first, second), jnp.where(odd, second, first)


def apply_operator(v_ref, shift_ref, x_in, y_in, z_in, out_ref, packed=None):
    width, nx, ny, _ = v_ref.shape
    odd_x, odd_y, odd_z = parity("gx"), parity("gy"), parity("gz")
    lane = lax.broadcasted_iota(jnp.int32, (ny, LANES), 1)
    row = lax.broadcasted_iota(jnp.int32, (ny, LANES), 0)
    low_z, high_z = pick(odd_z, z_in, lambda ref: ref[...])
    ends = jnp.where(
        lax.rem(lane, 2) == 0, pltpu.roll(low_z, 1, 1), pltpu.roll(high_z, LANES - 1, 1)
    )

    def field(f, packed):
        low_x, high_x = pick(odd_x, x_in, lambda ref: ref[f])
        for x in range(nx):
            m = f * nx + x
            low_y, high_y = pick(odd_y, y_in, lambda ref: ref[f, x])
            v = v_ref[f, x]
            end = pltpu.roll(ends, lax.rem(LANES - 2 * m, LANES), 1)
            beside = (v_ref[f, x - 1] if x > 0 else low_x) + (v_ref[f, x + 1] if x < nx - 1 else high_x)
            beside += jnp.where(row == 0, low_y, pltpu.roll(v, 1, 0))
            beside += jnp.where(row == ny - 1, high_y, pltpu.roll(v, ny - 1, 0))
            beside += jnp.where(lane == 0, end, pltpu.roll(v, 1, 1))
            beside += jnp.where(lane == LANES - 1, end, pltpu.roll(v, LANES - 1, 1))
            out = ((6.0 - CENTRE) + shift_ref[x]) * v - beside
            out_ref[f, x] = out
            if packed is not None:
                packed = packed_ends(out, m, packed, lane)
        return packed

    if packed is None:
        lax.fori_loop(0, width, lambda f, c: (field(f, None), c)[1], 0)
        return None
    return lax.fori_loop(0, width, field, packed)


def operator_kernel(nx_r, ny_r, nz_r, *refs):
    v_ref, shift_ref = refs[:2]
    at = 2
    x_in, y_in, z_in = refs[at : at + nx_r], refs[at + nx_r : at + nx_r + ny_r], refs[at + nx_r + ny_r : at + nx_r + ny_r + nz_r]
    outs = refs[at + nx_r + ny_r + nz_r :]
    out_ref = outs[0]
    x_out, y_out, z_out = outs[1 : 1 + nx_r], outs[1 + nx_r : 1 + nx_r + ny_r], outs[1 + nx_r + ny_r]
    ny = v_ref.shape[2]
    z_out[...] = apply_operator(v_ref, shift_ref, x_in, y_in, z_in, out_ref, jnp.zeros((ny, LANES), F32))
    write_xy_faces(out_ref, x_out, y_out)


def add_moment(a_ref, b_ref, at, payload):
    width, nx, ny, _ = a_ref.shape
    pairs = [(i, j) for i in range(width) for j in range(i + 1)]

    def plane(x, sums):
        sums = list(sums)
        for y in range(0, ny, 8):
            a = [a_ref[f, x, y : y + 8, :] for f in range(width)]
            b = a if b_ref is a_ref else [b_ref[f, x, y : y + 8, :] for f in range(width)]
            for k, (i, j) in enumerate(pairs):
                sums[k] = sums[k] + a[i] * b[j]
        return tuple(sums)

    sums = lax.fori_loop(0, nx, plane, tuple(jnp.zeros((8, LANES), F32) for _ in pairs))
    rows = {}
    for (i, j), value in zip(pairs, sums):
        rows[i, j] = rows[j, i] = jnp.sum(value, axis=0, keepdims=True)
    lane = lax.broadcasted_iota(jnp.int32, (8, LANES), 1)
    for i in range(width):
        column = jnp.sum(jnp.concatenate([rows[i, j] for j in range(width)], axis=0), axis=1, keepdims=True)
        payload = jnp.where(lane == at + i, column, payload)
    return payload


def early_moments_kernel(b_ref, u_ref, out_ref):
    width = b_ref.shape[0]
    payload = add_moment(b_ref, b_ref, 0, jnp.zeros((8, LANES), F32))
    payload = add_moment(b_ref, u_ref, width, payload)
    out_ref[...] = add_moment(u_ref, u_ref, 2 * width, payload)


def late_moments_kernel(nx_r, ny_r, nz_r, *refs):
    u_ref, shift_ref = refs[:2]
    at = 2
    x_in, y_in, z_in = refs[at : at + nx_r], refs[at + nx_r : at + nx_r + ny_r], refs[at + nx_r + ny_r : at + nx_r + ny_r + nz_r]
    early_ref, out_ref, t_ref = refs[at + nx_r + ny_r + nz_r :]
    width = u_ref.shape[0]
    apply_operator(u_ref, shift_ref, x_in, y_in, z_in, t_ref)
    payload = add_moment(u_ref, t_ref, 3 * width, early_ref[...])
    payload = add_moment(t_ref, t_ref, 4 * width, payload)
    out_ref[...] = jnp.broadcast_to(payload[None], out_ref.shape)


def lanes_of(matrix, j):
    return jnp.broadcast_to(matrix[:, j : j + 1], matrix.shape)


def rows_of(matrix, i):
    return jnp.broadcast_to(matrix[i : i + 1, :], matrix.shape)


def times(left, at, right):
    count = left.shape[0]
    total = lanes_of(left, at) * rows_of(right, 0)
    for k in range(1, count):
        total = total + lanes_of(left, at + k) * rows_of(right, k)
    return total


def shift_lanes(matrix, by):
    return pltpu.roll(matrix, by % LANES, 1)


def eliminate(blocks):
    size = blocks[0].shape[0]
    sub = lax.broadcasted_iota(jnp.int32, blocks[0].shape, 0)
    for j in range(size * len(blocks)):
        own, local = divmod(j, size)
        columns = [lanes_of(block, j) for block in blocks]
        pivot = rows_of(blocks[own], local) / rows_of(columns[own], local)
        blocks = [block - column * pivot for block, column in zip(blocks, columns)]
        blocks[own] = jnp.where(sub == local, pivot, blocks[own])
    return blocks


def small_algebra(s):
    n = s.shape[0]
    c0 = CENTRE
    lane = lax.broadcasted_iota(jnp.int32, s.shape, 1)
    sub = lax.broadcasted_iota(jnp.int32, s.shape, 0)
    n0, n1, n2, n3, n4 = shift_lanes(s, n), s, shift_lanes(s, -n), shift_lanes(s, -2 * n), shift_lanes(s, -3 * n)
    (e,) = eliminate([s])
    p1 = times(s, n, e)
    p2 = times(s, 2 * n, e)
    p3 = times(s, 3 * n, e)
    cc = times(e, n, e)
    e2c = times(e, 2 * n, e)
    g = n2 - p1
    q = shift_lanes(e, -n) - cc
    n3c = n3 - p2
    f3 = n3c - times(s, n, q)
    f4 = n4 - p3 - times(s, n, shift_lanes(e, -2 * n) - e2c)
    m11 = n2 + 2.0 * c0 * n1 + c0 * c0 * n0
    m12 = n3c + 2.0 * c0 * g
    m21 = n3 - shift_lanes(p1, -n) + 2.0 * c0 * g
    m22 = f4 + 2.0 * c0 * f3 + c0 * c0 * g
    r1 = n1 + c0 * n0

    def assemble(first, second, third):
        joined = jnp.where(lane < n, shift_lanes(first, -n), second)
        return jnp.where(lane < 2 * n, joined, shift_lanes(third, n))

    pa, qa = eliminate([assemble(m11, m12, r1), assemble(m21, m22, g)])
    cq = times(e, n, qa)
    on_b = pa - cq
    unit = jnp.where(lane == sub + 2 * n, 1.0, 0.0)
    part = unit - times(e, n, pa) - c0 * pa - times(q, n, qa)
    squares = part * times(s, 0, part)
    pq = pa + c0 * qa
    squares = squares + pq * (times(g, n, pq) + 2.0 * times(f3, n, qa))
    squares = squares + qa * times(f4 - times(g, n, q), n, qa)
    return on_b, qa, jnp.sum(squares, axis=0, keepdims=True)


def finish_kernel(parts_ref, b_ref, u_ref, out_ref, norms_ref, coeff_ref):
    width, nx, ny, _ = b_ref.shape
    n = width
    total = jnp.sum(parts_ref[...], axis=0)
    on_b, on_u, squares = small_algebra(total)
    norms_ref[...] = jnp.sqrt(shift_lanes(squares, -2 * n))[:, :n]
    for f in range(width):
        coeff_ref[0, f] = lanes_of(on_b, 2 * n + f)
        coeff_ref[1, f] = lanes_of(on_u, 2 * n + f)
    group = 2

    def fields(k, carry):
        first = [[[rows_of(coeff_ref[h, group * k + d], g) for g in range(width)] for h in range(2)] for d in range(group)]

        def plane(x, carry):
            for y in range(0, ny, 8):
                b = [b_ref[g, x, y : y + 8, :] for g in range(width)]
                u = [u_ref[g, x, y : y + 8, :] for g in range(width)]
                for d in range(group):
                    total = first[d][0][0] * b[0] + first[d][1][0] * u[0]
                    for g in range(1, width):
                        total = total + (first[d][0][g] * b[g] + first[d][1][g] * u[g])
                    out_ref[group * k + d, x, y : y + 8, :] = total
            return carry

        return lax.fori_loop(0, nx, plane, carry)

    lax.fori_loop(0, width // group, fields, 0)


def call(kernel, out_shape, operands, scratch=(), flops=1_000_000, name=None):
    return pl.pallas_call(
        kernel,
        out_shape=out_shape,
        in_specs=[pl.BlockSpec(memory_space=pltpu.VMEM)] * len(operands),
        out_specs=jax.tree.map(lambda _: pl.BlockSpec(memory_space=pltpu.VMEM), out_shape),
        scratch_shapes=list(scratch),
        cost_estimate=pl.CostEstimate(flops=flops, bytes_accessed=1 << 20, transcendentals=0),
        name=name,
    )(*operands)


def trade(x_faces, y_faces, ends):
    pairs_x, pairs_y, pairs_z = (swap_pairs(lax.axis_size(axis)) for axis in AXES)
    got_x = [lax.ppermute(face, "gx", pairs) for face, pairs in zip(x_faces, pairs_x)]
    got_z = [lax.ppermute(ends, "gz", pairs) for pairs in pairs_z]
    got_y = [lax.ppermute(face, "gy", pairs) for face, pairs in zip(y_faces, pairs_y)]
    return [*got_x, *got_y, *got_z]


def body(right_side, shift):
    width, nx, ny, nz = right_side.shape
    assert width == 8 and nz == LANES and ny % 8 == 0 and width * nx <= LANES // 2
    nx_r, ny_r, nz_r = rounds_of()
    devices = 1
    for axis in AXES:
        devices *= lax.axis_size(axis)
    block = jax.ShapeDtypeStruct(right_side.shape, F32)
    faces = [jax.ShapeDtypeStruct((width, ny, nz), F32)] * nx_r
    faces += [jax.ShapeDtypeStruct((width, nx, 1, nz), F32)] * ny_r
    faces += [jax.ShapeDtypeStruct((ny, LANES), F32)]

    packed = call(functools.partial(pack_kernel, nx_r, ny_r), faces, [right_side], name="pack")
    halo = trade(packed[:nx_r], packed[nx_r : nx_r + ny_r], packed[-1])
    u, *packed = call(
        functools.partial(operator_kernel, nx_r, ny_r, nz_r), [block, *faces], [right_side, shift, *halo], name="operator"
    )
    halo = trade(packed[:nx_r], packed[nx_r : nx_r + ny_r], packed[-1])
    early = call(
        early_moments_kernel, jax.ShapeDtypeStruct((8, LANES), F32), [right_side, u], flops=30_000_000, name="early"
    )
    copies = call(
        functools.partial(late_moments_kernel, nx_r, ny_r, nz_r),
        jax.ShapeDtypeStruct((devices, 8, LANES), F32),
        [u, shift, *halo, early],
        scratch=[pltpu.VMEM(right_side.shape, F32)],
        name="late",
    )
    parts = lax.all_to_all(copies, AXES, 0, 0, tiled=True)
    out, norms = call(
        finish_kernel,
        [block, jax.ShapeDtypeStruct((1, width), F32)],
        [parts, right_side, u],
        scratch=[pltpu.VMEM((2, width, 8, LANES), F32)],
        name="finish",
    )
    return out, norms.reshape(width)


def solution(mesh):
    in_specs = (P(None, "gx", "gy", "gz"), P("gx", "gy", "gz"))
    out_specs = (P(None, "gx", "gy", "gz"), P())
    return jax.shard_map(body, mesh=mesh, in_specs=in_specs, out_specs=out_specs, check_vma=False)
```

time: 229 us -> 60.1 us (0.26)
  blocking collectives: 127 us -> 13.5 us
  Pallas kernels: 0 us -> 22.7 us
  other arithmetic: 21 us -> 0 us
  local copies, waits for them, and re-layouts: 22.6 us -> 2.58 us
  matrix products: 16.4 us -> 0 us
  starting transfers between devices: 33.1 us -> 18.2 us
  waiting for transfers between devices: 6.95 us -> 1.95 us
    psum x3 -> x0, blocking collectives: 127 us -> none  [the longest x2 85.1 us: body(): lax.psum(small_dot(jnp.concatenate([stacked, image], axis=0), image.T), (...]
    pallas_call x0 -> x5, Pallas kernels: none -> 22.7 us  [call(): pl.pallas_call(kernel, out_shape=out_shape, in_specs=[pl.BlockSpec(memory...]
    dot_general x12 -> x0, matrix products: 15.7 us -> none  [small_dot(): return jnp.dot(left, right, precision=lax.Precision.HIGHEST)]
    ppermute x12 -> x10, starting transfers between devices: 33.1 us -> 18.2 us  [the longest x4 9.57 us: trade(): got_z = [lax.ppermute(ends, 'gz', pairs) for pairs in pairs_z]]
    another operation x22 -> x0, other arithmetic: 14.1 us -> none  [the longest x9 4.29 us: body(): lower = jnp.linalg.cholesky(gram)]
    all_to_all x0 -> x1, blocking collectives: none -> 13.5 us  [body(): parts = lax.all_to_all(copies, AXES, 0, 0, tiled=True)]
    slice x8 -> x0, local copies, waits for them, and re-layouts: 9.7 us -> none  [the longest x4 7.72 us: padded_2(): lax.slice_in_dim(block, 0, width, axis=dim)]
    ppermute x4 -> x0, local copies, waits for them, and re-layouts: 6.48 us -> none  [the longest x2 4.34 us: padded_2(): lax.ppermute(lax.slice_in_dim(block, block.shape[dim] - width, None, axis...]
  transfers between devices with their start and end apart: 12 -> 10, of which waited for: 7 -> 1; matrix products, arithmetic and copies ran while one was open for 3% -> 0% of each run, Pallas kernels for 0% -> 6%
where the time goes in v1:
time: 60.1 us; the launch traced here: 59.7 us
  Pallas kernels  22.7 us (38%)
  starting transfers between devices  18.2 us (30%)
  blocking collectives  13.5 us (22%)
  local copies, waits for them, and re-layouts  2.58 us (4%)
  waiting for transfers between devices  1.95 us (3%)
  between operations  0.77 us (1%)
    pallas_call x5, Pallas kernels, call(): pl.pallas_call(kernel, out_shape=out_shape, in_specs=[pl.BlockSpec(memory...  22.7 us
    all_to_all x1, blocking collectives, body(): parts = lax.all_to_all(copies, AXES, 0, 0, tiled=True)  13.5 us
    ppermute x4, starting transfers between devices, trade(): got_z = [lax.ppermute(ends, 'gz', pairs) for pairs in pairs_z]  9.57 us
    ppermute x4, starting transfers between devices, trade(): lax.ppermute(face, 'gx', pairs)  8.5 us
    unnamed x20, local copies, waits for them, and re-layouts  2.58 us
    ppermute x4, waiting for transfers between devices, trade(): got_z = [lax.ppermute(ends, 'gz', pairs) for pairs in pairs_z]  1.93 us
  transfers between devices with their start and end apart: 10, of which 1 were waited for; matrix products, arithmetic and copies ran while one was open for 0% of the time, Pallas kernels for 6%

profile of v1, /device:TPU:0, one launch (start us, length us, event | category | flops | bytes accessed | tf_op | source)
XLA Modules:
  0.0 59.7 jit_solution(12403315786520640479)
XLA Ops:
  0.6 2.7 %pack.1 = (f32[8,32,128]{2,1,0:T(8,128)}, f32[8,32,128]{2,1,0:T(8,128)}, f32[8,8,1,128]{3,2,1,0:T(1,128)}, f32[32,128]{1,0:T(8,128)}) custom-call(f32[8,8,32,128]{3,2,1,0:T(8,128)} %b_ref.3), custom_call_target="tpu_custom_call" | custom-call | flops 1000000 | bytes 1048576 | tf_op jit(solution)/shard_map/pack/pallas_call | solution.py:258
  3.3 3.0 %collective-permute-start = (f32[8,32,128]{2,1,0:T(8,128)}, f32[8,32,128]{2,1,0:T(8,128)S(1)}, u32[]{:S(2)}, u32[]{:S(2)}) collective-permute-start(f32[8,32,128]{2,1,0:T(8,128)} %get-tuple-element.13), channel_id=1, source_target_pairs={{0,8},{8,0},{16,24},{24,16},{1,9},{9,1},{17,25},{25,17},{2,10},{10... | collective-permute-start | bytes 393224 | tf_op jit(solution)/shard_map/ppermute | solution.py:271
  6.3 0.7 %collective-permute-start.1 = (f32[8,32,128]{2,1,0:T(8,128)}, f32[8,32,128]{2,1,0:T(8,128)S(1)}, u32[]{:S(2)}, u32[]{:S(2)}) collective-permute-start(f32[8,32,128]{2,1,0:T(8,128)} %get-tuple-element.14), channel_id=1, source_target_pairs={{8,16},{16,8},{9,17},{17,9},{10,18},{18,10},{11,19},{19,11},{12,20... | collective-permute-start | bytes 393224 | tf_op jit(solution)/shard_map/ppermute | solution.py:271
  7.0 0.1 collective-permute-start.2
  7.1 0.7 %collective-permute-start.4 = (f32[32,128]{1,0:T(8,128)}, f32[32,128]{1,0:T(8,128)S(1)}, u32[]{:S(2)}, u32[]{:S(2)}) collective-permute-start(f32[32,128]{1,0:T(8,128)} %get-tuple-element.16), channel_id=1, source_target_pairs={{1,2},{2,1},{5,6},{6,5},{9,10},{10,9},{13,14},{14,13},{17,18},{18,... | collective-permute-start | bytes 49160 | tf_op jit(solution)/shard_map/ppermute | solution.py:272
  7.7 4.5 %collective-permute-start.3 = (f32[32,128]{1,0:T(8,128)}, f32[32,128]{1,0:T(8,128)S(1)}, u32[]{:S(2)}, u32[]{:S(2)}) collective-permute-start(f32[32,128]{1,0:T(8,128)} %get-tuple-element.16), channel_id=1, source_target_pairs={{0,1},{1,0},{2,3},{3,2},{4,5},{5,4},{6,7},{7,6},{8,9},{9,8},{10,11... | collective-permute-start | bytes 49160 | tf_op jit(solution)/shard_map/ppermute | solution.py:272
  12.2 0.0 collective-permute-done.4.refs_6_
  12.2 0.0 copy-start.6
  12.2 1.9 %collective-permute-done.3.refs_5_ = f32[32,128]{1,0:T(8,128)S(1)} collective-permute-done((f32[32,128]{1,0:T(8,128)}, f32[32,128]{1,0:T(8,128)S(1)}, u32[]{:S(2)}, u32[]{:S(2)}) %collective-permute-start.3) | collective-permute-done | bytes 16416 | tf_op jit(solution)/shard_map/ppermute | solution.py:272
  14.1 0.0 copy-start.7
  14.1 0.0 collective-permute-done.2.refs_4_
  14.1 0.0 copy-start.4
  14.1 0.0 collective-permute-done.refs_2_
  14.1 0.0 copy-start
  14.1 0.0 collective-permute-done.1.refs_3_
  14.2 0.0 copy-done.6
  14.2 0.5 copy-done.7
  14.7 0.0 copy-done.4
  14.7 0.0 copy-done
  14.8 0.0 copy-start.1
  14.8 0.7 %copy-done.1 = f32[8,32,128]{2,1,0:T(8,128)} copy-done((f32[8,32,128]{2,1,0:T(8,128)}, f32[8,32,128]{2,1,0:T(8,128)S(1)}, u32[]{:S(2)}) %copy-start.1) | copy-done | bytes 131096
  15.5 4.8 %operator.1 = (f32[8,8,32,128]{3,2,1,0:T(8,128)}, f32[8,32,128]{2,1,0:T(8,128)}, f32[8,32,128]{2,1,0:T(8,128)}, f32[8,8,1,128]{3,2,1,0:T(1,128)}, f32[32,128]{1,0:T(8,128)}) custom-call(f32[8,8,32,128]{3,2,1,0:T(8,128)} %b_ref.3, f32[8,32,128]{2,1,0:T(8,128)} %refs_1_.3, f32[8,32,128]{2,1,0:T(8,128)} %copy-done, f32[8,32,128]{2,1,0:T(8,128)} %copy-done.1, ...), custom_call_target="tpu_custom_call" | custom-call | flops 1000000 | bytes 1048576 | tf_op jit(solution)/shard_map/operator/pallas_call | solution.py:258
  20.2 4.2 %collective-permute-start.5 = (f32[8,32,128]{2,1,0:T(8,128)}, f32[8,32,128]{2,1,0:T(8,128)S(1)}, u32[]{:S(2)}, u32[]{:S(2)}) collective-permute-start(f32[8,32,128]{2,1,0:T(8,128)} %get-tuple-element.18), channel_id=1, source_target_pairs={{0,8},{8,0},{16,24},{24,16},{1,9},{9,1},{17,25},{25,17},{2,10},{10... | collective-permute-start | bytes 393224 | tf_op jit(solution)/shard_map/ppermute | solution.py:271
  24.4 0.7 %collective-permute-start.6 = (f32[8,32,128]{2,1,0:T(8,128)}, f32[8,32,128]{2,1,0:T(8,128)S(1)}, u32[]{:S(2)}, u32[]{:S(2)}) collective-permute-start(f32[8,32,128]{2,1,0:T(8,128)} %get-tuple-element.19), channel_id=1, source_target_pairs={{8,16},{16,8},{9,17},{17,9},{10,18},{18,10},{11,19},{19,11},{12,20... | collective-permute-start | bytes 393224 | tf_op jit(solution)/shard_map/ppermute | solution.py:271
  25.1 0.1 collective-permute-start.7
  25.2 0.7 %collective-permute-start.9 = (f32[32,128]{1,0:T(8,128)}, f32[32,128]{1,0:T(8,128)S(1)}, u32[]{:S(2)}, u32[]{:S(2)}) collective-permute-start(f32[32,128]{1,0:T(8,128)} %get-tuple-element.21), channel_id=1, source_target_pairs={{1,2},{2,1},{5,6},{6,5},{9,10},{10,9},{13,14},{14,13},{17,18},{18,... | collective-permute-start | bytes 49160 | tf_op jit(solution)/shard_map/ppermute | solution.py:272
  25.8 3.8 %collective-permute-start.8 = (f32[32,128]{1,0:T(8,128)}, f32[32,128]{1,0:T(8,128)S(1)}, u32[]{:S(2)}, u32[]{:S(2)}) collective-permute-start(f32[32,128]{1,0:T(8,128)} %get-tuple-element.21), channel_id=1, source_target_pairs={{0,1},{1,0},{2,3},{3,2},{4,5},{5,4},{6,7},{7,6},{8,9},{9,8},{10,11... | collective-permute-start | bytes 49160 | tf_op jit(solution)/shard_map/ppermute | solution.py:272
  29.6 3.6 %early.1.refs_7_ = f32[8,128]{1,0:T(8,128)} custom-call(f32[8,8,32,128]{3,2,1,0:T(8,128)} %b_ref.3, f32[8,8,32,128]{3,2,1,0:T(8,128)} %get-tuple-element.17.u_ref.refs_0_), custom_call_target="tpu_custom_call" | custom-call | flops 30000000 | bytes 1048576 | tf_op jit(solution)/shard_map/early/pallas_call | solution.py:258
  33.3 0.0 collective-permute-done.9.refs_6_
  33.3 0.0 copy-start.8
  33.3 0.0 collective-permute-done.8.refs_5_
  33.3 0.0 copy-start.9
  33.3 0.0 collective-permute-done.7.refs_4_
  33.3 0.0 copy-start.5
  33.3 0.0 collective-permute-done.5.refs_2_
  33.3 0.0 copy-start.2
  33.3 0.0 collective-permute-done.6.refs_3_
  33.3 0.5 copy-done.8
  33.9 0.0 copy-done.9
  33.9 0.0 copy-done.5
  33.9 0.1 copy-done.2
  34.0 0.0 copy-start.3
  34.0 0.6 %copy-done.3 = f32[8,32,128]{2,1,0:T(8,128)} copy-done((f32[8,32,128]{2,1,0:T(8,128)}, f32[8,32,128]{2,1,0:T(8,128)S(1)}, u32[]{:S(2)}) %copy-start.3) | copy-done | bytes 131096
  34.6 4.5 %late.1 = f32[32,8,128]{2,1,0:T(8,128)} custom-call(f32[8,8,32,128]{3,2,1,0:T(8,128)} %get-tuple-element.17.u_ref.refs_0_, f32[8,32,128]{2,1,0:T(8,128)} %refs_1_.3, f32[8,32,128]{2,1,0:T(8,128)} %copy-done.2, f32[8,32,128]{2,1,0:T(8,128)} %copy-done.3, f32[8,8,1,128]{3,2,1,0:T(1,128)} %copy-done.5, f32[32,128]{1,0:T(8,128)} %copy-done.9, ...), custom_call_target="tpu_custom_call" | custom-call | flops 1000000 | bytes 1048576 | tf_op jit(solution)/shard_map/late/pallas_call | solution.py:258
  39.1 13.5 %all_to_all.5.parts_ref = f32[32,8,128]{2,1,0:T(8,128)} all-to-all(f32[32,8,128]{2,1,0:T(8,128)} %late.1), channel_id=1, replica_groups=mesh['gx'=4,'gy'=2,'gz'=4] {'gx','gy','gz'}, dimensions={0} | all-to-all | bytes 262144 | tf_op jit(solution)/shard_map/all_to_all | solution.py:305
  52.6 7.1 %finish.1 = (f32[8,8,32,128]{3,2,1,0:T(8,128)}, f32[1,8]{1,0:T(1,128)}) custom-call(f32[32,8,128]{2,1,0:T(8,128)} %all_to_all.5.parts_ref, f32[8,8,32,128]{3,2,1,0:T(8,128)} %b_ref.3, f32[8,8,32,128]{3,2,1,0:T(8,128)} %get-tuple-element.17.u_ref.refs_0_), custom_call_target="tpu_custom_call" | custom-call | flops 1000000 | bytes 1048576 | tf_op jit(solution)/shard_map/finish/pallas_call | solution.py:258
Async XLA Ops:
  3.3 10.8 %collective-permute-start = (f32[8,32,128]{2,1,0:T(8,128)}, f32[8,32,128]{2,1,0:T(8,128)S(1)}, u32[]{:S(2)}, u32[]{:S(2)}) collective-permute-start(f32[8,32,128]{2,1,0:T(8,128)} %get-tuple-element.13), channel_id=1, source_target_pairs={{0,8},{8,0},{16,24},{24,16},{1,9},{9,1},{17,25},{25,17},{2,10},{10... | collective-permute-start | bytes 393224 | tf_op jit(solution)/shard_map/ppermute | solution.py:271
  6.3 7.8 %collective-permute-start.1 = (f32[8,32,128]{2,1,0:T(8,128)}, f32[8,32,128]{2,1,0:T(8,128)S(1)}, u32[]{:S(2)}, u32[]{:S(2)}) collective-permute-start(f32[8,32,128]{2,1,0:T(8,128)} %get-tuple-element.14), channel_id=1, source_target_pairs={{8,16},{16,8},{9,17},{17,9},{10,18},{18,10},{11,19},{19,11},{12,20... | collective-permute-start | bytes 393224 | tf_op jit(solution)/shard_map/ppermute | solution.py:271
  7.0 7.1 %collective-permute-start.2 = (f32[8,8,1,128]{3,2,1,0:T(1,128)}, f32[8,8,1,128]{3,2,1,0:T(1,128)S(1)}, u32[]{:S(2)}, u32[]{:S(2)}) collective-permute-start(f32[8,8,1,128]{3,2,1,0:T(1,128)} %get-tuple-element.15), channel_id=1, source_target_pairs={{0,4},{4,0},{1,5},{5,1},{2,6},{6,2},{3,7},{7,3},{8,12},{12,8},{9,1... | collective-permute-start | bytes 98312 | tf_op jit(solution)/shard_map/ppermute | solution.py:273
  7.1 5.1 %collective-permute-start.4 = (f32[32,128]{1,0:T(8,128)}, f32[32,128]{1,0:T(8,128)S(1)}, u32[]{:S(2)}, u32[]{:S(2)}) collective-permute-start(f32[32,128]{1,0:T(8,128)} %get-tuple-element.16), channel_id=1, source_target_pairs={{1,2},{2,1},{5,6},{6,5},{9,10},{10,9},{13,14},{14,13},{17,18},{18,... | collective-permute-start | bytes 49160 | tf_op jit(solution)/shard_map/ppermute | solution.py:272
  7.7 6.4 %collective-permute-start.3 = (f32[32,128]{1,0:T(8,128)}, f32[32,128]{1,0:T(8,128)S(1)}, u32[]{:S(2)}, u32[]{:S(2)}) collective-permute-start(f32[32,128]{1,0:T(8,128)} %get-tuple-element.16), channel_id=1, source_target_pairs={{0,1},{1,0},{2,3},{3,2},{4,5},{5,4},{6,7},{7,6},{8,9},{9,8},{10,11... | collective-permute-start | bytes 49160 | tf_op jit(solution)/shard_map/ppermute | solution.py:272
  12.2 2.0 %copy-start.6 = (f32[32,128]{1,0:T(8,128)}, f32[32,128]{1,0:T(8,128)S(1)}, u32[]{:S(2)}) copy-start(f32[32,128]{1,0:T(8,128)S(1)} %collective-permute-done.4.refs_6_) | copy-start | bytes 49156
  14.1 0.6 copy-start.7
  14.1 0.6 %copy-start.4 = (f32[8,8,1,128]{3,2,1,0:T(1,128)}, f32[8,8,1,128]{3,2,1,0:T(1,128)S(1)}, u32[]{:S(2)}) copy-start(f32[8,8,1,128]{3,2,1,0:T(1,128)S(1)} %collective-permute-done.2.refs_4_) | copy-start | bytes 98308
  14.1 0.7 %copy-start = (f32[8,32,128]{2,1,0:T(8,128)}, f32[8,32,128]{2,1,0:T(8,128)S(1)}, u32[]{:S(2)}) copy-start(f32[8,32,128]{2,1,0:T(8,128)S(1)} %collective-permute-done.refs_2_) | copy-start | bytes 393220
  14.8 0.7 %copy-start.1 = (f32[8,32,128]{2,1,0:T(8,128)}, f32[8,32,128]{2,1,0:T(8,128)S(1)}, u32[]{:S(2)}) copy-start(f32[8,32,128]{2,1,0:T(8,128)S(1)} %collective-permute-done.1.refs_3_) | copy-start | bytes 393220
  20.2 13.1 %collective-permute-start.5 = (f32[8,32,128]{2,1,0:T(8,128)}, f32[8,32,128]{2,1,0:T(8,128)S(1)}, u32[]{:S(2)}, u32[]{:S(2)}) collective-permute-start(f32[8,32,128]{2,1,0:T(8,128)} %get-tuple-element.18), channel_id=1, source_target_pairs={{0,8},{8,0},{16,24},{24,16},{1,9},{9,1},{17,25},{25,17},{2,10},{10... | collective-permute-start | bytes 393224 | tf_op jit(solution)/shard_map/ppermute | solution.py:271
  24.4 8.9 %collective-permute-start.6 = (f32[8,32,128]{2,1,0:T(8,128)}, f32[8,32,128]{2,1,0:T(8,128)S(1)}, u32[]{:S(2)}, u32[]{:S(2)}) collective-permute-start(f32[8,32,128]{2,1,0:T(8,128)} %get-tuple-element.19), channel_id=1, source_target_pairs={{8,16},{16,8},{9,17},{17,9},{10,18},{18,10},{11,19},{19,11},{12,20... | collective-permute-start | bytes 393224 | tf_op jit(solution)/shard_map/ppermute | solution.py:271
  25.1 8.2 %collective-permute-start.7 = (f32[8,8,1,128]{3,2,1,0:T(1,128)}, f32[8,8,1,128]{3,2,1,0:T(1,128)S(1)}, u32[]{:S(2)}, u32[]{:S(2)}) collective-permute-start(f32[8,8,1,128]{3,2,1,0:T(1,128)} %get-tuple-element.20), channel_id=1, source_target_pairs={{0,4},{4,0},{1,5},{5,1},{2,6},{6,2},{3,7},{7,3},{8,12},{12,8},{9,1... | collective-permute-start | bytes 98312 | tf_op jit(solution)/shard_map/ppermute | solution.py:273
  25.2 8.1 %collective-permute-start.9 = (f32[32,128]{1,0:T(8,128)}, f32[32,128]{1,0:T(8,128)S(1)}, u32[]{:S(2)}, u32[]{:S(2)}) collective-permute-start(f32[32,128]{1,0:T(8,128)} %get-tuple-element.21), channel_id=1, source_target_pairs={{1,2},{2,1},{5,6},{6,5},{9,10},{10,9},{13,14},{14,13},{17,18},{18,... | collective-permute-start | bytes 49160 | tf_op jit(solution)/shard_map/ppermute | solution.py:272
  25.8 7.4 %collective-permute-start.8 = (f32[32,128]{1,0:T(8,128)}, f32[32,128]{1,0:T(8,128)S(1)}, u32[]{:S(2)}, u32[]{:S(2)}) collective-permute-start(f32[32,128]{1,0:T(8,128)} %get-tuple-element.21), channel_id=1, source_target_pairs={{0,1},{1,0},{2,3},{3,2},{4,5},{5,4},{6,7},{7,6},{8,9},{9,8},{10,11... | collective-permute-start | bytes 49160 | tf_op jit(solution)/shard_map/ppermute | solution.py:272
  33.3 0.6 %copy-start.8 = (f32[32,128]{1,0:T(8,128)}, f32[32,128]{1,0:T(8,128)S(1)}, u32[]{:S(2)}) copy-start(f32[32,128]{1,0:T(8,128)S(1)} %collective-permute-done.9.refs_6_) | copy-start | bytes 49156
  33.3 0.6 %copy-start.9 = (f32[32,128]{1,0:T(8,128)}, f32[32,128]{1,0:T(8,128)S(1)}, u32[]{:S(2)}) copy-start(f32[32,128]{1,0:T(8,128)S(1)} %collective-permute-done.8.refs_5_) | copy-start | bytes 49156
  33.3 0.6 %copy-start.5 = (f32[8,8,1,128]{3,2,1,0:T(1,128)}, f32[8,8,1,128]{3,2,1,0:T(1,128)S(1)}, u32[]{:S(2)}) copy-start(f32[8,8,1,128]{3,2,1,0:T(1,128)S(1)} %collective-permute-done.7.refs_4_) | copy-start | bytes 98308
  33.3 0.7 %copy-start.2 = (f32[8,32,128]{2,1,0:T(8,128)}, f32[8,32,128]{2,1,0:T(8,128)S(1)}, u32[]{:S(2)}) copy-start(f32[8,32,128]{2,1,0:T(8,128)S(1)} %collective-permute-done.5.refs_2_) | copy-start | bytes 393220
  34.0 0.7 %copy-start.3 = (f32[8,32,128]{2,1,0:T(8,128)}, f32[8,32,128]{2,1,0:T(8,128)S(1)}, u32[]{:S(2)}) copy-start(f32[8,32,128]{2,1,0:T(8,128)S(1)} %collective-permute-done.6.refs_3_) | copy-start | bytes 393220

commit v2 on v1

--- a/solution.py
+++ b/solution.py
@@ -261,6 +261,7 @@
         in_specs=[pl.BlockSpec(memory_space=pltpu.VMEM)] * len(operands),
         out_specs=jax.tree.map(lambda _: pl.BlockSpec(memory_space=pltpu.VMEM), out_shape),
         scratch_shapes=list(scratch),
+        compiler_params=pltpu.CompilerParams(vmem_limit_bytes=8 << 20),
         cost_estimate=pl.CostEstimate(flops=flops, bytes_accessed=1 << 20, transcendentals=0),
         name=name,
     )(*operands)

time: 60.1 us -> 49 us (0.82)
  Pallas kernels: 22.7 us -> 12.8 us
  local copies, waits for them, and re-layouts: 2.58 us -> 1.23 us
    pallas_call x5, Pallas kernels: 22.7 us -> 12.8 us  [call(): pl.pallas_call(kernel, out_shape=out_shape, in_specs=[pl.BlockSpec(memory...]
    unnamed x20 -> x6, local copies, waits for them, and re-layouts: 2.58 us -> 1.23 us
  transfers between devices with their start and end apart: 10 -> 10, of which waited for: 1 -> 2; matrix products, arithmetic and copies ran while one was open for 0% -> 0% of each run, Pallas kernels for 6% -> 3%
where the time goes in v2:
time: 49 us; the launch traced here: 48.8 us
  starting transfers between devices  18.3 us (37%)
  blocking collectives  13.7 us (28%)
  Pallas kernels  12.8 us (26%)
  waiting for transfers between devices  1.95 us (4%)
  local copies, waits for them, and re-layouts  1.23 us (3%)
  between operations  0.74 us (2%)
    all_to_all x1, blocking collectives, body(): parts = lax.all_to_all(copies, AXES, 0, 0, tiled=True)  13.7 us
    pallas_call x5, Pallas kernels, call(): pl.pallas_call(kernel, out_shape=out_shape, in_specs=[pl.BlockSpec(memory...  12.8 us
    ppermute x4, starting transfers between devices, trade(): got_z = [lax.ppermute(ends, 'gz', pairs) for pairs in pairs_z]  9.57 us
    ppermute x4, starting transfers between devices, trade(): lax.ppermute(face, 'gx', pairs)  8.63 us
    ppermute x4, waiting for transfers between devices, trade(): got_z = [lax.ppermute(ends, 'gz', pairs) for pairs in pairs_z]  1.93 us
    unnamed x6, local copies, waits for them, and re-layouts  1.23 us
  transfers between devices with their start and end apart: 10, of which 2 were waited for; matrix products, arithmetic and copies ran while one was open for 0% of the time, Pallas kernels for 3%

profile of v2, /device:TPU:0, one launch (start us, length us, event | category | flops | bytes accessed | tf_op | source)
XLA Modules:
  0.0 48.8 jit_solution(5323946043011189674)
XLA Ops:
  0.6 0.0 copy-start
  0.6 1.2 %copy-done = f32[8,8,32,128]{3,2,1,0:T(8,128)S(1)} copy-done((f32[8,8,32,128]{3,2,1,0:T(8,128)S(1)}, f32[8,8,32,128]{3,2,1,0:T(8,128)}, u32[]{:S(2)}) %copy-start) | copy-done | bytes 1048600
  1.9 0.0 copy-start.2
  1.9 0.9 %pack.1 = (f32[8,32,128]{2,1,0:T(8,128)S(1)}, f32[8,32,128]{2,1,0:T(8,128)S(1)}, f32[8,8,1,128]{3,2,1,0:T(1,128)S(1)}, f32[32,128]{1,0:T(8,128)S(1)}) custom-call(f32[8,8,32,128]{3,2,1,0:T(8,128)S(1)} %copy-done), custom_call_target="tpu_custom_call" | custom-call | flops 1000000 | bytes 1048576 | tf_op jit(solution)/shard_map/pack/pallas_call | solution.py:258
  2.7 3.0 %collective-permute-start = (f32[8,32,128]{2,1,0:T(8,128)S(1)}, f32[8,32,128]{2,1,0:T(8,128)S(1)}, u32[]{:S(2)}, u32[]{:S(2)}) collective-permute-start(f32[8,32,128]{2,1,0:T(8,128)S(1)} %get-tuple-element.13), channel_id=1, source_target_pairs={{0,8},{8,0},{16,24},{24,16},{1,9},{9,1},{17,25},{25,17},{2,10},{10... | collective-permute-start | bytes 393224 | tf_op jit(solution)/shard_map/ppermute | solution.py:272
  5.8 0.7 %collective-permute-start.1 = (f32[8,32,128]{2,1,0:T(8,128)S(1)}, f32[8,32,128]{2,1,0:T(8,128)S(1)}, u32[]{:S(2)}, u32[]{:S(2)}) collective-permute-start(f32[8,32,128]{2,1,0:T(8,128)S(1)} %get-tuple-element.14), channel_id=1, source_target_pairs={{8,16},{16,8},{9,17},{17,9},{10,18},{18,10},{11,19},{19,11},{12,20... | collective-permute-start | bytes 393224 | tf_op jit(solution)/shard_map/ppermute | solution.py:272
  6.4 0.1 collective-permute-start.2
  6.5 0.7 %collective-permute-start.4 = (f32[32,128]{1,0:T(8,128)S(1)}, f32[32,128]{1,0:T(8,128)S(1)}, u32[]{:S(2)}, u32[]{:S(2)}) collective-permute-start(f32[32,128]{1,0:T(8,128)S(1)} %get-tuple-element.16), channel_id=1, source_target_pairs={{1,2},{2,1},{5,6},{6,5},{9,10},{10,9},{13,14},{14,13},{17,18},{18,... | collective-permute-start | bytes 49160 | tf_op jit(solution)/shard_map/ppermute | solution.py:273
  7.2 4.5 %collective-permute-start.3 = (f32[32,128]{1,0:T(8,128)S(1)}, f32[32,128]{1,0:T(8,128)S(1)}, u32[]{:S(2)}, u32[]{:S(2)}) collective-permute-start(f32[32,128]{1,0:T(8,128)S(1)} %get-tuple-element.16), channel_id=1, source_target_pairs={{0,1},{1,0},{2,3},{3,2},{4,5},{5,4},{6,7},{7,6},{8,9},{9,8},{10,11... | collective-permute-start | bytes 49160 | tf_op jit(solution)/shard_map/ppermute | solution.py:273
  11.6 0.0 collective-permute-done.4.refs_6_
  11.6 1.7 %collective-permute-done.3.refs_5_ = f32[32,128]{1,0:T(8,128)S(1)} collective-permute-done((f32[32,128]{1,0:T(8,128)S(1)}, f32[32,128]{1,0:T(8,128)S(1)}, u32[]{:S(2)}, u32[]{:S(2)}) %collective-permute-start.3) | collective-permute-done | bytes 16416 | tf_op jit(solution)/shard_map/ppermute | solution.py:273
  13.3 0.0 collective-permute-done.2.refs_4_
  13.4 0.0 collective-permute-done.refs_2_
  13.4 0.0 collective-permute-done.1.refs_3_
  13.4 0.0 copy-done.2
  13.4 2.4 %operator.1 = (f32[8,8,32,128]{3,2,1,0:T(8,128)S(1)}, f32[8,32,128]{2,1,0:T(8,128)S(1)}, f32[8,32,128]{2,1,0:T(8,128)S(1)}, f32[8,8,1,128]{3,2,1,0:T(1,128)S(1)}, f32[32,128]{1,0:T(8,128)S(1)}) custom-call(f32[8,8,32,128]{3,2,1,0:T(8,128)S(1)} %copy-done, f32[8,32,128]{2,1,0:T(8,128)S(1)} %copy-done.2, f32[8,32,128]{2,1,0:T(8,128)S(1)} %collective-permute-done.refs_2_, ...), custom_call_target="tpu_custom_call" | custom-call | flops 1000000 | bytes 1048576 | tf_op jit(solution)/shard_map/operator/pallas_call | solution.py:258
  15.8 4.3 %collective-permute-start.5 = (f32[8,32,128]{2,1,0:T(8,128)S(1)}, f32[8,32,128]{2,1,0:T(8,128)S(1)}, u32[]{:S(2)}, u32[]{:S(2)}) collective-permute-start(f32[8,32,128]{2,1,0:T(8,128)S(1)} %get-tuple-element.18), channel_id=1, source_target_pairs={{0,8},{8,0},{16,24},{24,16},{1,9},{9,1},{17,25},{25,17},{2,10},{10... | collective-permute-start | bytes 393224 | tf_op jit(solution)/shard_map/ppermute | solution.py:272
  20.1 0.7 %collective-permute-start.6 = (f32[8,32,128]{2,1,0:T(8,128)S(1)}, f32[8,32,128]{2,1,0:T(8,128)S(1)}, u32[]{:S(2)}, u32[]{:S(2)}) collective-permute-start(f32[8,32,128]{2,1,0:T(8,128)S(1)} %get-tuple-element.19), channel_id=1, source_target_pairs={{8,16},{16,8},{9,17},{17,9},{10,18},{18,10},{11,19},{19,11},{12,20... | collective-permute-start | bytes 393224 | tf_op jit(solution)/shard_map/ppermute | solution.py:272
  20.8 0.1 collective-permute-start.7
  20.8 0.7 %collective-permute-start.9 = (f32[32,128]{1,0:T(8,128)S(1)}, f32[32,128]{1,0:T(8,128)S(1)}, u32[]{:S(2)}, u32[]{:S(2)}) collective-permute-start(f32[32,128]{1,0:T(8,128)S(1)} %get-tuple-element.21), channel_id=1, source_target_pairs={{1,2},{2,1},{5,6},{6,5},{9,10},{10,9},{13,14},{14,13},{17,18},{18,... | collective-permute-start | bytes 49160 | tf_op jit(solution)/shard_map/ppermute | solution.py:273
  21.5 3.8 %collective-permute-start.8 = (f32[32,128]{1,0:T(8,128)S(1)}, f32[32,128]{1,0:T(8,128)S(1)}, u32[]{:S(2)}, u32[]{:S(2)}) collective-permute-start(f32[32,128]{1,0:T(8,128)S(1)} %get-tuple-element.21), channel_id=1, source_target_pairs={{0,1},{1,0},{2,3},{3,2},{4,5},{5,4},{6,7},{7,6},{8,9},{9,8},{10,11... | collective-permute-start | bytes 49160 | tf_op jit(solution)/shard_map/ppermute | solution.py:273
  25.3 1.5 %early.1.refs_7_ = f32[8,128]{1,0:T(8,128)S(1)} custom-call(f32[8,8,32,128]{3,2,1,0:T(8,128)S(1)} %copy-done, f32[8,8,32,128]{3,2,1,0:T(8,128)S(1)} %get-tuple-element.17.u_ref.refs_0_), custom_call_target="tpu_custom_call" | custom-call | flops 30000000 | bytes 1048576 | tf_op jit(solution)/shard_map/early/pallas_call | solution.py:258
  26.8 0.0 copy-start.1
  26.8 0.0 collective-permute-done.9.refs_6_
  26.8 0.2 collective-permute-done.8.refs_5_
  27.0 0.0 collective-permute-done.7.refs_4_
  27.0 0.0 collective-permute-done.5.refs_2_
  27.0 0.0 collective-permute-done.6.refs_3_
  27.0 2.5 %late.1 = f32[32,8,128]{2,1,0:T(8,128)S(1)} custom-call(f32[8,8,32,128]{3,2,1,0:T(8,128)S(1)} %get-tuple-element.17.u_ref.refs_0_, f32[8,32,128]{2,1,0:T(8,128)S(1)} %copy-done.2, f32[8,32,128]{2,1,0:T(8,128)S(1)} %collective-permute-done.5.refs_2_, f32[8,32,128]{2,1,0:T(8,128)S(1)} %collective-permute-done.6.refs_3_, ...), custom_call_target="tpu_custom_call" | custom-call | flops 1000000 | bytes 1048576 | tf_op jit(solution)/shard_map/late/pallas_call | solution.py:258
  29.5 13.7 %all_to_all.5.parts_ref = f32[32,8,128]{2,1,0:T(8,128)S(1)} all-to-all(f32[32,8,128]{2,1,0:T(8,128)S(1)} %late.1), channel_id=1, replica_groups=mesh['gx'=4,'gy'=2,'gz'=4] {'gx','gy','gz'}, dimensions={0} | all-to-all | bytes 262144 | tf_op jit(solution)/shard_map/all_to_all | solution.py:306
  43.2 0.0 copy-done.1
  43.3 5.5 %finish.1 = (f32[8,8,32,128]{3,2,1,0:T(8,128)}, f32[1,8]{1,0:T(1,128)}) custom-call(f32[32,8,128]{2,1,0:T(8,128)S(1)} %all_to_all.5.parts_ref, f32[8,8,32,128]{3,2,1,0:T(8,128)S(1)} %copy-done.1, f32[8,8,32,128]{3,2,1,0:T(8,128)S(1)} %get-tuple-element.17.u_ref.refs_0_), custom_call_target="tpu_custom_call" | custom-call | flops 1000000 | bytes 1048576 | tf_op jit(solution)/shard_map/finish/pallas_call | solution.py:258
Async XLA Ops:
  0.6 1.2 %copy-start = (f32[8,8,32,128]{3,2,1,0:T(8,128)S(1)}, f32[8,8,32,128]{3,2,1,0:T(8,128)}, u32[]{:S(2)}) copy-start(f32[8,8,32,128]{3,2,1,0:T(8,128)} %b_ref.3) | copy-start | bytes 3145732
  1.9 11.5 %copy-start.2 = (f32[8,32,128]{2,1,0:T(8,128)S(1)}, f32[8,32,128]{2,1,0:T(8,128)}, u32[]{:S(2)}) copy-start(f32[8,32,128]{2,1,0:T(8,128)} %refs_1_.3) | copy-start | bytes 393220
  2.7 10.6 %collective-permute-start = (f32[8,32,128]{2,1,0:T(8,128)S(1)}, f32[8,32,128]{2,1,0:T(8,128)S(1)}, u32[]{:S(2)}, u32[]{:S(2)}) collective-permute-start(f32[8,32,128]{2,1,0:T(8,128)S(1)} %get-tuple-element.13), channel_id=1, source_target_pairs={{0,8},{8,0},{16,24},{24,16},{1,9},{9,1},{17,25},{25,17},{2,10},{10... | collective-permute-start | bytes 393224 | tf_op jit(solution)/shard_map/ppermute | solution.py:272
  5.8 7.6 %collective-permute-start.1 = (f32[8,32,128]{2,1,0:T(8,128)S(1)}, f32[8,32,128]{2,1,0:T(8,128)S(1)}, u32[]{:S(2)}, u32[]{:S(2)}) collective-permute-start(f32[8,32,128]{2,1,0:T(8,128)S(1)} %get-tuple-element.14), channel_id=1, source_target_pairs={{8,16},{16,8},{9,17},{17,9},{10,18},{18,10},{11,19},{19,11},{12,20... | collective-permute-start | bytes 393224 | tf_op jit(solution)/shard_map/ppermute | solution.py:272
  6.4 6.9 %collective-permute-start.2 = (f32[8,8,1,128]{3,2,1,0:T(1,128)S(1)}, f32[8,8,1,128]{3,2,1,0:T(1,128)S(1)}, u32[]{:S(2)}, u32[]{:S(2)}) collective-permute-start(f32[8,8,1,128]{3,2,1,0:T(1,128)S(1)} %get-tuple-element.15), channel_id=1, source_target_pairs={{0,4},{4,0},{1,5},{5,1},{2,6},{6,2},{3,7},{7,3},{8,12},{12,8},{9,1... | collective-permute-start | bytes 98312 | tf_op jit(solution)/shard_map/ppermute | solution.py:274
  6.5 5.1 %collective-permute-start.4 = (f32[32,128]{1,0:T(8,128)S(1)}, f32[32,128]{1,0:T(8,128)S(1)}, u32[]{:S(2)}, u32[]{:S(2)}) collective-permute-start(f32[32,128]{1,0:T(8,128)S(1)} %get-tuple-element.16), channel_id=1, source_target_pairs={{1,2},{2,1},{5,6},{6,5},{9,10},{10,9},{13,14},{14,13},{17,18},{18,... | collective-permute-start | bytes 49160 | tf_op jit(solution)/shard_map/ppermute | solution.py:273
  7.2 6.2 %collective-permute-start.3 = (f32[32,128]{1,0:T(8,128)S(1)}, f32[32,128]{1,0:T(8,128)S(1)}, u32[]{:S(2)}, u32[]{:S(2)}) collective-permute-start(f32[32,128]{1,0:T(8,128)S(1)} %get-tuple-element.16), channel_id=1, source_target_pairs={{0,1},{1,0},{2,3},{3,2},{4,5},{5,4},{6,7},{7,6},{8,9},{9,8},{10,11... | collective-permute-start | bytes 49160 | tf_op jit(solution)/shard_map/ppermute | solution.py:273
  15.8 11.2 %collective-permute-start.5 = (f32[8,32,128]{2,1,0:T(8,128)S(1)}, f32[8,32,128]{2,1,0:T(8,128)S(1)}, u32[]{:S(2)}, u32[]{:S(2)}) collective-permute-start(f32[8,32,128]{2,1,0:T(8,128)S(1)} %get-tuple-element.18), channel_id=1, source_target_pairs={{0,8},{8,0},{16,24},{24,16},{1,9},{9,1},{17,25},{25,17},{2,10},{10... | collective-permute-start | bytes 393224 | tf_op jit(solution)/shard_map/ppermute | solution.py:272
  20.1 6.9 %collective-permute-start.6 = (f32[8,32,128]{2,1,0:T(8,128)S(1)}, f32[8,32,128]{2,1,0:T(8,128)S(1)}, u32[]{:S(2)}, u32[]{:S(2)}) collective-permute-start(f32[8,32,128]{2,1,0:T(8,128)S(1)} %get-tuple-element.19), channel_id=1, source_target_pairs={{8,16},{16,8},{9,17},{17,9},{10,18},{18,10},{11,19},{19,11},{12,20... | collective-permute-start | bytes 393224 | tf_op jit(solution)/shard_map/ppermute | solution.py:272
  20.8 6.3 %collective-permute-start.7 = (f32[8,8,1,128]{3,2,1,0:T(1,128)S(1)}, f32[8,8,1,128]{3,2,1,0:T(1,128)S(1)}, u32[]{:S(2)}, u32[]{:S(2)}) collective-permute-start(f32[8,8,1,128]{3,2,1,0:T(1,128)S(1)} %get-tuple-element.20), channel_id=1, source_target_pairs={{0,4},{4,0},{1,5},{5,1},{2,6},{6,2},{3,7},{7,3},{8,12},{12,8},{9,1... | collective-permute-start | bytes 98312 | tf_op jit(solution)/shard_map/ppermute | solution.py:274
  20.8 6.0 %collective-permute-start.9 = (f32[32,128]{1,0:T(8,128)S(1)}, f32[32,128]{1,0:T(8,128)S(1)}, u32[]{:S(2)}, u32[]{:S(2)}) collective-permute-start(f32[32,128]{1,0:T(8,128)S(1)} %get-tuple-element.21), channel_id=1, source_target_pairs={{1,2},{2,1},{5,6},{6,5},{9,10},{10,9},{13,14},{14,13},{17,18},{18,... | collective-permute-start | bytes 49160 | tf_op jit(solution)/shard_map/ppermute | solution.py:273
  21.5 5.5 %collective-permute-start.8 = (f32[32,128]{1,0:T(8,128)S(1)}, f32[32,128]{1,0:T(8,128)S(1)}, u32[]{:S(2)}, u32[]{:S(2)}) collective-permute-start(f32[32,128]{1,0:T(8,128)S(1)} %get-tuple-element.21), channel_id=1, source_target_pairs={{0,1},{1,0},{2,3},{3,2},{4,5},{5,4},{6,7},{7,6},{8,9},{9,8},{10,11... | collective-permute-start | bytes 49160 | tf_op jit(solution)/shard_map/ppermute | solution.py:273
  26.8 16.5 %copy-start.1 = (f32[8,8,32,128]{3,2,1,0:T(8,128)S(1)}, f32[8,8,32,128]{3,2,1,0:T(8,128)}, u32[]{:S(2)}) copy-start(f32[8,8,32,128]{3,2,1,0:T(8,128)} %b_ref.3) | copy-start | bytes 3145732

commit v3 on v2

--- a/solution.py
+++ b/solution.py
@@ -17,6 +17,18 @@
     first = [(i, j) for a in range(0, count - 1, 2) for i, j in ((a, a + 1), (a + 1, a))]
     second = [(i, j) for a in range(1, count - 1, 2) for i, j in ((a, a + 1), (a + 1, a))]
     return [pairs for pairs in (first, second) if pairs]
+
+
+def swap(values, axis, pairs):
+    side = lax.axis_size("gy")
+    if axis == "gy" or side % 2:
+        return lax.ppermute(values, axis, pairs)
+    count = lax.axis_size(axis)
+    named = {i for i, _ in pairs}
+    at = (lambda i, y: i * side + y) if axis == "gx" else (lambda i, y: y * count + i)
+    joint = [(at(i, y), at(j, y)) for i, j in pairs for y in range(side)]
+    joint += [(at(i, y), at(i, y ^ 1)) for i in range(count) if i not in named for y in range(side)]
+    return lax.ppermute(values, ("gx", "gy") if axis == "gx" else ("gy", "gz"), joint)
 
 
 def rounds_of():
@@ -58,27 +70,31 @@
     z_ref[...] = lax.fori_loop(0, width, field, jnp.zeros((ny, LANES), F32))
 
 
-def pick(odd, refs, load):
-    first = load(refs[0]) if refs else 0.0
+def pick(axis, refs, load):
+    if not refs:
+        return 0.0, 0.0
+    odd, at = parity(axis), lax.axis_index(axis)
+    first = load(refs[0])
     second = load(refs[1]) if len(refs) > 1 else jnp.zeros_like(first)
-    return jnp.where(odd, first, second), jnp.where(odd, second, first)
+    low = jnp.where(at == 0, 0.0, jnp.where(odd, first, second))
+    high = jnp.where(at == lax.axis_size(axis) - 1, 0.0, jnp.where(odd, second, first))
+    return low, high
 
 
 def apply_operator(v_ref, shift_ref, x_in, y_in, z_in, out_ref, packed=None):
     width, nx, ny, _ = v_ref.shape
-    odd_x, odd_y, odd_z = parity("gx"), parity("gy"), parity("gz")
     lane = lax.broadcasted_iota(jnp.int32, (ny, LANES), 1)
     row = lax.broadcasted_iota(jnp.int32, (ny, LANES), 0)
-    low_z, high_z = pick(odd_z, z_in, lambda ref: ref[...])
+    low_z, high_z = pick("gz", z_in, lambda ref: ref[...])
     ends = jnp.where(
         lax.rem(lane, 2) == 0, pltpu.roll(low_z, 1, 1), pltpu.roll(high_z, LANES - 1, 1)
     )
 
     def field(f, packed):
-        low_x, high_x = pick(odd_x, x_in, lambda ref: ref[f])
+        low_x, high_x = pick("gx", x_in, lambda ref: ref[f])
         for x in range(nx):
             m = f * nx + x
-            low_y, high_y = pick(odd_y, y_in, lambda ref: ref[f, x])
+            low_y, high_y = pick("gy", y_in, lambda ref: ref[f, x])
             v = v_ref[f, x]
             end = pltpu.roll(ends, lax.rem(LANES - 2 * m, LANES), 1)
             beside = (v_ref[f, x - 1] if x > 0 else low_x) + (v_ref[f, x + 1] if x < nx - 1 else high_x)
@@ -269,9 +285,9 @@
 
 def trade(x_faces, y_faces, ends):
     pairs_x, pairs_y, pairs_z = (swap_pairs(lax.axis_size(axis)) for axis in AXES)
-    got_x = [lax.ppermute(face, "gx", pairs) for face, pairs in zip(x_faces, pairs_x)]
-    got_z = [lax.ppermute(ends, "gz", pairs) for pairs in pairs_z]
-    got_y = [lax.ppermute(face, "gy", pairs) for face, pairs in zip(y_faces, pairs_y)]
+    got_x = [swap(face, "gx", pairs) for face, pairs in zip(x_faces, pairs_x)]
+    got_z = [swap(ends, "gz", pairs) for pairs in pairs_z]
+    got_y = [swap(face, "gy", pairs) for face, pairs in zip(y_faces, pairs_y)]
     return [*got_x, *got_y, *got_z]
 
 

time: 49 us -> 43.9 us (0.90)
  starting transfers between devices: 18.3 us -> 14 us
  blocking collectives: 13.7 us -> 13.1 us
    ppermute x10, starting transfers between devices: 18.3 us -> 14 us  [the longest x8 13 us: swap(): lax.ppermute(values, ('gx', 'gy') if axis == 'gx' else ('gy', 'gz'), joint)]
    all_to_all x1, blocking collectives: 13.7 us -> 13.1 us  [body(): parts = lax.all_to_all(copies, AXES, 0, 0, tiled=True)]
where the time goes in v3:
time: 43.9 us; the launch traced here: 43.8 us
  starting transfers between devices  14 us (32%)
  blocking collectives  13.1 us (30%)
  Pallas kernels  12.8 us (29%)
  waiting for transfers between devices  1.94 us (4%)
  local copies, waits for them, and re-layouts  1.23 us (3%)
  between operations  0.69 us (2%)
    all_to_all x1, blocking collectives, body(): parts = lax.all_to_all(copies, AXES, 0, 0, tiled=True)  13.1 us
    ppermute x8, starting transfers between devices, swap(): lax.ppermute(values, ('gx', 'gy') if axis == 'gx' else ('gy', 'gz'), joint)  13 us
    pallas_call x5, Pallas kernels, call(): pl.pallas_call(kernel, out_shape=out_shape, in_specs=[pl.BlockSpec(memory...  12.8 us
    ppermute x8, waiting for transfers between devices, swap(): lax.ppermute(values, ('gx', 'gy') if axis == 'gx' else ('gy', 'gz'), joint)  1.94 us
    unnamed x6, local copies, waits for them, and re-layouts  1.23 us
    ppermute x2, starting transfers between devices, swap(): return lax.ppermute(values, axis, pairs)  1.01 us
  transfers between devices with their start and end apart: 10, of which 2 were waited for; matrix products, arithmetic and copies ran while one was open for 0% of the time, Pallas kernels for 3%

profile of v3, /device:TPU:0, one launch (start us, length us, event | category | flops | bytes accessed | tf_op | source)
XLA Modules:
  0.0 43.8 jit_solution(13453684588253168512)
XLA Ops:
  0.6 0.0 copy-start
  0.6 1.2 %copy-done = f32[8,8,32,128]{3,2,1,0:T(8,128)S(1)} copy-done((f32[8,8,32,128]{3,2,1,0:T(8,128)S(1)}, f32[8,8,32,128]{3,2,1,0:T(8,128)}, u32[]{:S(2)}) %copy-start) | copy-done | bytes 1048600
  1.9 0.0 copy-start.2
  1.9 0.9 %pack.1 = (f32[8,32,128]{2,1,0:T(8,128)S(1)}, f32[8,32,128]{2,1,0:T(8,128)S(1)}, f32[8,8,1,128]{3,2,1,0:T(1,128)S(1)}, f32[32,128]{1,0:T(8,128)S(1)}) custom-call(f32[8,8,32,128]{3,2,1,0:T(8,128)S(1)} %copy-done), custom_call_target="tpu_custom_call" | custom-call | flops 1000000 | bytes 1048576 | tf_op jit(solution)/shard_map/pack/pallas_call | solution.py:274
  2.7 3.0 %collective-permute-start = (f32[8,32,128]{2,1,0:T(8,128)S(1)}, f32[8,32,128]{2,1,0:T(8,128)S(1)}, u32[]{:S(2)}, u32[]{:S(2)}) collective-permute-start(f32[8,32,128]{2,1,0:T(8,128)S(1)} %get-tuple-element.13), channel_id=1, source_target_pairs={{0,8},{4,12},{8,0},{12,4},{16,24},{20,28},{24,16},{28,20},{1,9},{5... | collective-permute-start | bytes 393224 | tf_op jit(solution)/shard_map/ppermute | solution.py:31
  5.8 0.0 collective-permute-start.1
  5.8 0.5 %collective-permute-start.2 = (f32[8,8,1,128]{3,2,1,0:T(1,128)S(1)}, f32[8,8,1,128]{3,2,1,0:T(1,128)S(1)}, u32[]{:S(2)}, u32[]{:S(2)}) collective-permute-start(f32[8,8,1,128]{3,2,1,0:T(1,128)S(1)} %get-tuple-element.15), channel_id=1, source_target_pairs={{0,4},{4,0},{1,5},{5,1},{2,6},{6,2},{3,7},{7,3},{8,12},{12,8},{9,1... | collective-permute-start | bytes 98312 | tf_op jit(solution)/shard_map/ppermute | solution.py:25
  6.3 0.0 collective-permute-start.4
  6.3 3.1 %collective-permute-start.3 = (f32[32,128]{1,0:T(8,128)S(1)}, f32[32,128]{1,0:T(8,128)S(1)}, u32[]{:S(2)}, u32[]{:S(2)}) collective-permute-start(f32[32,128]{1,0:T(8,128)S(1)} %get-tuple-element.16), channel_id=1, source_target_pairs={{0,1},{4,5},{1,0},{5,4},{2,3},{6,7},{3,2},{7,6},{8,9},{12,13},{9,8... | collective-permute-start | bytes 49160 | tf_op jit(solution)/shard_map/ppermute | solution.py:31
  9.4 0.0 collective-permute-done.4.refs_6_
  9.4 1.7 %collective-permute-done.3.refs_5_ = f32[32,128]{1,0:T(8,128)S(1)} collective-permute-done((f32[32,128]{1,0:T(8,128)S(1)}, f32[32,128]{1,0:T(8,128)S(1)}, u32[]{:S(2)}, u32[]{:S(2)}) %collective-permute-start.3) | collective-permute-done | bytes 16416 | tf_op jit(solution)/shard_map/ppermute | solution.py:31
  11.1 0.0 collective-permute-done.2.refs_4_
  11.1 0.0 collective-permute-done.refs_2_
  11.1 0.0 collective-permute-done.1.refs_3_
  11.1 0.0 copy-done.2
  11.2 2.4 %operator.1 = (f32[8,8,32,128]{3,2,1,0:T(8,128)S(1)}, f32[8,32,128]{2,1,0:T(8,128)S(1)}, f32[8,32,128]{2,1,0:T(8,128)S(1)}, f32[8,8,1,128]{3,2,1,0:T(1,128)S(1)}, f32[32,128]{1,0:T(8,128)S(1)}) custom-call(f32[8,8,32,128]{3,2,1,0:T(8,128)S(1)} %copy-done, f32[8,32,128]{2,1,0:T(8,128)S(1)} %copy-done.2, f32[8,32,128]{2,1,0:T(8,128)S(1)} %collective-permute-done.refs_2_, ...), custom_call_target="tpu_custom_call" | custom-call | flops 1000000 | bytes 1048576 | tf_op jit(solution)/shard_map/operator/pallas_call | solution.py:274
  13.6 3.7 %collective-permute-start.5 = (f32[8,32,128]{2,1,0:T(8,128)S(1)}, f32[8,32,128]{2,1,0:T(8,128)S(1)}, u32[]{:S(2)}, u32[]{:S(2)}) collective-permute-start(f32[8,32,128]{2,1,0:T(8,128)S(1)} %get-tuple-element.18), channel_id=1, source_target_pairs={{0,8},{4,12},{8,0},{12,4},{16,24},{20,28},{24,16},{28,20},{1,9},{5... | collective-permute-start | bytes 393224 | tf_op jit(solution)/shard_map/ppermute | solution.py:31
  17.3 0.0 collective-permute-start.6
  17.3 0.5 %collective-permute-start.7 = (f32[8,8,1,128]{3,2,1,0:T(1,128)S(1)}, f32[8,8,1,128]{3,2,1,0:T(1,128)S(1)}, u32[]{:S(2)}, u32[]{:S(2)}) collective-permute-start(f32[8,8,1,128]{3,2,1,0:T(1,128)S(1)} %get-tuple-element.20), channel_id=1, source_target_pairs={{0,4},{4,0},{1,5},{5,1},{2,6},{6,2},{3,7},{7,3},{8,12},{12,8},{9,1... | collective-permute-start | bytes 98312 | tf_op jit(solution)/shard_map/ppermute | solution.py:25
  17.8 0.0 collective-permute-start.9
  17.8 3.1 %collective-permute-start.8 = (f32[32,128]{1,0:T(8,128)S(1)}, f32[32,128]{1,0:T(8,128)S(1)}, u32[]{:S(2)}, u32[]{:S(2)}) collective-permute-start(f32[32,128]{1,0:T(8,128)S(1)} %get-tuple-element.21), channel_id=1, source_target_pairs={{0,1},{4,5},{1,0},{5,4},{2,3},{6,7},{3,2},{7,6},{8,9},{12,13},{9,8... | collective-permute-start | bytes 49160 | tf_op jit(solution)/shard_map/ppermute | solution.py:31
  20.9 1.5 %early.1.refs_7_ = f32[8,128]{1,0:T(8,128)S(1)} custom-call(f32[8,8,32,128]{3,2,1,0:T(8,128)S(1)} %copy-done, f32[8,8,32,128]{3,2,1,0:T(8,128)S(1)} %get-tuple-element.17.u_ref.refs_0_), custom_call_target="tpu_custom_call" | custom-call | flops 30000000 | bytes 1048576 | tf_op jit(solution)/shard_map/early/pallas_call | solution.py:274
  22.4 0.0 copy-start.1
  22.4 0.0 collective-permute-done.9.refs_6_
  22.4 0.2 collective-permute-done.8.refs_5_
  22.6 0.0 collective-permute-done.7.refs_4_
  22.6 0.0 collective-permute-done.5.refs_2_
  22.6 0.0 collective-permute-done.6.refs_3_
  22.6 2.5 %late.1 = f32[32,8,128]{2,1,0:T(8,128)S(1)} custom-call(f32[8,8,32,128]{3,2,1,0:T(8,128)S(1)} %get-tuple-element.17.u_ref.refs_0_, f32[8,32,128]{2,1,0:T(8,128)S(1)} %copy-done.2, f32[8,32,128]{2,1,0:T(8,128)S(1)} %collective-permute-done.5.refs_2_, f32[8,32,128]{2,1,0:T(8,128)S(1)} %collective-permute-done.6.refs_3_, ...), custom_call_target="tpu_custom_call" | custom-call | flops 1000000 | bytes 1048576 | tf_op jit(solution)/shard_map/late/pallas_call | solution.py:274
  25.1 13.1 %all_to_all.5.parts_ref = f32[32,8,128]{2,1,0:T(8,128)S(1)} all-to-all(f32[32,8,128]{2,1,0:T(8,128)S(1)} %late.1), channel_id=1, replica_groups=mesh['gx'=4,'gy'=2,'gz'=4] {'gx','gy','gz'}, dimensions={0} | all-to-all | bytes 262144 | tf_op jit(solution)/shard_map/all_to_all | solution.py:322
  38.2 0.0 copy-done.1
  38.2 5.5 %finish.1 = (f32[8,8,32,128]{3,2,1,0:T(8,128)}, f32[1,8]{1,0:T(1,128)}) custom-call(f32[32,8,128]{2,1,0:T(8,128)S(1)} %all_to_all.5.parts_ref, f32[8,8,32,128]{3,2,1,0:T(8,128)S(1)} %copy-done.1, f32[8,8,32,128]{3,2,1,0:T(8,128)S(1)} %get-tuple-element.17.u_ref.refs_0_), custom_call_target="tpu_custom_call" | custom-call | flops 1000000 | bytes 1048576 | tf_op jit(solution)/shard_map/finish/pallas_call | solution.py:274
Async XLA Ops:
  0.6 1.2 %copy-start = (f32[8,8,32,128]{3,2,1,0:T(8,128)S(1)}, f32[8,8,32,128]{3,2,1,0:T(8,128)}, u32[]{:S(2)}) copy-start(f32[8,8,32,128]{3,2,1,0:T(8,128)} %b_ref.3) | copy-start | bytes 3145732
  1.9 9.3 %copy-start.2 = (f32[8,32,128]{2,1,0:T(8,128)S(1)}, f32[8,32,128]{2,1,0:T(8,128)}, u32[]{:S(2)}) copy-start(f32[8,32,128]{2,1,0:T(8,128)} %refs_1_.3) | copy-start | bytes 393220
  2.7 8.4 %collective-permute-start = (f32[8,32,128]{2,1,0:T(8,128)S(1)}, f32[8,32,128]{2,1,0:T(8,128)S(1)}, u32[]{:S(2)}, u32[]{:S(2)}) collective-permute-start(f32[8,32,128]{2,1,0:T(8,128)S(1)} %get-tuple-element.13), channel_id=1, source_target_pairs={{0,8},{4,12},{8,0},{12,4},{16,24},{20,28},{24,16},{28,20},{1,9},{5... | collective-permute-start | bytes 393224 | tf_op jit(solution)/shard_map/ppermute | solution.py:31
  5.8 5.4 %collective-permute-start.1 = (f32[8,32,128]{2,1,0:T(8,128)S(1)}, f32[8,32,128]{2,1,0:T(8,128)S(1)}, u32[]{:S(2)}, u32[]{:S(2)}) collective-permute-start(f32[8,32,128]{2,1,0:T(8,128)S(1)} %get-tuple-element.14), channel_id=1, source_target_pairs={{8,16},{12,20},{16,8},{20,12},{0,4},{4,0},{24,28},{28,24},{9,17},{... | collective-permute-start | bytes 393224 | tf_op jit(solution)/shard_map/ppermute | solution.py:31
  5.8 5.4 %collective-permute-start.2 = (f32[8,8,1,128]{3,2,1,0:T(1,128)S(1)}, f32[8,8,1,128]{3,2,1,0:T(1,128)S(1)}, u32[]{:S(2)}, u32[]{:S(2)}) collective-permute-start(f32[8,8,1,128]{3,2,1,0:T(1,128)S(1)} %get-tuple-element.15), channel_id=1, source_target_pairs={{0,4},{4,0},{1,5},{5,1},{2,6},{6,2},{3,7},{7,3},{8,12},{12,8},{9,1... | collective-permute-start | bytes 98312 | tf_op jit(solution)/shard_map/ppermute | solution.py:25
  6.3 3.2 %collective-permute-start.4 = (f32[32,128]{1,0:T(8,128)S(1)}, f32[32,128]{1,0:T(8,128)S(1)}, u32[]{:S(2)}, u32[]{:S(2)}) collective-permute-start(f32[32,128]{1,0:T(8,128)S(1)} %get-tuple-element.16), channel_id=1, source_target_pairs={{1,2},{5,6},{2,1},{6,5},{0,4},{4,0},{3,7},{7,3},{9,10},{13,14},{10... | collective-permute-start | bytes 49160 | tf_op jit(solution)/shard_map/ppermute | solution.py:31
  6.3 4.9 %collective-permute-start.3 = (f32[32,128]{1,0:T(8,128)S(1)}, f32[32,128]{1,0:T(8,128)S(1)}, u32[]{:S(2)}, u32[]{:S(2)}) collective-permute-start(f32[32,128]{1,0:T(8,128)S(1)} %get-tuple-element.16), channel_id=1, source_target_pairs={{0,1},{4,5},{1,0},{5,4},{2,3},{6,7},{3,2},{7,6},{8,9},{12,13},{9,8... | collective-permute-start | bytes 49160 | tf_op jit(solution)/shard_map/ppermute | solution.py:31
  13.6 9.0 %collective-permute-start.5 = (f32[8,32,128]{2,1,0:T(8,128)S(1)}, f32[8,32,128]{2,1,0:T(8,128)S(1)}, u32[]{:S(2)}, u32[]{:S(2)}) collective-permute-start(f32[8,32,128]{2,1,0:T(8,128)S(1)} %get-tuple-element.18), channel_id=1, source_target_pairs={{0,8},{4,12},{8,0},{12,4},{16,24},{20,28},{24,16},{28,20},{1,9},{5... | collective-permute-start | bytes 393224 | tf_op jit(solution)/shard_map/ppermute | solution.py:31
  17.3 5.4 %collective-permute-start.6 = (f32[8,32,128]{2,1,0:T(8,128)S(1)}, f32[8,32,128]{2,1,0:T(8,128)S(1)}, u32[]{:S(2)}, u32[]{:S(2)}) collective-permute-start(f32[8,32,128]{2,1,0:T(8,128)S(1)} %get-tuple-element.19), channel_id=1, source_target_pairs={{8,16},{12,20},{16,8},{20,12},{0,4},{4,0},{24,28},{28,24},{9,17},{... | collective-permute-start | bytes 393224 | tf_op jit(solution)/shard_map/ppermute | solution.py:31
  17.3 5.4 %collective-permute-start.7 = (f32[8,8,1,128]{3,2,1,0:T(1,128)S(1)}, f32[8,8,1,128]{3,2,1,0:T(1,128)S(1)}, u32[]{:S(2)}, u32[]{:S(2)}) collective-permute-start(f32[8,8,1,128]{3,2,1,0:T(1,128)S(1)} %get-tuple-element.20), channel_id=1, source_target_pairs={{0,4},{4,0},{1,5},{5,1},{2,6},{6,2},{3,7},{7,3},{8,12},{12,8},{9,1... | collective-permute-start | bytes 98312 | tf_op jit(solution)/shard_map/ppermute | solution.py:25
  17.8 4.7 %collective-permute-start.9 = (f32[32,128]{1,0:T(8,128)S(1)}, f32[32,128]{1,0:T(8,128)S(1)}, u32[]{:S(2)}, u32[]{:S(2)}) collective-permute-start(f32[32,128]{1,0:T(8,128)S(1)} %get-tuple-element.21), channel_id=1, source_target_pairs={{1,2},{5,6},{2,1},{6,5},{0,4},{4,0},{3,7},{7,3},{9,10},{13,14},{10... | collective-permute-start | bytes 49160 | tf_op jit(solution)/shard_map/ppermute | solution.py:31
  17.8 4.9 %collective-permute-start.8 = (f32[32,128]{1,0:T(8,128)S(1)}, f32[32,128]{1,0:T(8,128)S(1)}, u32[]{:S(2)}, u32[]{:S(2)}) collective-permute-start(f32[32,128]{1,0:T(8,128)S(1)} %get-tuple-element.21), channel_id=1, source_target_pairs={{0,1},{4,5},{1,0},{5,4},{2,3},{6,7},{3,2},{7,6},{8,9},{12,13},{9,8... | collective-permute-start | bytes 49160 | tf_op jit(solution)/shard_map/ppermute | solution.py:31
  22.4 15.8 %copy-start.1 = (f32[8,8,32,128]{3,2,1,0:T(8,128)S(1)}, f32[8,8,32,128]{3,2,1,0:T(8,128)}, u32[]{:S(2)}) copy-start(f32[8,8,32,128]{3,2,1,0:T(8,128)} %b_ref.3) | copy-start | bytes 3145732

commit v4 on v3

--- a/solution.py
+++ b/solution.py
@@ -39,14 +39,26 @@
     return lax.rem(lax.axis_index(axis), 2) == 1
 
 
-def write_xy_faces(v_ref, x_refs, y_refs):
-    width, nx, ny, _ = v_ref.shape
-    odd_x, odd_y = parity("gx"), parity("gy")
-    for k, ref in enumerate(x_refs):
-        high = jnp.logical_xor(odd_x, k == 0)
-        ref[...] = v_ref[:, jnp.where(high, nx - 1, 0)]
+def x_plane(k, nx):
+    return jnp.where(jnp.logical_xor(parity("gx"), k == 0), nx - 1, 0)
+
+
+def cut_x_kernel(v_ref, *refs):
+    faces, sems = refs[:-1], refs[-1]
+    copies = [
+        pltpu.make_async_copy(v_ref.at[:, x_plane(k, v_ref.shape[1])], ref, sems.at[k]) for k, ref in enumerate(faces)
+    ]
+    for copy in copies:
+        copy.start()
+    for copy in copies:
+        copy.wait()
+
+
+def write_y_faces(v_ref, y_refs):
+    ny = v_ref.shape[2]
+    odd = parity("gy")
     for k, ref in enumerate(y_refs):
-        high = jnp.logical_xor(odd_y, k == 0)
+        high = jnp.logical_xor(odd, k == 0)
         ref[...] = jnp.where(high, v_ref[:, :, ny - 1 : ny, :], v_ref[:, :, 0:1, :])
 
 
@@ -56,10 +68,9 @@
     return jnp.where(hit, pltpu.roll(tile, at, 1), packed)
 
 
-def pack_kernel(nx_r, ny_r, v_ref, *refs):
+def pack_kernel(v_ref, *refs):
     width, nx, ny, _ = v_ref.shape
-    x_refs, y_refs, z_ref = refs[:nx_r], refs[nx_r : nx_r + ny_r], refs[nx_r + ny_r]
-    write_xy_faces(v_ref, x_refs, y_refs)
+    write_y_faces(v_ref, refs[:-1])
     lane = lax.broadcasted_iota(jnp.int32, (ny, LANES), 1)
 
     def field(f, packed):
@@ -67,7 +78,7 @@
             packed = packed_ends(v_ref[f, x], f * nx + x, packed, lane)
         return packed
 
-    z_ref[...] = lax.fori_loop(0, width, field, jnp.zeros((ny, LANES), F32))
+    refs[-1][...] = lax.fori_loop(0, width, field, jnp.zeros((ny, LANES), F32))
 
 
 def pick(axis, refs, load):
@@ -81,7 +92,7 @@
     return low, high
 
 
-def apply_operator(v_ref, shift_ref, x_in, y_in, z_in, out_ref, packed=None):
+def apply_operator(planes, v_ref, shift_ref, x_in, y_in, z_in, out_ref, packed=None):
     width, nx, ny, _ = v_ref.shape
     lane = lax.broadcasted_iota(jnp.int32, (ny, LANES), 1)
     row = lax.broadcasted_iota(jnp.int32, (ny, LANES), 0)
@@ -92,7 +103,7 @@
 
     def field(f, packed):
         low_x, high_x = pick("gx", x_in, lambda ref: ref[f])
-        for x in range(nx):
+        for x in planes:
             m = f * nx + x
             low_y, high_y = pick("gy", y_in, lambda ref: ref[f, x])
             v = v_ref[f, x]
@@ -114,24 +125,47 @@
     return lax.fori_loop(0, width, field, packed)
 
 
-def operator_kernel(nx_r, ny_r, nz_r, *refs):
-    v_ref, shift_ref = refs[:2]
-    at = 2
-    x_in, y_in, z_in = refs[at : at + nx_r], refs[at + nx_r : at + nx_r + ny_r], refs[at + nx_r + ny_r : at + nx_r + ny_r + nz_r]
-    outs = refs[at + nx_r + ny_r + nz_r :]
-    out_ref = outs[0]
-    x_out, y_out, z_out = outs[1 : 1 + nx_r], outs[1 + nx_r : 1 + nx_r + ny_r], outs[1 + nx_r + ny_r]
-    ny = v_ref.shape[2]
-    z_out[...] = apply_operator(v_ref, shift_ref, x_in, y_in, z_in, out_ref, jnp.zeros((ny, LANES), F32))
-    write_xy_faces(out_ref, x_out, y_out)
-
-
-def add_moment(a_ref, b_ref, at, payload):
-    width, nx, ny, _ = a_ref.shape
-    pairs = [(i, j) for i in range(width) for j in range(i + 1)]
-
-    def plane(x, sums):
-        sums = list(sums)
+def split(refs, *counts):
+    parts, at = [], 0
+    for count in counts:
+        parts.append(refs[at : at + count])
+        at += count
+    return (*parts, refs[at:])
+
+
+def inner_planes(ref):
+    return range(1, ref.shape[1] - 1)
+
+
+def outer_planes(ref):
+    return (0, ref.shape[1] - 1)
+
+
+def inner_operator_kernel(ny_r, nz_r, v_ref, shift_ref, *refs):
+    y_in, z_in, (out_ref, ends_ref) = split(refs, ny_r, nz_r)
+    start = jnp.zeros(ends_ref.shape, F32)
+    ends_ref[...] = apply_operator(inner_planes(v_ref), v_ref, shift_ref, (), y_in, z_in, out_ref, start)
+
+
+def outer_operator_kernel(nx_r, ny_r, nz_r, v_ref, shift_ref, inner_ref, ends_ref, *refs):
+    x_in, y_in, z_in, (out_ref,), x_out, y_out, (z_out,) = split(refs, nx_r, ny_r, nz_r, 1, nx_r, ny_r)
+    planes = outer_planes(v_ref)
+    z_out[...] = apply_operator(planes, v_ref, shift_ref, x_in, y_in, z_in, out_ref, ends_ref[...])
+    for k, ref in enumerate(x_out):
+        ref[...] = out_ref[:, x_plane(k, v_ref.shape[1])]
+    write_y_faces(out_ref, y_out)
+
+
+def pairs_of(width):
+    return [(i, j) for i in range(width) for j in range(i + 1)]
+
+
+def moment_sums(first, last, step, a_ref, b_ref, sums):
+    width, _, ny, _ = a_ref.shape
+    pairs = pairs_of(width)
+
+    def plane(k, sums):
+        sums, x = list(sums), first + k * step
         for y in range(0, ny, 8):
             a = [a_ref[f, x, y : y + 8, :] for f in range(width)]
             b = a if b_ref is a_ref else [b_ref[f, x, y : y + 8, :] for f in range(width)]
@@ -139,9 +173,16 @@
                 sums[k] = sums[k] + a[i] * b[j]
         return tuple(sums)
 
-    sums = lax.fori_loop(0, nx, plane, tuple(jnp.zeros((8, LANES), F32) for _ in pairs))
+    return lax.fori_loop(0, -((first - last) // step), plane, tuple(sums))
+
+
+def no_sums(width):
+    return [jnp.zeros((8, LANES), F32) for _ in pairs_of(width)]
+
+
+def put_moment(width, sums, at, payload):
     rows = {}
-    for (i, j), value in zip(pairs, sums):
+    for (i, j), value in zip(pairs_of(width), sums):
         rows[i, j] = rows[j, i] = jnp.sum(value, axis=0, keepdims=True)
     lane = lax.broadcasted_iota(jnp.int32, (8, LANES), 1)
     for i in range(width):
@@ -151,21 +192,30 @@
 
 
 def early_moments_kernel(b_ref, u_ref, out_ref):
-    width = b_ref.shape[0]
-    payload = add_moment(b_ref, b_ref, 0, jnp.zeros((8, LANES), F32))
-    payload = add_moment(b_ref, u_ref, width, payload)
-    out_ref[...] = add_moment(u_ref, u_ref, 2 * width, payload)
-
-
-def late_moments_kernel(nx_r, ny_r, nz_r, *refs):
-    u_ref, shift_ref = refs[:2]
-    at = 2
-    x_in, y_in, z_in = refs[at : at + nx_r], refs[at + nx_r : at + nx_r + ny_r], refs[at + nx_r + ny_r : at + nx_r + ny_r + nz_r]
-    early_ref, out_ref, t_ref = refs[at + nx_r + ny_r + nz_r :]
-    width = u_ref.shape[0]
-    apply_operator(u_ref, shift_ref, x_in, y_in, z_in, t_ref)
-    payload = add_moment(u_ref, t_ref, 3 * width, early_ref[...])
-    payload = add_moment(t_ref, t_ref, 4 * width, payload)
+    width, nx = b_ref.shape[:2]
+    payload = jnp.zeros((8, LANES), F32)
+    for k, (left, right) in enumerate(((b_ref, b_ref), (b_ref, u_ref), (u_ref, u_ref))):
+        payload = put_moment(width, moment_sums(0, nx, 1, left, right, no_sums(width)), k * width, payload)
+    out_ref[...] = payload
+
+
+def inner_late_kernel(ny_r, nz_r, u_ref, shift_ref, *refs):
+    y_in, z_in, (sums_ref, t_ref) = split(refs, ny_r, nz_r)
+    width, nx = u_ref.shape[:2]
+    apply_operator(inner_planes(u_ref), u_ref, shift_ref, (), y_in, z_in, t_ref)
+    for h, left in enumerate((u_ref, t_ref)):
+        for k, value in enumerate(moment_sums(1, nx - 1, 1, left, t_ref, no_sums(width))):
+            sums_ref[h, k] = value
+
+
+def outer_late_kernel(nx_r, ny_r, nz_r, u_ref, shift_ref, sums_ref, early_ref, *refs):
+    x_in, y_in, z_in, (out_ref, t_ref) = split(refs, nx_r, ny_r, nz_r)
+    width, nx = u_ref.shape[:2]
+    apply_operator(outer_planes(u_ref), u_ref, shift_ref, x_in, y_in, z_in, t_ref)
+    payload = early_ref[...]
+    for h, left in enumerate((u_ref, t_ref)):
+        inner = [sums_ref[h, k] for k in range(len(pairs_of(width)))]
+        payload = put_moment(width, moment_sums(0, nx, nx - 1, left, t_ref, inner), (3 + h) * width, payload)
     out_ref[...] = jnp.broadcast_to(payload[None], out_ref.shape)
 
 
@@ -270,54 +320,73 @@
     lax.fori_loop(0, width // group, fields, 0)
 
 
-def call(kernel, out_shape, operands, scratch=(), flops=1_000_000, name=None):
+def call(kernel, out_shape, operands, scratch=(), flops=1_000_000, name=None, aliases=None, far=False):
     return pl.pallas_call(
         kernel,
         out_shape=out_shape,
-        in_specs=[pl.BlockSpec(memory_space=pltpu.VMEM)] * len(operands),
+        in_specs=[pl.BlockSpec(memory_space=pl.ANY if far else pltpu.VMEM)] * len(operands),
         out_specs=jax.tree.map(lambda _: pl.BlockSpec(memory_space=pltpu.VMEM), out_shape),
         scratch_shapes=list(scratch),
+        input_output_aliases=aliases or {},
         compiler_params=pltpu.CompilerParams(vmem_limit_bytes=8 << 20),
         cost_estimate=pl.CostEstimate(flops=flops, bytes_accessed=1 << 20, transcendentals=0),
         name=name,
     )(*operands)
 
 
-def trade(x_faces, y_faces, ends):
-    pairs_x, pairs_y, pairs_z = (swap_pairs(lax.axis_size(axis)) for axis in AXES)
-    got_x = [swap(face, "gx", pairs) for face, pairs in zip(x_faces, pairs_x)]
-    got_z = [swap(ends, "gz", pairs) for pairs in pairs_z]
-    got_y = [swap(face, "gy", pairs) for face, pairs in zip(y_faces, pairs_y)]
-    return [*got_x, *got_y, *got_z]
+def trade(turn, axis, faces):
+    out = []
+    for k, (face, pairs) in enumerate(zip(faces, swap_pairs(lax.axis_size(axis)))):
+        with jax.named_scope(f"turn{turn}_{axis}_{k}"):
+            out.append(swap(face, axis, pairs))
+    return out
 
 
 def body(right_side, shift):
     width, nx, ny, nz = right_side.shape
-    assert width == 8 and nz == LANES and ny % 8 == 0 and width * nx <= LANES // 2
+    assert width == 8 and nz == LANES and ny % 8 == 0 and nx > 2 and width * nx <= LANES // 2
     nx_r, ny_r, nz_r = rounds_of()
     devices = 1
     for axis in AXES:
         devices *= lax.axis_size(axis)
     block = jax.ShapeDtypeStruct(right_side.shape, F32)
-    faces = [jax.ShapeDtypeStruct((width, ny, nz), F32)] * nx_r
-    faces += [jax.ShapeDtypeStruct((width, nx, 1, nz), F32)] * ny_r
-    faces += [jax.ShapeDtypeStruct((ny, LANES), F32)]
-
-    packed = call(functools.partial(pack_kernel, nx_r, ny_r), faces, [right_side], name="pack")
-    halo = trade(packed[:nx_r], packed[nx_r : nx_r + ny_r], packed[-1])
-    u, *packed = call(
-        functools.partial(operator_kernel, nx_r, ny_r, nz_r), [block, *faces], [right_side, shift, *halo], name="operator"
-    )
-    halo = trade(packed[:nx_r], packed[nx_r : nx_r + ny_r], packed[-1])
-    early = call(
-        early_moments_kernel, jax.ShapeDtypeStruct((8, LANES), F32), [right_side, u], flops=30_000_000, name="early"
+    x_faces = [jax.ShapeDtypeStruct((width, ny, nz), F32)] * nx_r
+    y_faces = [jax.ShapeDtypeStruct((width, nx, 1, nz), F32)] * ny_r
+    ends_of = jax.ShapeDtypeStruct((ny, LANES), F32)
+    full = pltpu.VMEM(right_side.shape, F32)
+    kernel = functools.partial
+
+    faces = call(cut_x_kernel, x_faces, [right_side], scratch=[pltpu.SemaphoreType.DMA((max(nx_r, 1),))], name="cut", far=True)
+    halo_x = trade(1, "gx", faces)
+    *faces, ends = call(pack_kernel, [*y_faces, ends_of], [right_side], name="pack")
+    halo = [*trade(1, "gy", faces), *trade(1, "gz", [ends] * nz_r)]
+    inner, ends = call(
+        kernel(inner_operator_kernel, ny_r, nz_r), [block, ends_of], [right_side, shift, *halo], flops=20_000_000, name="inner1"
+    )
+    u, *faces = call(
+        kernel(outer_operator_kernel, nx_r, ny_r, nz_r),
+        [block, *x_faces, *y_faces, ends_of],
+        [right_side, shift, inner, ends, *halo_x, *halo],
+        aliases={2: 0},
+        name="outer1",
+    )
+    halo_x = trade(2, "gx", faces[:nx_r])
+    halo = [*trade(2, "gy", faces[nx_r:-1]), *trade(2, "gz", faces[-1:] * nz_r)]
+    early = call(early_moments_kernel, jax.ShapeDtypeStruct((8, LANES), F32), [right_side, u], flops=15_000_000, name="early")
+    sums = call(
+        kernel(inner_late_kernel, ny_r, nz_r),
+        jax.ShapeDtypeStruct((2, len(pairs_of(width)), 8, LANES), F32),
+        [u, shift, *halo],
+        scratch=[full],
+        flops=15_000_000,
+        name="inner2",
     )
     copies = call(
-        functools.partial(late_moments_kernel, nx_r, ny_r, nz_r),
+        kernel(outer_late_kernel, nx_r, ny_r, nz_r),
         jax.ShapeDtypeStruct((devices, 8, LANES), F32),
-        [u, shift, *halo, early],
-        scratch=[pltpu.VMEM(right_side.shape, F32)],
-        name="late",
+        [u, shift, sums, early, *halo_x, *halo],
+        scratch=[full],
+        name="outer2",
     )
     parts = lax.all_to_all(copies, AXES, 0, 0, tiled=True)
     out, norms = call(

time: 43.9 us -> 42.9 us (0.977)
  Pallas kernels: 12.8 us -> 14.4 us
  starting transfers between devices: 14 us -> 12.4 us
  blocking collectives: 13.1 us -> 12.1 us
    ppermute x8, starting transfers between devices: 13 us -> 11.3 us  [swap(): lax.ppermute(values, ('gx', 'gy') if axis == 'gx' else ('gy', 'gz'), joint)]
    pallas_call x5 -> x8, Pallas kernels: 12.8 us -> 14.4 us  [call(): pl.pallas_call(kernel, out_shape=out_shape, in_specs=[pl.BlockSpec(memory...]
    all_to_all x1, blocking collectives: 13.1 us -> 12.1 us  [body(): parts = lax.all_to_all(copies, AXES, 0, 0, tiled=True)]
  transfers between devices with their start and end apart: 10 -> 10, of which waited for: 2 -> 2; matrix products, arithmetic and copies ran while one was open for 0% -> 0% of each run, Pallas kernels for 3% -> 14%
where the time goes in v4:
time: 42.9 us; the launch traced here: 42.7 us
  Pallas kernels  14.4 us (34%)
  starting transfers between devices  12.4 us (29%)
  blocking collectives  12.1 us (28%)
  waiting for transfers between devices  1.95 us (5%)
  local copies, waits for them, and re-layouts  1.23 us (3%)
  between operations  0.71 us (2%)
    pallas_call x8, Pallas kernels, call(): pl.pallas_call(kernel, out_shape=out_shape, in_specs=[pl.BlockSpec(memory...  14.4 us
    all_to_all x1, blocking collectives, body(): parts = lax.all_to_all(copies, AXES, 0, 0, tiled=True)  12.1 us
    ppermute x8, starting transfers between devices, swap(): lax.ppermute(values, ('gx', 'gy') if axis == 'gx' else ('gy', 'gz'), joint)  11.3 us
    ppermute x8, waiting for transfers between devices, swap(): lax.ppermute(values, ('gx', 'gy') if axis == 'gx' else ('gy', 'gz'), joint)  1.94 us
    unnamed x6, local copies, waits for them, and re-layouts  1.23 us
    ppermute x2, starting transfers between devices, swap(): return lax.ppermute(values, axis, pairs)  1.08 us
  transfers between devices with their start and end apart: 10, of which 2 were waited for; matrix products, arithmetic and copies ran while one was open for 0% of the time, Pallas kernels for 14%

profile of v4, /device:TPU:0, one launch (start us, length us, event | category | flops | bytes accessed | tf_op | source)
XLA Modules:
  0.0 42.7 jit_solution(7065052273144058411)
XLA Ops:
  0.6 0.0 copy-start
  0.6 1.2 %copy-done = f32[8,8,32,128]{3,2,1,0:T(8,128)S(1)} copy-done((f32[8,8,32,128]{3,2,1,0:T(8,128)S(1)}, f32[8,8,32,128]{3,2,1,0:T(8,128)}, u32[]{:S(2)}) %copy-start) | copy-done | bytes 1048600
  1.9 0.1 cut.1
  1.9 3.0 %collective-permute-start.3 = (f32[8,32,128]{2,1,0:T(8,128)S(1)}, f32[8,32,128]{2,1,0:T(8,128)S(1)}, u32[]{:S(2)}, u32[]{:S(2)}) collective-permute-start(f32[8,32,128]{2,1,0:T(8,128)S(1)} %get-tuple-element.19), channel_id=1, source_target_pairs={{0,8},{4,12},{8,0},{12,4},{16,24},{20,28},{24,16},{28,20},{1,9},{5... | collective-permute-start | bytes 393224 | tf_op jit(solution)/shard_map/turn1_gx_0/ppermute | solution.py:31
  5.0 0.0 copy-start.2
  5.0 0.0 collective-permute-start.4
  5.0 0.8 %pack.1 = (f32[8,8,1,128]{3,2,1,0:T(1,128)S(1)}, f32[32,128]{1,0:T(8,128)S(1)}) custom-call(f32[8,8,32,128]{3,2,1,0:T(8,128)S(1)} %copy-done), custom_call_target="tpu_custom_call" | custom-call | flops 1000000 | bytes 1048576 | tf_op jit(solution)/shard_map/pack/pallas_call | solution.py:324
  5.8 0.6 %collective-permute-start = (f32[8,8,1,128]{3,2,1,0:T(1,128)S(1)}, f32[8,8,1,128]{3,2,1,0:T(1,128)S(1)}, u32[]{:S(2)}, u32[]{:S(2)}) collective-permute-start(f32[8,8,1,128]{3,2,1,0:T(1,128)S(1)} %get-tuple-element.15), channel_id=1, source_target_pairs={{0,4},{4,0},{1,5},{5,1},{2,6},{6,2},{3,7},{7,3},{8,12},{12,8},{9,1... | collective-permute-start | bytes 98312 | tf_op jit(solution)/shard_map/turn1_gy_0/ppermute | solution.py:25
  6.4 0.1 collective-permute-start.2
  6.5 3.1 %collective-permute-start.1 = (f32[32,128]{1,0:T(8,128)S(1)}, f32[32,128]{1,0:T(8,128)S(1)}, u32[]{:S(2)}, u32[]{:S(2)}) collective-permute-start(f32[32,128]{1,0:T(8,128)S(1)} %get-tuple-element.16), channel_id=1, source_target_pairs={{0,1},{4,5},{1,0},{5,4},{2,3},{6,7},{3,2},{7,6},{8,9},{12,13},{9,8... | collective-permute-start | bytes 49160 | tf_op jit(solution)/shard_map/turn1_gz_0/ppermute | solution.py:31
  9.5 0.0 collective-permute-done.2.refs_2_.refs_4_
  9.5 1.7 %collective-permute-done.1.refs_1_.refs_3_ = f32[32,128]{1,0:T(8,128)S(1)} collective-permute-done((f32[32,128]{1,0:T(8,128)S(1)}, f32[32,128]{1,0:T(8,128)S(1)}, u32[]{:S(2)}, u32[]{:S(2)}) %collective-permute-start.1) | collective-permute-done | bytes 16416 | tf_op jit(solution)/shard_map/turn1_gz_0/ppermute | solution.py:31
  11.3 0.0 collective-permute-done.refs_0_.refs_2_
  11.3 0.0 copy-done.2
  11.3 1.9 %inner1.1 = (f32[8,8,32,128]{3,2,1,0:T(8,128)S(1)}, f32[32,128]{1,0:T(8,128)S(1)}) custom-call(f32[8,8,32,128]{3,2,1,0:T(8,128)S(1)} %copy-done, f32[8,32,128]{2,1,0:T(8,128)S(1)} %copy-done.2, f32[8,8,1,128]{3,2,1,0:T(1,128)S(1)} %collective-permute-done.refs_0_.refs_2_, f32[32,128]{1,0:T(8,128)S(1)} %collective-permute-done.1.refs_1_.refs_3_, ...), custom_call_target="tpu_custom_call" | custom-call | flops 20000000 | bytes 1048576 | tf_op jit(solution)/shard_map/inner1/pallas_call | solution.py:324
  13.1 0.0 collective-permute-done.3.refs_0_
  13.1 0.0 collective-permute-done.4.refs_1_
  13.1 1.5 %outer1.1 = (f32[8,8,32,128]{3,2,1,0:T(8,128)S(1)}, f32[8,32,128]{2,1,0:T(8,128)S(1)}, f32[8,32,128]{2,1,0:T(8,128)S(1)}, f32[8,8,1,128]{3,2,1,0:T(1,128)S(1)}, f32[32,128]{1,0:T(8,128)S(1)}) custom-call(f32[8,8,32,128]{3,2,1,0:T(8,128)S(1)} %copy-done, f32[8,32,128]{2,1,0:T(8,128)S(1)} %copy-done.2, ...), custom_call_target="tpu_custom_call", output_to_operand_aliasing={{0}: (2, {})} | custom-call | flops 1000000 | bytes 1048576 | tf_op jit(solution)/shard_map/outer1/pallas_call | solution.py:324
  14.6 2.6 %collective-permute-start.8 = (f32[8,32,128]{2,1,0:T(8,128)S(1)}, f32[8,32,128]{2,1,0:T(8,128)S(1)}, u32[]{:S(2)}, u32[]{:S(2)}) collective-permute-start(f32[8,32,128]{2,1,0:T(8,128)S(1)} %get-tuple-element.24), channel_id=1, source_target_pairs={{0,8},{4,12},{8,0},{12,4},{16,24},{20,28},{24,16},{28,20},{1,9},{5... | collective-permute-start | bytes 393224 | tf_op jit(solution)/shard_map/turn2_gx_0/ppermute | solution.py:31
  17.2 0.0 collective-permute-start.9
  17.2 0.5 %collective-permute-start.5 = (f32[8,8,1,128]{3,2,1,0:T(1,128)S(1)}, f32[8,8,1,128]{3,2,1,0:T(1,128)S(1)}, u32[]{:S(2)}, u32[]{:S(2)}) collective-permute-start(f32[8,8,1,128]{3,2,1,0:T(1,128)S(1)} %get-tuple-element.22), channel_id=1, source_target_pairs={{0,4},{4,0},{1,5},{5,1},{2,6},{6,2},{3,7},{7,3},{8,12},{12,8},{9,1... | collective-permute-start | bytes 98312 | tf_op jit(solution)/shard_map/turn2_gy_0/ppermute | solution.py:25
  17.7 0.0 collective-permute-start.7
  17.7 2.5 %collective-permute-start.6 = (f32[32,128]{1,0:T(8,128)S(1)}, f32[32,128]{1,0:T(8,128)S(1)}, u32[]{:S(2)}, u32[]{:S(2)}) collective-permute-start(f32[32,128]{1,0:T(8,128)S(1)} %get-tuple-element.23), channel_id=1, source_target_pairs={{0,1},{4,5},{1,0},{5,4},{2,3},{6,7},{3,2},{7,6},{8,9},{12,13},{9,8... | collective-permute-start | bytes 49160 | tf_op jit(solution)/shard_map/turn2_gz_0/ppermute | solution.py:31
  20.2 1.5 %early.1.early_ref = f32[8,128]{1,0:T(8,128)S(1)} custom-call(f32[8,8,32,128]{3,2,1,0:T(8,128)S(1)} %copy-done, f32[8,8,32,128]{3,2,1,0:T(8,128)S(1)} %get-tuple-element.21.u_ref), custom_call_target="tpu_custom_call" | custom-call | flops 15000000 | bytes 1048576 | tf_op jit(solution)/shard_map/early/pallas_call | solution.py:324
  21.7 0.0 collective-permute-done.7.refs_2_.refs_4_
  21.7 0.2 collective-permute-done.6.refs_1_.refs_3_
  21.9 0.0 collective-permute-done.5.refs_0_.refs_2_
  21.9 1.8 %inner2.1.sums_ref = f32[2,36,8,128]{3,2,1,0:T(8,128)S(1)} custom-call(f32[8,8,32,128]{3,2,1,0:T(8,128)S(1)} %get-tuple-element.21.u_ref, f32[8,32,128]{2,1,0:T(8,128)S(1)} %copy-done.2, f32[8,8,1,128]{3,2,1,0:T(1,128)S(1)} %collective-permute-done.5.refs_0_.refs_2_, f32[32,128]{1,0:T(8,128)S(1)} %collective-permute-done.6.refs_1_.refs_3_, ...), custom_call_target="tpu_custom_call" | custom-call | flops 15000000 | bytes 1048576 | tf_op jit(solution)/shard_map/inner2/pallas_call | solution.py:324
  23.8 0.0 copy-start.1
  23.8 0.0 collective-permute-done.8.refs_0_
  23.8 0.0 collective-permute-done.9.refs_1_
  23.8 1.3 %outer2.1 = f32[32,8,128]{2,1,0:T(8,128)S(1)} custom-call(f32[8,8,32,128]{3,2,1,0:T(8,128)S(1)} %get-tuple-element.21.u_ref, f32[8,32,128]{2,1,0:T(8,128)S(1)} %copy-done.2, f32[2,36,8,128]{3,2,1,0:T(8,128)S(1)} %inner2.1.sums_ref, f32[8,128]{1,0:T(8,128)S(1)} %early.1.early_ref, f32[8,32,128]{2,1,0:T(8,128)S(1)} %collective-permute-done.8.refs_0_, ...), custom_call_target="tpu_custom_call" | custom-call | flops 1000000 | bytes 1048576 | tf_op jit(solution)/shard_map/outer2/pallas_call | solution.py:324
  25.1 12.1 %all_to_all.5.parts_ref = f32[32,8,128]{2,1,0:T(8,128)S(1)} all-to-all(f32[32,8,128]{2,1,0:T(8,128)S(1)} %outer2.1), channel_id=1, replica_groups=mesh['gx'=4,'gy'=2,'gz'=4] {'gx','gy','gz'}, dimensions={0} | all-to-all | bytes 262144 | tf_op jit(solution)/shard_map/all_to_all | solution.py:391
  37.2 0.0 copy-done.1
  37.2 5.5 %finish.1 = (f32[8,8,32,128]{3,2,1,0:T(8,128)}, f32[1,8]{1,0:T(1,128)}) custom-call(f32[32,8,128]{2,1,0:T(8,128)S(1)} %all_to_all.5.parts_ref, f32[8,8,32,128]{3,2,1,0:T(8,128)S(1)} %copy-done.1, f32[8,8,32,128]{3,2,1,0:T(8,128)S(1)} %get-tuple-element.21.u_ref), custom_call_target="tpu_custom_call" | custom-call | flops 1000000 | bytes 1048576 | tf_op jit(solution)/shard_map/finish/pallas_call | solution.py:324
Async XLA Ops:
  0.6 1.2 %copy-start = (f32[8,8,32,128]{3,2,1,0:T(8,128)S(1)}, f32[8,8,32,128]{3,2,1,0:T(8,128)}, u32[]{:S(2)}) copy-start(f32[8,8,32,128]{3,2,1,0:T(8,128)} %b_ref.3) | copy-start | bytes 3145732
  1.9 11.2 %collective-permute-start.3 = (f32[8,32,128]{2,1,0:T(8,128)S(1)}, f32[8,32,128]{2,1,0:T(8,128)S(1)}, u32[]{:S(2)}, u32[]{:S(2)}) collective-permute-start(f32[8,32,128]{2,1,0:T(8,128)S(1)} %get-tuple-element.19), channel_id=1, source_target_pairs={{0,8},{4,12},{8,0},{12,4},{16,24},{20,28},{24,16},{28,20},{1,9},{5... | collective-permute-start | bytes 393224 | tf_op jit(solution)/shard_map/turn1_gx_0/ppermute | solution.py:31
  5.0 6.3 %copy-start.2 = (f32[8,32,128]{2,1,0:T(8,128)S(1)}, f32[8,32,128]{2,1,0:T(8,128)}, u32[]{:S(2)}) copy-start(f32[8,32,128]{2,1,0:T(8,128)} %shift_ref.7) | copy-start | bytes 393220
  5.0 8.2 %collective-permute-start.4 = (f32[8,32,128]{2,1,0:T(8,128)S(1)}, f32[8,32,128]{2,1,0:T(8,128)S(1)}, u32[]{:S(2)}, u32[]{:S(2)}) collective-permute-start(f32[8,32,128]{2,1,0:T(8,128)S(1)} %get-tuple-element.20), channel_id=1, source_target_pairs={{8,16},{12,20},{16,8},{20,12},{0,4},{4,0},{24,28},{28,24},{9,17},{... | collective-permute-start | bytes 393224 | tf_op jit(solution)/shard_map/turn1_gx_1/ppermute | solution.py:31
  5.8 5.4 %collective-permute-start = (f32[8,8,1,128]{3,2,1,0:T(1,128)S(1)}, f32[8,8,1,128]{3,2,1,0:T(1,128)S(1)}, u32[]{:S(2)}, u32[]{:S(2)}) collective-permute-start(f32[8,8,1,128]{3,2,1,0:T(1,128)S(1)} %get-tuple-element.15), channel_id=1, source_target_pairs={{0,4},{4,0},{1,5},{5,1},{2,6},{6,2},{3,7},{7,3},{8,12},{12,8},{9,1... | collective-permute-start | bytes 98312 | tf_op jit(solution)/shard_map/turn1_gy_0/ppermute | solution.py:25
  6.4 3.2 %collective-permute-start.2 = (f32[32,128]{1,0:T(8,128)S(1)}, f32[32,128]{1,0:T(8,128)S(1)}, u32[]{:S(2)}, u32[]{:S(2)}) collective-permute-start(f32[32,128]{1,0:T(8,128)S(1)} %get-tuple-element.16), channel_id=1, source_target_pairs={{1,2},{5,6},{2,1},{6,5},{0,4},{4,0},{3,7},{7,3},{9,10},{13,14},{10... | collective-permute-start | bytes 49160 | tf_op jit(solution)/shard_map/turn1_gz_1/ppermute | solution.py:31
  6.5 4.8 %collective-permute-start.1 = (f32[32,128]{1,0:T(8,128)S(1)}, f32[32,128]{1,0:T(8,128)S(1)}, u32[]{:S(2)}, u32[]{:S(2)}) collective-permute-start(f32[32,128]{1,0:T(8,128)S(1)} %get-tuple-element.16), channel_id=1, source_target_pairs={{0,1},{4,5},{1,0},{5,4},{2,3},{6,7},{3,2},{7,6},{8,9},{12,13},{9,8... | collective-permute-start | bytes 49160 | tf_op jit(solution)/shard_map/turn1_gz_0/ppermute | solution.py:31
  14.6 9.2 %collective-permute-start.8 = (f32[8,32,128]{2,1,0:T(8,128)S(1)}, f32[8,32,128]{2,1,0:T(8,128)S(1)}, u32[]{:S(2)}, u32[]{:S(2)}) collective-permute-start(f32[8,32,128]{2,1,0:T(8,128)S(1)} %get-tuple-element.24), channel_id=1, source_target_pairs={{0,8},{4,12},{8,0},{12,4},{16,24},{20,28},{24,16},{28,20},{1,9},{5... | collective-permute-start | bytes 393224 | tf_op jit(solution)/shard_map/turn2_gx_0/ppermute | solution.py:31
  17.2 6.6 %collective-permute-start.9 = (f32[8,32,128]{2,1,0:T(8,128)S(1)}, f32[8,32,128]{2,1,0:T(8,128)S(1)}, u32[]{:S(2)}, u32[]{:S(2)}) collective-permute-start(f32[8,32,128]{2,1,0:T(8,128)S(1)} %get-tuple-element.25), channel_id=1, source_target_pairs={{8,16},{12,20},{16,8},{20,12},{0,4},{4,0},{24,28},{28,24},{9,17},{... | collective-permute-start | bytes 393224 | tf_op jit(solution)/shard_map/turn2_gx_1/ppermute | solution.py:31
  17.2 4.7 %collective-permute-start.5 = (f32[8,8,1,128]{3,2,1,0:T(1,128)S(1)}, f32[8,8,1,128]{3,2,1,0:T(1,128)S(1)}, u32[]{:S(2)}, u32[]{:S(2)}) collective-permute-start(f32[8,8,1,128]{3,2,1,0:T(1,128)S(1)} %get-tuple-element.22), channel_id=1, source_target_pairs={{0,4},{4,0},{1,5},{5,1},{2,6},{6,2},{3,7},{7,3},{8,12},{12,8},{9,1... | collective-permute-start | bytes 98312 | tf_op jit(solution)/shard_map/turn2_gy_0/ppermute | solution.py:25
  17.7 4.0 %collective-permute-start.7 = (f32[32,128]{1,0:T(8,128)S(1)}, f32[32,128]{1,0:T(8,128)S(1)}, u32[]{:S(2)}, u32[]{:S(2)}) collective-permute-start(f32[32,128]{1,0:T(8,128)S(1)} %get-tuple-element.23), channel_id=1, source_target_pairs={{1,2},{5,6},{2,1},{6,5},{0,4},{4,0},{3,7},{7,3},{9,10},{13,14},{10... | collective-permute-start | bytes 49160 | tf_op jit(solution)/shard_map/turn2_gz_1/ppermute | solution.py:31
  17.7 4.2 %collective-permute-start.6 = (f32[32,128]{1,0:T(8,128)S(1)}, f32[32,128]{1,0:T(8,128)S(1)}, u32[]{:S(2)}, u32[]{:S(2)}) collective-permute-start(f32[32,128]{1,0:T(8,128)S(1)} %get-tuple-element.23), channel_id=1, source_target_pairs={{0,1},{4,5},{1,0},{5,4},{2,3},{6,7},{3,2},{7,6},{8,9},{12,13},{9,8... | collective-permute-start | bytes 49160 | tf_op jit(solution)/shard_map/turn2_gz_0/ppermute | solution.py:31
  23.8 13.4 %copy-start.1 = (f32[8,8,32,128]{3,2,1,0:T(8,128)S(1)}, f32[8,8,32,128]{3,2,1,0:T(8,128)}, u32[]{:S(2)}) copy-start(f32[8,8,32,128]{3,2,1,0:T(8,128)} %b_ref.3) | copy-start | bytes 3145732

commit v5 on v4

--- a/solution.py
+++ b/solution.py
@@ -62,23 +62,39 @@
         ref[...] = jnp.where(high, v_ref[:, :, ny - 1 : ny, :], v_ref[:, :, 0:1, :])
 
 
-def packed_ends(tile, m, packed, lane):
-    at = 2 * m
-    hit = (lane == at) | (lane == lax.rem(at + LANES - 1, LANES))
-    return jnp.where(hit, pltpu.roll(tile, at, 1), packed)
-
-
-def pack_kernel(v_ref, *refs):
+def packed_ends(tile, m, lane, near, far=None):
+    def at(offset):
+        return lane == lax.rem(2 * m + offset + LANES, LANES)
+
+    turned = pltpu.roll(tile, 2 * m, 1)
+    near = jnp.where(at(0) | at(-1), turned, near)
+    if far is None:
+        return near
+    return near, jnp.where(at(1) | at(-2), turned, far)
+
+
+def pack_kernel(v_ref, shift_ref, *refs):
     width, nx, ny, _ = v_ref.shape
     write_y_faces(v_ref, refs[:-1])
     lane = lax.broadcasted_iota(jnp.int32, (ny, LANES), 1)
+    nothing = jnp.zeros((ny, LANES), F32)
 
     def field(f, packed):
         for x in range(nx):
-            packed = packed_ends(v_ref[f, x], f * nx + x, packed, lane)
+            packed = packed_ends(v_ref[f, x], f * nx + x, lane, *packed)
         return packed
 
-    refs[-1][...] = lax.fori_loop(0, width, field, jnp.zeros((ny, LANES), F32))
+    near, far = lax.fori_loop(0, width, field, (nothing, nothing))
+    diagonal = nothing
+    for x in range(nx):
+        diagonal = packed_ends((6.0 - CENTRE) + shift_ref[x], x, lane, diagonal)
+    copies = 1
+    while copies < width:
+        diagonal = diagonal + pltpu.roll(diagonal, 2 * nx * copies, 1)
+        copies *= 2
+    refs[-1][0] = near
+    refs[-1][1] = far
+    refs[-1][2] = diagonal
 
 
 def pick(axis, refs, load):
@@ -92,37 +108,70 @@
     return low, high
 
 
-def apply_operator(planes, v_ref, shift_ref, x_in, y_in, z_in, out_ref, packed=None):
+def halo_ends(z_in, layer):
+    low, high = pick("gz", z_in, lambda ref: ref[layer])
+    if not z_in:
+        return None
+    lane = lax.broadcasted_iota(jnp.int32, low.shape, 1)
+    by = 2 if layer == 1 else 1
+    return jnp.where(lax.rem(lane, 2) == 0, pltpu.roll(low, by, 1), pltpu.roll(high, LANES - by, 1))
+
+
+def inside_grid(lane):
+    low = jnp.where(lax.axis_index("gz") == 0, 0.0, 1.0)
+    high = jnp.where(lax.axis_index("gz") == lax.axis_size("gz") - 1, 0.0, 1.0)
+    return jnp.where(lax.rem(lane, 2) == 0, low, high)
+
+
+def lane_x(lane, nx):
+    return lax.rem((lane + 1) // 2, nx)
+
+
+def operator_on_ends(nx, own, z_in):
+    near, far, diagonal = (halo_ends(z_in, layer) for layer in range(3))
+    ny = near.shape[0]
+    lane = lax.broadcasted_iota(jnp.int32, near.shape, 1)
+    row = lax.broadcasted_iota(jnp.int32, near.shape, 0)
+    x = lane_x(lane, nx)
+    beside = own + far
+    beside += jnp.where(x == 0, 0.0, pltpu.roll(near, 2, 1)) + jnp.where(x == nx - 1, 0.0, pltpu.roll(near, LANES - 2, 1))
+    beside += jnp.where(row == 0, 0.0, pltpu.roll(near, 1, 0)) + jnp.where(row == ny - 1, 0.0, pltpu.roll(near, ny - 1, 0))
+    return near, inside_grid(lane) * (diagonal * near - beside)
+
+
+def finished_ends(nx, base, x_in, y_in, width):
+    ny = base.shape[0]
+    lane = lax.broadcasted_iota(jnp.int32, base.shape, 1)
+    row = lax.broadcasted_iota(jnp.int32, base.shape, 0)
+    low_y, high_y = pick("gy", y_in, lambda ref: ref[width, 0])
+    beside = jnp.where(row == 0, low_y, 0.0) + jnp.where(row == ny - 1, high_y, 0.0)
+    if x_in:
+        x, by = lane_x(lane, nx), 2 * (nx - 1)
+        low_x, high_x = pick("gx", x_in, lambda ref: ref[width])
+        beside += jnp.where(x == 0, pltpu.roll(low_x, LANES - by, 1), 0.0)
+        beside += jnp.where(x == nx - 1, pltpu.roll(high_x, by, 1), 0.0)
+    return base - inside_grid(lane) * beside
+
+
+def apply_operator(planes, v_ref, shift_ref, x_in, y_in, ends, out_ref):
     width, nx, ny, _ = v_ref.shape
     lane = lax.broadcasted_iota(jnp.int32, (ny, LANES), 1)
     row = lax.broadcasted_iota(jnp.int32, (ny, LANES), 0)
-    low_z, high_z = pick("gz", z_in, lambda ref: ref[...])
-    ends = jnp.where(
-        lax.rem(lane, 2) == 0, pltpu.roll(low_z, 1, 1), pltpu.roll(high_z, LANES - 1, 1)
-    )
-
-    def field(f, packed):
+    def field(f, carry):
         low_x, high_x = pick("gx", x_in, lambda ref: ref[f])
         for x in planes:
-            m = f * nx + x
             low_y, high_y = pick("gy", y_in, lambda ref: ref[f, x])
             v = v_ref[f, x]
-            end = pltpu.roll(ends, lax.rem(LANES - 2 * m, LANES), 1)
+            end = pltpu.roll(ends, lax.rem(LANES - 2 * (f * nx + x), LANES), 1)
             beside = (v_ref[f, x - 1] if x > 0 else low_x) + (v_ref[f, x + 1] if x < nx - 1 else high_x)
             beside += jnp.where(row == 0, low_y, pltpu.roll(v, 1, 0))
             beside += jnp.where(row == ny - 1, high_y, pltpu.roll(v, ny - 1, 0))
             beside += jnp.where(lane == 0, end, pltpu.roll(v, 1, 1))
             beside += jnp.where(lane == LANES - 1, end, pltpu.roll(v, LANES - 1, 1))
-            out = ((6.0 - CENTRE) + shift_ref[x]) * v - beside
-            out_ref[f, x] = out
-            if packed is not None:
-                packed = packed_ends(out, m, packed, lane)
-        return packed
-
-    if packed is None:
-        lax.fori_loop(0, width, lambda f, c: (field(f, None), c)[1], 0)
-        return None
-    return lax.fori_loop(0, width, field, packed)
+            out_ref[f, x] = ((6.0 - CENTRE) + shift_ref[x]) * v - beside
+        return carry
+
+    lax.fori_loop(0, width, field, 0)
 
 
 def split(refs, *counts):
@@ -141,19 +190,28 @@
     return (0, ref.shape[1] - 1)
 
 
-def inner_operator_kernel(ny_r, nz_r, v_ref, shift_ref, *refs):
+def inner_operator_kernel(ny_r, nz_r, v_ref, shift_ref, own_ref, *refs):
     y_in, z_in, (out_ref, ends_ref) = split(refs, ny_r, nz_r)
-    start = jnp.zeros(ends_ref.shape, F32)
-    ends_ref[...] = apply_operator(inner_planes(v_ref), v_ref, shift_ref, (), y_in, z_in, out_ref, start)
-
-
-def outer_operator_kernel(nx_r, ny_r, nz_r, v_ref, shift_ref, inner_ref, ends_ref, *refs):
-    x_in, y_in, z_in, (out_ref,), x_out, y_out, (z_out,) = split(refs, nx_r, ny_r, nz_r, 1, nx_r, ny_r)
-    planes = outer_planes(v_ref)
-    z_out[...] = apply_operator(planes, v_ref, shift_ref, x_in, y_in, z_in, out_ref, ends_ref[...])
+    near, base = operator_on_ends(v_ref.shape[1], own_ref[0], z_in)
+    ends_ref[0] = near
+    ends_ref[1] = base
+    apply_operator(inner_planes(v_ref), v_ref, shift_ref, (), y_in, near, out_ref)
+
+
+def outer_operator_kernel(nx_r, ny_r, v_ref, shift_ref, inner_ref, ends_ref, *refs):
+    x_in, y_in, (out_ref,), x_out, y_out = split(refs, nx_r, ny_r, 1, nx_r)
+    width, nx, ny, _ = v_ref.shape
+    near = ends_ref[0]
+    apply_operator(outer_planes(v_ref), v_ref, shift_ref, x_in, y_in, near, out_ref)
     for k, ref in enumerate(x_out):
-        ref[...] = out_ref[:, x_plane(k, v_ref.shape[1])]
-    write_y_faces(out_ref, y_out)
+        ref[:width] = out_ref[:, x_plane(k, nx)]
+        ref[width] = near
+    write_y_faces(out_ref, [ref.at[:width] for ref in y_out])
+    for k, ref in enumerate(y_out):
+        high = jnp.logical_xor(parity("gy"), k == 0)
+        line = jnp.where(high, near[ny - 1 : ny], near[0:1])
+        for x in range(nx):
+            ref[width, x] = line
 
 
 def pairs_of(width):
@@ -199,19 +257,21 @@
     out_ref[...] = payload
 
 
-def inner_late_kernel(ny_r, nz_r, u_ref, shift_ref, *refs):
-    y_in, z_in, (sums_ref, t_ref) = split(refs, ny_r, nz_r)
+def inner_late_kernel(ny_r, u_ref, shift_ref, ends_ref, *refs):
+    y_in, (sums_ref, t_ref) = split(refs, ny_r)
     width, nx = u_ref.shape[:2]
-    apply_operator(inner_planes(u_ref), u_ref, shift_ref, (), y_in, z_in, t_ref)
+    ends = finished_ends(nx, ends_ref[1], (), y_in, width)
+    apply_operator(inner_planes(u_ref), u_ref, shift_ref, (), y_in, ends, t_ref)
     for h, left in enumerate((u_ref, t_ref)):
         for k, value in enumerate(moment_sums(1, nx - 1, 1, left, t_ref, no_sums(width))):
             sums_ref[h, k] = value
 
 
-def outer_late_kernel(nx_r, ny_r, nz_r, u_ref, shift_ref, sums_ref, early_ref, *refs):
-    x_in, y_in, z_in, (out_ref, t_ref) = split(refs, nx_r, ny_r, nz_r)
+def outer_late_kernel(nx_r, ny_r, u_ref, shift_ref, ends_ref, sums_ref, early_ref, *refs):
+    x_in, y_in, (out_ref, t_ref) = split(refs, nx_r, ny_r)
     width, nx = u_ref.shape[:2]
-    apply_operator(outer_planes(u_ref), u_ref, shift_ref, x_in, y_in, z_in, t_ref)
+    ends = finished_ends(nx, ends_ref[1], x_in, y_in, width)
+    apply_operator(outer_planes(u_ref), u_ref, shift_ref, x_in, y_in, ends, t_ref)
     payload = early_ref[...]
     for h, left in enumerate((u_ref, t_ref)):
         inner = [sums_ref[h, k] for k in range(len(pairs_of(width)))]
@@ -349,42 +409,54 @@
     devices = 1
     for axis in AXES:
         devices *= lax.axis_size(axis)
+    assert nz_r > 0
     block = jax.ShapeDtypeStruct(right_side.shape, F32)
-    x_faces = [jax.ShapeDtypeStruct((width, ny, nz), F32)] * nx_r
-    y_faces = [jax.ShapeDtypeStruct((width, nx, 1, nz), F32)] * ny_r
-    ends_of = jax.ShapeDtypeStruct((ny, LANES), F32)
     full = pltpu.VMEM(right_side.shape, F32)
     kernel = functools.partial
 
-    faces = call(cut_x_kernel, x_faces, [right_side], scratch=[pltpu.SemaphoreType.DMA((max(nx_r, 1),))], name="cut", far=True)
+    def x_faces(fields):
+        return [jax.ShapeDtypeStruct((fields, ny, nz), F32)] * nx_r
+
+    def y_faces(fields):
+        return [jax.ShapeDtypeStruct((fields, nx, 1, nz), F32)] * ny_r
+
+    def ends_of(layers):
+        return jax.ShapeDtypeStruct((layers, ny, LANES), F32)
+
+    faces = call(cut_x_kernel, x_faces(width), [right_side], scratch=[pltpu.SemaphoreType.DMA((max(nx_r, 1),))], name="cut", far=True)
     halo_x = trade(1, "gx", faces)
-    *faces, ends = call(pack_kernel, [*y_faces, ends_of], [right_side], name="pack")
-    halo = [*trade(1, "gy", faces), *trade(1, "gz", [ends] * nz_r)]
+    *faces, own = call(pack_kernel, [*y_faces(width), ends_of(3)], [right_side, shift], name="pack")
+    halo_y = trade(1, "gy", faces)
+    halo_z = trade(1, "gz", [own] * nz_r)
     inner, ends = call(
-        kernel(inner_operator_kernel, ny_r, nz_r), [block, ends_of], [right_side, shift, *halo], flops=20_000_000, name="inner1"
+        kernel(inner_operator_kernel, ny_r, nz_r),
+        [block, ends_of(2)],
+        [right_side, shift, own, *halo_y, *halo_z],
+        flops=20_000_000,
+        name="inner1",
     )
     u, *faces = call(
-        kernel(outer_operator_kernel, nx_r, ny_r, nz_r),
-        [block, *x_faces, *y_faces, ends_of],
-        [right_side, shift, inner, ends, *halo_x, *halo],
+        kernel(outer_operator_kernel, nx_r, ny_r),
+        [block, *x_faces(width + 1), *y_faces(width + 1)],
+        [right_side, shift, inner, ends, *halo_x, *halo_y],
         aliases={2: 0},
         name="outer1",
     )
     halo_x = trade(2, "gx", faces[:nx_r])
-    halo = [*trade(2, "gy", faces[nx_r:-1]), *trade(2, "gz", faces[-1:] * nz_r)]
+    halo_y = trade(2, "gy", faces[nx_r:])
     early = call(early_moments_kernel, jax.ShapeDtypeStruct((8, LANES), F32), [right_side, u], flops=15_000_000, name="early")
     sums = call(
-        kernel(inner_late_kernel, ny_r, nz_r),
+        kernel(inner_late_kernel, ny_r),
         jax.ShapeDtypeStruct((2, len(pairs_of(width)), 8, LANES), F32),
-        [u, shift, *halo],
+        [u, shift, ends, *halo_y],
         scratch=[full],
         flops=15_000_000,
         name="inner2",
     )
     copies = call(
-        kernel(outer_late_kernel, nx_r, ny_r, nz_r),
+        kernel(outer_late_kernel, nx_r, ny_r),
         jax.ShapeDtypeStruct((devices, 8, LANES), F32),
-        [u, shift, sums, early, *halo_x, *halo],
+        [u, shift, ends, sums, early, *halo_x, *halo_y],
         scratch=[full],
         name="outer2",
     )

time: 42.9 us -> 42.3 us (0.986)
  starting transfers between devices: 12.4 us -> 9.69 us
  blocking collectives: 12.1 us -> 14 us
  waiting for transfers between devices: 1.95 us -> 3.03 us
  Pallas kernels: 14.4 us -> 13.4 us
    ppermute x8 -> x6, starting transfers between devices: 11.3 us -> 9.18 us  [swap(): lax.ppermute(values, ('gx', 'gy') if axis == 'gx' else ('gy', 'gz'), joint)]
    all_to_all x1, blocking collectives: 12.1 us -> 14 us  [body(): parts = lax.all_to_all(copies, AXES, 0, 0, tiled=True)]
    ppermute x2, waiting for transfers between devices: 0.01 us -> 1.21 us  [swap(): return lax.ppermute(values, axis, pairs)]
    pallas_call x8, Pallas kernels: 14.4 us -> 13.4 us  [call(): pl.pallas_call(kernel, out_shape=out_shape, in_specs=[pl.BlockSpec(memory...]
    ppermute x2, starting transfers between devices: 1.08 us -> 0.51 us  [swap(): return lax.ppermute(values, axis, pairs)]
    ppermute x8 -> x6, waiting for transfers between devices: 1.94 us -> 1.82 us  [swap(): lax.ppermute(values, ('gx', 'gy') if axis == 'gx' else ('gy', 'gz'), joint)]
  transfers between devices with their start and end apart: 10 -> 8, of which waited for: 2 -> 3; matrix products, arithmetic and copies ran while one was open for 0% -> 0% of each run, Pallas kernels for 14% -> 14%
where the time goes in v5:
time: 42.3 us; the launch traced here: 42.1 us
  blocking collectives  14 us (33%)
  Pallas kernels  13.4 us (32%)
  starting transfers between devices  9.69 us (23%)
  waiting for transfers between devices  3.03 us (7%)
  local copies, waits for them, and re-layouts  1.23 us (3%)
  between operations  0.71 us (2%)
    all_to_all x1, blocking collectives, body(): parts = lax.all_to_all(copies, AXES, 0, 0, tiled=True)  14 us
    pallas_call x8, Pallas kernels, call(): pl.pallas_call(kernel, out_shape=out_shape, in_specs=[pl.BlockSpec(memory...  13.4 us
    ppermute x6, starting transfers between devices, swap(): lax.ppermute(values, ('gx', 'gy') if axis == 'gx' else ('gy', 'gz'), joint)  9.18 us
    ppermute x6, waiting for transfers between devices, swap(): lax.ppermute(values, ('gx', 'gy') if axis == 'gx' else ('gy', 'gz'), joint)  1.82 us
    unnamed x6, local copies, waits for them, and re-layouts  1.23 us
    ppermute x2, waiting for transfers between devices, swap(): return lax.ppermute(values, axis, pairs)  1.21 us
  transfers between devices with their start and end apart: 8, of which 3 were waited for; matrix products, arithmetic and copies ran while one was open for 0% of the time, Pallas kernels for 14%

profile of v5, /device:TPU:0, one launch (start us, length us, event | category | flops | bytes accessed | tf_op | source)
XLA Modules:
  0.0 42.1 jit_solution(13401852985607533791)
XLA Ops:
  0.6 0.0 copy-start
  0.6 1.2 %copy-done = f32[8,8,32,128]{3,2,1,0:T(8,128)S(1)} copy-done((f32[8,8,32,128]{3,2,1,0:T(8,128)S(1)}, f32[8,8,32,128]{3,2,1,0:T(8,128)}, u32[]{:S(2)}) %copy-start) | copy-done | bytes 1048600
  1.9 0.0 copy-start.2
  1.9 0.1 cut.1
  1.9 3.0 %collective-permute-start.3 = (f32[8,32,128]{2,1,0:T(8,128)S(1)}, f32[8,32,128]{2,1,0:T(8,128)S(1)}, u32[]{:S(2)}, u32[]{:S(2)}) collective-permute-start(f32[8,32,128]{2,1,0:T(8,128)S(1)} %get-tuple-element.18), channel_id=1, source_target_pairs={{0,8},{4,12},{8,0},{12,4},{16,24},{20,28},{24,16},{28,20},{1,9},{5... | collective-permute-start | bytes 393224 | tf_op jit(solution)/shard_map/turn1_gx_0/ppermute | solution.py:31
  5.0 0.0 collective-permute-start.4
  5.0 0.0 copy-done.2
  5.0 1.1 %pack.1 = (f32[8,8,1,128]{3,2,1,0:T(1,128)S(1)}, f32[3,32,128]{2,1,0:T(8,128)S(1)}) custom-call(f32[8,8,32,128]{3,2,1,0:T(8,128)S(1)} %copy-done, f32[8,32,128]{2,1,0:T(8,128)S(1)} %copy-done.2), custom_call_target="tpu_custom_call" | custom-call | flops 1000000 | bytes 1048576 | tf_op jit(solution)/shard_map/pack/pallas_call | solution.py:384
  6.1 0.5 %collective-permute-start.2 = (f32[3,32,128]{2,1,0:T(8,128)S(1)}, f32[3,32,128]{2,1,0:T(8,128)S(1)}, u32[]{:S(2)}, u32[]{:S(2)}) collective-permute-start(f32[3,32,128]{2,1,0:T(8,128)S(1)} %get-tuple-element.14.own_ref), channel_id=1, source_target_pairs={{1,2},{5,6},{2,1},{6,5},{0,4},{4,0},{3,7},{7,3},{9,10},{13,14},{10... | collective-permute-start | bytes 147464 | tf_op jit(solution)/shard_map/turn1_gz_1/ppermute | solution.py:31
  6.6 2.6 %collective-permute-start.1 = (f32[3,32,128]{2,1,0:T(8,128)S(1)}, f32[3,32,128]{2,1,0:T(8,128)S(1)}, u32[]{:S(2)}, u32[]{:S(2)}) collective-permute-start(f32[3,32,128]{2,1,0:T(8,128)S(1)} %get-tuple-element.14.own_ref), channel_id=1, source_target_pairs={{0,1},{4,5},{1,0},{5,4},{2,3},{6,7},{3,2},{7,6},{8,9},{12,13},{9,8... | collective-permute-start | bytes 147464 | tf_op jit(solution)/shard_map/turn1_gz_0/ppermute | solution.py:31
  9.3 0.0 collective-permute-start
  9.3 1.2 %collective-permute-done.refs_0_.refs_2_ = f32[8,8,1,128]{3,2,1,0:T(1,128)S(1)} collective-permute-done((f32[8,8,1,128]{3,2,1,0:T(1,128)S(1)}, f32[8,8,1,128]{3,2,1,0:T(1,128)S(1)}, u32[]{:S(2)}, u32[]{:S(2)}) %collective-permute-start) | collective-permute-done | bytes 32800 | tf_op jit(solution)/shard_map/turn1_gy_0/ppermute | solution.py:25
  10.5 0.0 collective-permute-done.2.refs_2_
  10.5 0.9 %collective-permute-done.1.refs_1_ = f32[3,32,128]{2,1,0:T(8,128)S(1)} collective-permute-done((f32[3,32,128]{2,1,0:T(8,128)S(1)}, f32[3,32,128]{2,1,0:T(8,128)S(1)}, u32[]{:S(2)}, u32[]{:S(2)}) %collective-permute-start.1) | collective-permute-done | bytes 49184 | tf_op jit(solution)/shard_map/turn1_gz_0/ppermute | solution.py:31
  11.4 1.3 %inner1.1 = (f32[8,8,32,128]{3,2,1,0:T(8,128)S(1)}, f32[2,32,128]{2,1,0:T(8,128)S(1)}) custom-call(f32[8,8,32,128]{3,2,1,0:T(8,128)S(1)} %copy-done, f32[8,32,128]{2,1,0:T(8,128)S(1)} %copy-done.2, f32[3,32,128]{2,1,0:T(8,128)S(1)} %get-tuple-element.14.own_ref, f32[8,8,1,128]{3,2,1,0:T(1,128)S(1)} %collective-permute-done.refs_0_.refs_2_, ...), custom_call_target="tpu_custom_call" | custom-call | flops 20000000 | bytes 1048576 | tf_op jit(solution)/shard_map/inner1/pallas_call | solution.py:384
  12.7 0.0 collective-permute-done.3.refs_0_
  12.7 0.0 collective-permute-done.4.refs_1_
  12.8 0.8 %outer1.1 = (f32[8,8,32,128]{3,2,1,0:T(8,128)S(1)}, f32[9,32,128]{2,1,0:T(8,128)S(1)}, f32[9,32,128]{2,1,0:T(8,128)S(1)}, f32[9,8,1,128]{3,2,1,0:T(1,128)S(1)}) custom-call(f32[8,8,32,128]{3,2,1,0:T(8,128)S(1)} %copy-done, f32[8,32,128]{2,1,0:T(8,128)S(1)} %copy-done.2, ...), custom_call_target="tpu_custom_call", output_to_operand_aliasing={{0}: (2, {})} | custom-call | flops 1000000 | bytes 1048576 | tf_op jit(solution)/shard_map/outer1/pallas_call | solution.py:384
  13.6 3.0 %collective-permute-start.6 = (f32[9,32,128]{2,1,0:T(8,128)S(1)}, f32[9,32,128]{2,1,0:T(8,128)S(1)}, u32[]{:S(2)}, u32[]{:S(2)}) collective-permute-start(f32[9,32,128]{2,1,0:T(8,128)S(1)} %get-tuple-element.22), channel_id=1, source_target_pairs={{0,8},{4,12},{8,0},{12,4},{16,24},{20,28},{24,16},{28,20},{1,9},{5... | collective-permute-start | bytes 442376 | tf_op jit(solution)/shard_map/turn2_gx_0/ppermute | solution.py:31
  16.6 0.0 collective-permute-start.7
  16.6 0.5 %collective-permute-start.5 = (f32[9,8,1,128]{3,2,1,0:T(1,128)S(1)}, f32[9,8,1,128]{3,2,1,0:T(1,128)S(1)}, u32[]{:S(2)}, u32[]{:S(2)}) collective-permute-start(f32[9,8,1,128]{3,2,1,0:T(1,128)S(1)} %get-tuple-element.21), channel_id=1, source_target_pairs={{0,4},{4,0},{1,5},{5,1},{2,6},{6,2},{3,7},{7,3},{8,12},{12,8},{9,1... | collective-permute-start | bytes 110600 | tf_op jit(solution)/shard_map/turn2_gy_0/ppermute | solution.py:25
  17.1 1.5 %early.1.early_ref = f32[8,128]{1,0:T(8,128)S(1)} custom-call(f32[8,8,32,128]{3,2,1,0:T(8,128)S(1)} %copy-done, f32[8,8,32,128]{3,2,1,0:T(8,128)S(1)} %get-tuple-element.20.u_ref), custom_call_target="tpu_custom_call" | custom-call | flops 15000000 | bytes 1048576 | tf_op jit(solution)/shard_map/early/pallas_call | solution.py:384
  18.6 0.0 collective-permute-done.5.refs_0_.refs_2_
  18.6 1.8 %inner2.1.sums_ref = f32[2,36,8,128]{3,2,1,0:T(8,128)S(1)} custom-call(f32[8,8,32,128]{3,2,1,0:T(8,128)S(1)} %get-tuple-element.20.u_ref, f32[8,32,128]{2,1,0:T(8,128)S(1)} %copy-done.2, f32[2,32,128]{2,1,0:T(8,128)S(1)} %get-tuple-element.17.ends_ref, f32[9,8,1,128]{3,2,1,0:T(1,128)S(1)} %collective-permute-done.5.refs_0_.refs_2_), custom_call_target="tpu_custom_call" | custom-call | flops 15000000 | bytes 1048576 | tf_op jit(solution)/shard_map/inner2/pallas_call | solution.py:384
  20.4 0.0 copy-start.1
  20.4 0.9 %collective-permute-done.6.refs_0_ = f32[9,32,128]{2,1,0:T(8,128)S(1)} collective-permute-done((f32[9,32,128]{2,1,0:T(8,128)S(1)}, f32[9,32,128]{2,1,0:T(8,128)S(1)}, u32[]{:S(2)}, u32[]{:S(2)}) %collective-permute-start.6) | collective-permute-done | bytes 147488 | tf_op jit(solution)/shard_map/turn2_gx_0/ppermute | solution.py:31
  21.3 0.0 collective-permute-done.7.refs_1_
  21.3 1.3 %outer2.1 = f32[32,8,128]{2,1,0:T(8,128)S(1)} custom-call(f32[8,8,32,128]{3,2,1,0:T(8,128)S(1)} %get-tuple-element.20.u_ref, f32[8,32,128]{2,1,0:T(8,128)S(1)} %copy-done.2, f32[2,32,128]{2,1,0:T(8,128)S(1)} %get-tuple-element.17.ends_ref, f32[2,36,8,128]{3,2,1,0:T(8,128)S(1)} %inner2.1.sums_ref, f32[8,128]{1,0:T(8,128)S(1)} %early.1.early_ref, ...), custom_call_target="tpu_custom_call" | custom-call | flops 1000000 | bytes 1048576 | tf_op jit(solution)/shard_map/outer2/pallas_call | solution.py:384
  22.6 14.0 %all_to_all.5.parts_ref = f32[32,8,128]{2,1,0:T(8,128)S(1)} all-to-all(f32[32,8,128]{2,1,0:T(8,128)S(1)} %outer2.1), channel_id=1, replica_groups=mesh['gx'=4,'gy'=2,'gz'=4] {'gx','gy','gz'}, dimensions={0} | all-to-all | bytes 262144 | tf_op jit(solution)/shard_map/all_to_all | solution.py:463
  36.6 0.0 copy-done.1
  36.6 5.5 %finish.1 = (f32[8,8,32,128]{3,2,1,0:T(8,128)}, f32[1,8]{1,0:T(1,128)}) custom-call(f32[32,8,128]{2,1,0:T(8,128)S(1)} %all_to_all.5.parts_ref, f32[8,8,32,128]{3,2,1,0:T(8,128)S(1)} %copy-done.1, f32[8,8,32,128]{3,2,1,0:T(8,128)S(1)} %get-tuple-element.20.u_ref), custom_call_target="tpu_custom_call" | custom-call | flops 1000000 | bytes 1048576 | tf_op jit(solution)/shard_map/finish/pallas_call | solution.py:384
Async XLA Ops:
  0.6 1.2 %copy-start = (f32[8,8,32,128]{3,2,1,0:T(8,128)S(1)}, f32[8,8,32,128]{3,2,1,0:T(8,128)}, u32[]{:S(2)}) copy-start(f32[8,8,32,128]{3,2,1,0:T(8,128)} %b_ref.3) | copy-start | bytes 3145732
  1.9 3.1 %copy-start.2 = (f32[8,32,128]{2,1,0:T(8,128)S(1)}, f32[8,32,128]{2,1,0:T(8,128)}, u32[]{:S(2)}) copy-start(f32[8,32,128]{2,1,0:T(8,128)} %shift_ref.9) | copy-start | bytes 393220
  1.9 10.8 %collective-permute-start.3 = (f32[8,32,128]{2,1,0:T(8,128)S(1)}, f32[8,32,128]{2,1,0:T(8,128)S(1)}, u32[]{:S(2)}, u32[]{:S(2)}) collective-permute-start(f32[8,32,128]{2,1,0:T(8,128)S(1)} %get-tuple-element.18), channel_id=1, source_target_pairs={{0,8},{4,12},{8,0},{12,4},{16,24},{20,28},{24,16},{28,20},{1,9},{5... | collective-permute-start | bytes 393224 | tf_op jit(solution)/shard_map/turn1_gx_0/ppermute | solution.py:31
  5.0 7.8 %collective-permute-start.4 = (f32[8,32,128]{2,1,0:T(8,128)S(1)}, f32[8,32,128]{2,1,0:T(8,128)S(1)}, u32[]{:S(2)}, u32[]{:S(2)}) collective-permute-start(f32[8,32,128]{2,1,0:T(8,128)S(1)} %get-tuple-element.19), channel_id=1, source_target_pairs={{8,16},{12,20},{16,8},{20,12},{0,4},{4,0},{24,28},{28,24},{9,17},{... | collective-permute-start | bytes 393224 | tf_op jit(solution)/shard_map/turn1_gx_1/ppermute | solution.py:31
  6.1 4.4 %collective-permute-start.2 = (f32[3,32,128]{2,1,0:T(8,128)S(1)}, f32[3,32,128]{2,1,0:T(8,128)S(1)}, u32[]{:S(2)}, u32[]{:S(2)}) collective-permute-start(f32[3,32,128]{2,1,0:T(8,128)S(1)} %get-tuple-element.14.own_ref), channel_id=1, source_target_pairs={{1,2},{5,6},{2,1},{6,5},{0,4},{4,0},{3,7},{7,3},{9,10},{13,14},{10... | collective-permute-start | bytes 147464 | tf_op jit(solution)/shard_map/turn1_gz_1/ppermute | solution.py:31
  6.6 4.8 %collective-permute-start.1 = (f32[3,32,128]{2,1,0:T(8,128)S(1)}, f32[3,32,128]{2,1,0:T(8,128)S(1)}, u32[]{:S(2)}, u32[]{:S(2)}) collective-permute-start(f32[3,32,128]{2,1,0:T(8,128)S(1)} %get-tuple-element.14.own_ref), channel_id=1, source_target_pairs={{0,1},{4,5},{1,0},{5,4},{2,3},{6,7},{3,2},{7,6},{8,9},{12,13},{9,8... | collective-permute-start | bytes 147464 | tf_op jit(solution)/shard_map/turn1_gz_0/ppermute | solution.py:31
  9.3 1.2 %collective-permute-start = (f32[8,8,1,128]{3,2,1,0:T(1,128)S(1)}, f32[8,8,1,128]{3,2,1,0:T(1,128)S(1)}, u32[]{:S(2)}, u32[]{:S(2)}) collective-permute-start(f32[8,8,1,128]{3,2,1,0:T(1,128)S(1)} %get-tuple-element.15), channel_id=1, source_target_pairs={{0,4},{4,0},{1,5},{5,1},{2,6},{6,2},{3,7},{7,3},{8,12},{12,8},{9,1... | collective-permute-start | bytes 98312 | tf_op jit(solution)/shard_map/turn1_gy_0/ppermute | solution.py:25
  13.6 7.7 %collective-permute-start.6 = (f32[9,32,128]{2,1,0:T(8,128)S(1)}, f32[9,32,128]{2,1,0:T(8,128)S(1)}, u32[]{:S(2)}, u32[]{:S(2)}) collective-permute-start(f32[9,32,128]{2,1,0:T(8,128)S(1)} %get-tuple-element.22), channel_id=1, source_target_pairs={{0,8},{4,12},{8,0},{12,4},{16,24},{20,28},{24,16},{28,20},{1,9},{5... | collective-permute-start | bytes 442376 | tf_op jit(solution)/shard_map/turn2_gx_0/ppermute | solution.py:31
  16.6 4.7 %collective-permute-start.7 = (f32[9,32,128]{2,1,0:T(8,128)S(1)}, f32[9,32,128]{2,1,0:T(8,128)S(1)}, u32[]{:S(2)}, u32[]{:S(2)}) collective-permute-start(f32[9,32,128]{2,1,0:T(8,128)S(1)} %get-tuple-element.23), channel_id=1, source_target_pairs={{8,16},{12,20},{16,8},{20,12},{0,4},{4,0},{24,28},{28,24},{9,17},{... | collective-permute-start | bytes 442376 | tf_op jit(solution)/shard_map/turn2_gx_1/ppermute | solution.py:31
  16.6 2.0 %collective-permute-start.5 = (f32[9,8,1,128]{3,2,1,0:T(1,128)S(1)}, f32[9,8,1,128]{3,2,1,0:T(1,128)S(1)}, u32[]{:S(2)}, u32[]{:S(2)}) collective-permute-start(f32[9,8,1,128]{3,2,1,0:T(1,128)S(1)} %get-tuple-element.21), channel_id=1, source_target_pairs={{0,4},{4,0},{1,5},{5,1},{2,6},{6,2},{3,7},{7,3},{8,12},{12,8},{9,1... | collective-permute-start | bytes 110600 | tf_op jit(solution)/shard_map/turn2_gy_0/ppermute | solution.py:25
  20.4 16.2 %copy-start.1 = (f32[8,8,32,128]{3,2,1,0:T(8,128)S(1)}, f32[8,8,32,128]{3,2,1,0:T(8,128)}, u32[]{:S(2)}) copy-start(f32[8,8,32,128]{3,2,1,0:T(8,128)} %b_ref.3) | copy-start | bytes 3145732

commit v6 on v5

--- a/solution.py
+++ b/solution.py
@@ -299,16 +299,27 @@
     return pltpu.roll(matrix, by % LANES, 1)
 
 
-def eliminate(blocks):
-    size = blocks[0].shape[0]
-    sub = lax.broadcasted_iota(jnp.int32, blocks[0].shape, 0)
-    for j in range(size * len(blocks)):
+def solve(columns, right):
+    size = right[0].shape[0]
+    sub = lax.broadcasted_iota(jnp.int32, right[0].shape, 0)
+    for j in range(0, len(columns), 2):
         own, local = divmod(j, size)
-        columns = [lanes_of(block, j) for block in blocks]
-        pivot = rows_of(blocks[own], local) / rows_of(columns[own], local)
-        blocks = [block - column * pivot for block, column in zip(blocks, columns)]
-        blocks[own] = jnp.where(sub == local, pivot, blocks[own])
-    return blocks
+        first, second = columns[j], columns[j + 1]
+        a, b = rows_of(first[own], local), rows_of(second[own], local)
+        c, d = rows_of(first[own], local + 1), rows_of(second[own], local + 1)
+        scale = 1.0 / (a * d - b * c)
+        a, b, c, d = a * scale, b * scale, c * scale, d * scale
+
+        def step(value):
+            upper, lower = rows_of(value[own], local), rows_of(value[own], local + 1)
+            upper, lower = d * upper - b * lower, a * lower - c * upper
+            value = [v - (f * upper + s * lower) for v, f, s in zip(value, first, second)]
+            value[own] = jnp.where(sub == local, upper, jnp.where(sub == local + 1, lower, value[own]))
+            return value
+
+        columns = columns[: j + 2] + [step(column) for column in columns[j + 2 :]]
+        right = step(right)
+    return right
 
 
 def small_algebra(s):
@@ -317,31 +328,27 @@
     lane = lax.broadcasted_iota(jnp.int32, s.shape, 1)
     sub = lax.broadcasted_iota(jnp.int32, s.shape, 0)
     n0, n1, n2, n3, n4 = shift_lanes(s, n), s, shift_lanes(s, -n), shift_lanes(s, -2 * n), shift_lanes(s, -3 * n)
-    (e,) = eliminate([s])
+    (e,) = solve([[lanes_of(s, j)] for j in range(n)], [s])
     p1 = times(s, n, e)
     p2 = times(s, 2 * n, e)
     p3 = times(s, 3 * n, e)
     cc = times(e, n, e)
     e2c = times(e, 2 * n, e)
+    e2 = shift_lanes(e, -n)
     g = n2 - p1
-    q = shift_lanes(e, -n) - cc
+    q = e2 - cc
     n3c = n3 - p2
     f3 = n3c - times(s, n, q)
     f4 = n4 - p3 - times(s, n, shift_lanes(e, -2 * n) - e2c)
     m11 = n2 + 2.0 * c0 * n1 + c0 * c0 * n0
     m12 = n3c + 2.0 * c0 * g
-    m21 = n3 - shift_lanes(p1, -n) + 2.0 * c0 * g
+    m21 = n3 - times(s, n, e2) + 2.0 * c0 * g
     m22 = f4 + 2.0 * c0 * f3 + c0 * c0 * g
-    r1 = n1 + c0 * n0
-
-    def assemble(first, second, third):
-        joined = jnp.where(lane < n, shift_lanes(first, -n), second)
-        return jnp.where(lane < 2 * n, joined, shift_lanes(third, n))
-
-    pa, qa = eliminate([assemble(m11, m12, r1), assemble(m21, m22, g)])
-    cq = times(e, n, qa)
-    on_b = pa - cq
-    unit = jnp.where(lane == sub + 2 * n, 1.0, 0.0)
+    columns = [[lanes_of(m11, n + j), lanes_of(m21, n + j)] for j in range(n)]
+    columns += [[lanes_of(m12, n + j), lanes_of(m22, n + j)] for j in range(n)]
+    pa, qa = solve(columns, [n1 + c0 * n0, g])
+    on_b = pa - times(e, n, qa)
+    unit = jnp.where(lane == sub + n, 1.0, 0.0)
     part = unit - times(e, n, pa) - c0 * pa - times(q, n, qa)
     squares = part * times(s, 0, part)
     pq = pa + c0 * qa
@@ -355,10 +362,10 @@
     n = width
     total = jnp.sum(parts_ref[...], axis=0)
     on_b, on_u, squares = small_algebra(total)
-    norms_ref[...] = jnp.sqrt(shift_lanes(squares, -2 * n))[:, :n]
+    norms_ref[...] = jnp.sqrt(shift_lanes(squares, -n))[:, :n]
     for f in range(width):
-        coeff_ref[0, f] = lanes_of(on_b, 2 * n + f)
-        coeff_ref[1, f] = lanes_of(on_u, 2 * n + f)
+        coeff_ref[0, f] = lanes_of(on_b, n + f)
+        coeff_ref[1, f] = lanes_of(on_u, n + f)
     group = 2
 
     def fields(k, carry):

time: 42.3 us -> 40 us (0.946)
  Pallas kernels: 13.4 us -> 11.1 us
    pallas_call x8, Pallas kernels: 13.4 us -> 11.1 us  [call(): pl.pallas_call(kernel, out_shape=out_shape, in_specs=[pl.BlockSpec(memory...]
where the time goes in v6:
time: 40 us; the launch traced here: 39.8 us
  blocking collectives  14 us (35%)
  Pallas kernels  11.1 us (28%)
  starting transfers between devices  9.69 us (24%)
  waiting for transfers between devices  3.03 us (8%)
  local copies, waits for them, and re-layouts  1.23 us (3%)
  between operations  0.71 us (2%)
    all_to_all x1, blocking collectives, body(): parts = lax.all_to_all(copies, AXES, 0, 0, tiled=True)  14 us
    pallas_call x8, Pallas kernels, call(): pl.pallas_call(kernel, out_shape=out_shape, in_specs=[pl.BlockSpec(memory...  11.1 us
    ppermute x6, starting transfers between devices, swap(): lax.ppermute(values, ('gx', 'gy') if axis == 'gx' else ('gy', 'gz'), joint)  9.18 us
    ppermute x6, waiting for transfers between devices, swap(): lax.ppermute(values, ('gx', 'gy') if axis == 'gx' else ('gy', 'gz'), joint)  1.82 us
    unnamed x6, local copies, waits for them, and re-layouts  1.23 us
    ppermute x2, waiting for transfers between devices, swap(): return lax.ppermute(values, axis, pairs)  1.21 us
  transfers between devices with their start and end apart: 8, of which 3 were waited for; matrix products, arithmetic and copies ran while one was open for 0% of the time, Pallas kernels for 14%

profile of v6, /device:TPU:0, one launch (start us, length us, event | category | flops | bytes accessed | tf_op | source)
XLA Modules:
  0.0 39.8 jit_solution(8707791443892017472)
XLA Ops:
  0.6 0.0 copy-start
  0.6 1.2 %copy-done = f32[8,8,32,128]{3,2,1,0:T(8,128)S(1)} copy-done((f32[8,8,32,128]{3,2,1,0:T(8,128)S(1)}, f32[8,8,32,128]{3,2,1,0:T(8,128)}, u32[]{:S(2)}) %copy-start) | copy-done | bytes 1048600
  1.9 0.0 copy-start.2
  1.9 0.1 cut.1
  1.9 3.0 %collective-permute-start.3 = (f32[8,32,128]{2,1,0:T(8,128)S(1)}, f32[8,32,128]{2,1,0:T(8,128)S(1)}, u32[]{:S(2)}, u32[]{:S(2)}) collective-permute-start(f32[8,32,128]{2,1,0:T(8,128)S(1)} %get-tuple-element.18), channel_id=1, source_target_pairs={{0,8},{4,12},{8,0},{12,4},{16,24},{20,28},{24,16},{28,20},{1,9},{5... | collective-permute-start | bytes 393224 | tf_op jit(solution)/shard_map/turn1_gx_0/ppermute | solution.py:31
  5.0 0.0 collective-permute-start.4
  5.0 0.0 copy-done.2
  5.0 1.1 %pack.1 = (f32[8,8,1,128]{3,2,1,0:T(1,128)S(1)}, f32[3,32,128]{2,1,0:T(8,128)S(1)}) custom-call(f32[8,8,32,128]{3,2,1,0:T(8,128)S(1)} %copy-done, f32[8,32,128]{2,1,0:T(8,128)S(1)} %copy-done.2), custom_call_target="tpu_custom_call" | custom-call | flops 1000000 | bytes 1048576 | tf_op jit(solution)/shard_map/pack/pallas_call | solution.py:391
  6.1 0.5 %collective-permute-start.2 = (f32[3,32,128]{2,1,0:T(8,128)S(1)}, f32[3,32,128]{2,1,0:T(8,128)S(1)}, u32[]{:S(2)}, u32[]{:S(2)}) collective-permute-start(f32[3,32,128]{2,1,0:T(8,128)S(1)} %get-tuple-element.14.own_ref), channel_id=1, source_target_pairs={{1,2},{5,6},{2,1},{6,5},{0,4},{4,0},{3,7},{7,3},{9,10},{13,14},{10... | collective-permute-start | bytes 147464 | tf_op jit(solution)/shard_map/turn1_gz_1/ppermute | solution.py:31
  6.6 2.6 %collective-permute-start.1 = (f32[3,32,128]{2,1,0:T(8,128)S(1)}, f32[3,32,128]{2,1,0:T(8,128)S(1)}, u32[]{:S(2)}, u32[]{:S(2)}) collective-permute-start(f32[3,32,128]{2,1,0:T(8,128)S(1)} %get-tuple-element.14.own_ref), channel_id=1, source_target_pairs={{0,1},{4,5},{1,0},{5,4},{2,3},{6,7},{3,2},{7,6},{8,9},{12,13},{9,8... | collective-permute-start | bytes 147464 | tf_op jit(solution)/shard_map/turn1_gz_0/ppermute | solution.py:31
  9.3 0.0 collective-permute-start
  9.3 1.2 %collective-permute-done.refs_0_.refs_2_ = f32[8,8,1,128]{3,2,1,0:T(1,128)S(1)} collective-permute-done((f32[8,8,1,128]{3,2,1,0:T(1,128)S(1)}, f32[8,8,1,128]{3,2,1,0:T(1,128)S(1)}, u32[]{:S(2)}, u32[]{:S(2)}) %collective-permute-start) | collective-permute-done | bytes 32800 | tf_op jit(solution)/shard_map/turn1_gy_0/ppermute | solution.py:25
  10.5 0.0 collective-permute-done.2.refs_2_
  10.5 0.9 %collective-permute-done.1.refs_1_ = f32[3,32,128]{2,1,0:T(8,128)S(1)} collective-permute-done((f32[3,32,128]{2,1,0:T(8,128)S(1)}, f32[3,32,128]{2,1,0:T(8,128)S(1)}, u32[]{:S(2)}, u32[]{:S(2)}) %collective-permute-start.1) | collective-permute-done | bytes 49184 | tf_op jit(solution)/shard_map/turn1_gz_0/ppermute | solution.py:31
  11.4 1.3 %inner1.1 = (f32[8,8,32,128]{3,2,1,0:T(8,128)S(1)}, f32[2,32,128]{2,1,0:T(8,128)S(1)}) custom-call(f32[8,8,32,128]{3,2,1,0:T(8,128)S(1)} %copy-done, f32[8,32,128]{2,1,0:T(8,128)S(1)} %copy-done.2, f32[3,32,128]{2,1,0:T(8,128)S(1)} %get-tuple-element.14.own_ref, f32[8,8,1,128]{3,2,1,0:T(1,128)S(1)} %collective-permute-done.refs_0_.refs_2_, ...), custom_call_target="tpu_custom_call" | custom-call | flops 20000000 | bytes 1048576 | tf_op jit(solution)/shard_map/inner1/pallas_call | solution.py:391
  12.7 0.0 collective-permute-done.3.refs_0_
  12.7 0.0 collective-permute-done.4.refs_1_
  12.8 0.8 %outer1.1 = (f32[8,8,32,128]{3,2,1,0:T(8,128)S(1)}, f32[9,32,128]{2,1,0:T(8,128)S(1)}, f32[9,32,128]{2,1,0:T(8,128)S(1)}, f32[9,8,1,128]{3,2,1,0:T(1,128)S(1)}) custom-call(f32[8,8,32,128]{3,2,1,0:T(8,128)S(1)} %copy-done, f32[8,32,128]{2,1,0:T(8,128)S(1)} %copy-done.2, ...), custom_call_target="tpu_custom_call", output_to_operand_aliasing={{0}: (2, {})} | custom-call | flops 1000000 | bytes 1048576 | tf_op jit(solution)/shard_map/outer1/pallas_call | solution.py:391
  13.6 3.0 %collective-permute-start.6 = (f32[9,32,128]{2,1,0:T(8,128)S(1)}, f32[9,32,128]{2,1,0:T(8,128)S(1)}, u32[]{:S(2)}, u32[]{:S(2)}) collective-permute-start(f32[9,32,128]{2,1,0:T(8,128)S(1)} %get-tuple-element.22), channel_id=1, source_target_pairs={{0,8},{4,12},{8,0},{12,4},{16,24},{20,28},{24,16},{28,20},{1,9},{5... | collective-permute-start | bytes 442376 | tf_op jit(solution)/shard_map/turn2_gx_0/ppermute | solution.py:31
  16.6 0.0 collective-permute-start.7
  16.6 0.5 %collective-permute-start.5 = (f32[9,8,1,128]{3,2,1,0:T(1,128)S(1)}, f32[9,8,1,128]{3,2,1,0:T(1,128)S(1)}, u32[]{:S(2)}, u32[]{:S(2)}) collective-permute-start(f32[9,8,1,128]{3,2,1,0:T(1,128)S(1)} %get-tuple-element.21), channel_id=1, source_target_pairs={{0,4},{4,0},{1,5},{5,1},{2,6},{6,2},{3,7},{7,3},{8,12},{12,8},{9,1... | collective-permute-start | bytes 110600 | tf_op jit(solution)/shard_map/turn2_gy_0/ppermute | solution.py:25
  17.1 1.5 %early.1.early_ref = f32[8,128]{1,0:T(8,128)S(1)} custom-call(f32[8,8,32,128]{3,2,1,0:T(8,128)S(1)} %copy-done, f32[8,8,32,128]{3,2,1,0:T(8,128)S(1)} %get-tuple-element.20.u_ref), custom_call_target="tpu_custom_call" | custom-call | flops 15000000 | bytes 1048576 | tf_op jit(solution)/shard_map/early/pallas_call | solution.py:391
  18.6 0.0 collective-permute-done.5.refs_0_.refs_2_
  18.6 1.8 %inner2.1.sums_ref = f32[2,36,8,128]{3,2,1,0:T(8,128)S(1)} custom-call(f32[8,8,32,128]{3,2,1,0:T(8,128)S(1)} %get-tuple-element.20.u_ref, f32[8,32,128]{2,1,0:T(8,128)S(1)} %copy-done.2, f32[2,32,128]{2,1,0:T(8,128)S(1)} %get-tuple-element.17.ends_ref, f32[9,8,1,128]{3,2,1,0:T(1,128)S(1)} %collective-permute-done.5.refs_0_.refs_2_), custom_call_target="tpu_custom_call" | custom-call | flops 15000000 | bytes 1048576 | tf_op jit(solution)/shard_map/inner2/pallas_call | solution.py:391
  20.4 0.0 copy-start.1
  20.4 0.9 %collective-permute-done.6.refs_0_ = f32[9,32,128]{2,1,0:T(8,128)S(1)} collective-permute-done((f32[9,32,128]{2,1,0:T(8,128)S(1)}, f32[9,32,128]{2,1,0:T(8,128)S(1)}, u32[]{:S(2)}, u32[]{:S(2)}) %collective-permute-start.6) | collective-permute-done | bytes 147488 | tf_op jit(solution)/shard_map/turn2_gx_0/ppermute | solution.py:31
  21.3 0.0 collective-permute-done.7.refs_1_
  21.3 1.3 %outer2.1 = f32[32,8,128]{2,1,0:T(8,128)S(1)} custom-call(f32[8,8,32,128]{3,2,1,0:T(8,128)S(1)} %get-tuple-element.20.u_ref, f32[8,32,128]{2,1,0:T(8,128)S(1)} %copy-done.2, f32[2,32,128]{2,1,0:T(8,128)S(1)} %get-tuple-element.17.ends_ref, f32[2,36,8,128]{3,2,1,0:T(8,128)S(1)} %inner2.1.sums_ref, f32[8,128]{1,0:T(8,128)S(1)} %early.1.early_ref, ...), custom_call_target="tpu_custom_call" | custom-call | flops 1000000 | bytes 1048576 | tf_op jit(solution)/shard_map/outer2/pallas_call | solution.py:391
  22.6 14.0 %all_to_all.5.parts_ref = f32[32,8,128]{2,1,0:T(8,128)S(1)} all-to-all(f32[32,8,128]{2,1,0:T(8,128)S(1)} %outer2.1), channel_id=1, replica_groups=mesh['gx'=4,'gy'=2,'gz'=4] {'gx','gy','gz'}, dimensions={0} | all-to-all | bytes 262144 | tf_op jit(solution)/shard_map/all_to_all | solution.py:470
  36.6 0.0 copy-done.1
  36.6 3.2 %finish.1 = (f32[8,8,32,128]{3,2,1,0:T(8,128)}, f32[1,8]{1,0:T(1,128)}) custom-call(f32[32,8,128]{2,1,0:T(8,128)S(1)} %all_to_all.5.parts_ref, f32[8,8,32,128]{3,2,1,0:T(8,128)S(1)} %copy-done.1, f32[8,8,32,128]{3,2,1,0:T(8,128)S(1)} %get-tuple-element.20.u_ref), custom_call_target="tpu_custom_call" | custom-call | flops 1000000 | bytes 1048576 | tf_op jit(solution)/shard_map/finish/pallas_call | solution.py:391
Async XLA Ops:
  0.6 1.2 %copy-start = (f32[8,8,32,128]{3,2,1,0:T(8,128)S(1)}, f32[8,8,32,128]{3,2,1,0:T(8,128)}, u32[]{:S(2)}) copy-start(f32[8,8,32,128]{3,2,1,0:T(8,128)} %b_ref.3) | copy-start | bytes 3145732
  1.9 3.1 %copy-start.2 = (f32[8,32,128]{2,1,0:T(8,128)S(1)}, f32[8,32,128]{2,1,0:T(8,128)}, u32[]{:S(2)}) copy-start(f32[8,32,128]{2,1,0:T(8,128)} %shift_ref.9) | copy-start | bytes 393220
  1.9 10.8 %collective-permute-start.3 = (f32[8,32,128]{2,1,0:T(8,128)S(1)}, f32[8,32,128]{2,1,0:T(8,128)S(1)}, u32[]{:S(2)}, u32[]{:S(2)}) collective-permute-start(f32[8,32,128]{2,1,0:T(8,128)S(1)} %get-tuple-element.18), channel_id=1, source_target_pairs={{0,8},{4,12},{8,0},{12,4},{16,24},{20,28},{24,16},{28,20},{1,9},{5... | collective-permute-start | bytes 393224 | tf_op jit(solution)/shard_map/turn1_gx_0/ppermute | solution.py:31
  5.0 7.8 %collective-permute-start.4 = (f32[8,32,128]{2,1,0:T(8,128)S(1)}, f32[8,32,128]{2,1,0:T(8,128)S(1)}, u32[]{:S(2)}, u32[]{:S(2)}) collective-permute-start(f32[8,32,128]{2,1,0:T(8,128)S(1)} %get-tuple-element.19), channel_id=1, source_target_pairs={{8,16},{12,20},{16,8},{20,12},{0,4},{4,0},{24,28},{28,24},{9,17},{... | collective-permute-start | bytes 393224 | tf_op jit(solution)/shard_map/turn1_gx_1/ppermute | solution.py:31
  6.1 4.4 %collective-permute-start.2 = (f32[3,32,128]{2,1,0:T(8,128)S(1)}, f32[3,32,128]{2,1,0:T(8,128)S(1)}, u32[]{:S(2)}, u32[]{:S(2)}) collective-permute-start(f32[3,32,128]{2,1,0:T(8,128)S(1)} %get-tuple-element.14.own_ref), channel_id=1, source_target_pairs={{1,2},{5,6},{2,1},{6,5},{0,4},{4,0},{3,7},{7,3},{9,10},{13,14},{10... | collective-permute-start | bytes 147464 | tf_op jit(solution)/shard_map/turn1_gz_1/ppermute | solution.py:31
  6.6 4.8 %collective-permute-start.1 = (f32[3,32,128]{2,1,0:T(8,128)S(1)}, f32[3,32,128]{2,1,0:T(8,128)S(1)}, u32[]{:S(2)}, u32[]{:S(2)}) collective-permute-start(f32[3,32,128]{2,1,0:T(8,128)S(1)} %get-tuple-element.14.own_ref), channel_id=1, source_target_pairs={{0,1},{4,5},{1,0},{5,4},{2,3},{6,7},{3,2},{7,6},{8,9},{12,13},{9,8... | collective-permute-start | bytes 147464 | tf_op jit(solution)/shard_map/turn1_gz_0/ppermute | solution.py:31
  9.3 1.2 %collective-permute-start = (f32[8,8,1,128]{3,2,1,0:T(1,128)S(1)}, f32[8,8,1,128]{3,2,1,0:T(1,128)S(1)}, u32[]{:S(2)}, u32[]{:S(2)}) collective-permute-start(f32[8,8,1,128]{3,2,1,0:T(1,128)S(1)} %get-tuple-element.15), channel_id=1, source_target_pairs={{0,4},{4,0},{1,5},{5,1},{2,6},{6,2},{3,7},{7,3},{8,12},{12,8},{9,1... | collective-permute-start | bytes 98312 | tf_op jit(solution)/shard_map/turn1_gy_0/ppermute | solution.py:25
  13.6 7.7 %collective-permute-start.6 = (f32[9,32,128]{2,1,0:T(8,128)S(1)}, f32[9,32,128]{2,1,0:T(8,128)S(1)}, u32[]{:S(2)}, u32[]{:S(2)}) collective-permute-start(f32[9,32,128]{2,1,0:T(8,128)S(1)} %get-tuple-element.22), channel_id=1, source_target_pairs={{0,8},{4,12},{8,0},{12,4},{16,24},{20,28},{24,16},{28,20},{1,9},{5... | collective-permute-start | bytes 442376 | tf_op jit(solution)/shard_map/turn2_gx_0/ppermute | solution.py:31
  16.6 4.7 %collective-permute-start.7 = (f32[9,32,128]{2,1,0:T(8,128)S(1)}, f32[9,32,128]{2,1,0:T(8,128)S(1)}, u32[]{:S(2)}, u32[]{:S(2)}) collective-permute-start(f32[9,32,128]{2,1,0:T(8,128)S(1)} %get-tuple-element.23), channel_id=1, source_target_pairs={{8,16},{12,20},{16,8},{20,12},{0,4},{4,0},{24,28},{28,24},{9,17},{... | collective-permute-start | bytes 442376 | tf_op jit(solution)/shard_map/turn2_gx_1/ppermute | solution.py:31
  16.6 2.0 %collective-permute-start.5 = (f32[9,8,1,128]{3,2,1,0:T(1,128)S(1)}, f32[9,8,1,128]{3,2,1,0:T(1,128)S(1)}, u32[]{:S(2)}, u32[]{:S(2)}) collective-permute-start(f32[9,8,1,128]{3,2,1,0:T(1,128)S(1)} %get-tuple-element.21), channel_id=1, source_target_pairs={{0,4},{4,0},{1,5},{5,1},{2,6},{6,2},{3,7},{7,3},{8,12},{12,8},{9,1... | collective-permute-start | bytes 110600 | tf_op jit(solution)/shard_map/turn2_gy_0/ppermute | solution.py:25
  20.4 16.2 %copy-start.1 = (f32[8,8,32,128]{3,2,1,0:T(8,128)S(1)}, f32[8,8,32,128]{3,2,1,0:T(8,128)}, u32[]{:S(2)}) copy-start(f32[8,8,32,128]{3,2,1,0:T(8,128)} %b_ref.3) | copy-start | bytes 3145732

commit v7 on v6

--- a/solution.py
+++ b/solution.py
@@ -84,7 +84,7 @@
             packed = packed_ends(v_ref[f, x], f * nx + x, lane, *packed)
         return packed
 
-    near, far = lax.fori_loop(0, width, field, (nothing, nothing))
+    near, far = lax.fori_loop(0, width, field, (nothing, nothing), unroll=width)
     diagonal = nothing
     for x in range(nx):
         diagonal = packed_ends((6.0 - CENTRE) + shift_ref[x], x, lane, diagonal)
@@ -171,7 +171,7 @@
             out_ref[f, x] = ((6.0 - CENTRE) + shift_ref[x]) * v - beside
         return carry
 
-    lax.fori_loop(0, width, field, 0)
+    lax.fori_loop(0, width, field, 0, unroll=width)
 
 
 def split(refs, *counts):

time: 40 us -> 37.7 us (0.943)
  Pallas kernels: 11.1 us -> 8.28 us
  waiting for transfers between devices: 3.03 us -> 3.52 us
    pallas_call x8, Pallas kernels: 11.1 us -> 8.28 us  [call(): pl.pallas_call(kernel, out_shape=out_shape, in_specs=[pl.BlockSpec(memory...]
    ppermute x6, waiting for transfers between devices: 1.82 us -> 2.32 us  [swap(): lax.ppermute(values, ('gx', 'gy') if axis == 'gx' else ('gy', 'gz'), joint)]
  transfers between devices with their start and end apart: 8 -> 8, of which waited for: 3 -> 3; matrix products, arithmetic and copies ran while one was open for 0% -> 0% of each run, Pallas kernels for 14% -> 11%
where the time goes in v7:
time: 37.7 us; the launch traced here: 37.5 us
  blocking collectives  14 us (37%)
  starting transfers between devices  9.74 us (26%)
  Pallas kernels  8.28 us (22%)
  waiting for transfers between devices  3.52 us (9%)
  local copies, waits for them, and re-layouts  1.23 us (3%)
  between operations  0.71 us (2%)
    all_to_all x1, blocking collectives, body(): parts = lax.all_to_all(copies, AXES, 0, 0, tiled=True)  14 us
    ppermute x6, starting transfers between devices, swap(): lax.ppermute(values, ('gx', 'gy') if axis == 'gx' else ('gy', 'gz'), joint)  9.23 us
    pallas_call x8, Pallas kernels, call(): pl.pallas_call(kernel, out_shape=out_shape, in_specs=[pl.BlockSpec(memory...  8.28 us
    ppermute x6, waiting for transfers between devices, swap(): lax.ppermute(values, ('gx', 'gy') if axis == 'gx' else ('gy', 'gz'), joint)  2.32 us
    unnamed x6, local copies, waits for them, and re-layouts  1.23 us
    ppermute x2, waiting for transfers between devices, swap(): return lax.ppermute(values, axis, pairs)  1.21 us
  transfers between devices with their start and end apart: 8, of which 3 were waited for; matrix products, arithmetic and copies ran while one was open for 0% of the time, Pallas kernels for 11%

profile of v7, /device:TPU:0, one launch (start us, length us, event | category | flops | bytes accessed | tf_op | source)
XLA Modules:
  0.0 37.5 jit_solution(14084392528431471741)
XLA Ops:
  0.6 0.0 copy-start
  0.6 1.2 %copy-done = f32[8,8,32,128]{3,2,1,0:T(8,128)S(1)} copy-done((f32[8,8,32,128]{3,2,1,0:T(8,128)S(1)}, f32[8,8,32,128]{3,2,1,0:T(8,128)}, u32[]{:S(2)}) %copy-start) | copy-done | bytes 1048600
  1.9 0.0 copy-start.2
  1.9 0.1 cut.1
  1.9 3.0 %collective-permute-start.3 = (f32[8,32,128]{2,1,0:T(8,128)S(1)}, f32[8,32,128]{2,1,0:T(8,128)S(1)}, u32[]{:S(2)}, u32[]{:S(2)}) collective-permute-start(f32[8,32,128]{2,1,0:T(8,128)S(1)} %get-tuple-element.18), channel_id=1, source_target_pairs={{0,8},{4,12},{8,0},{12,4},{16,24},{20,28},{24,16},{28,20},{1,9},{5... | collective-permute-start | bytes 393224 | tf_op jit(solution)/shard_map/turn1_gx_0/ppermute | solution.py:31
  5.0 0.0 collective-permute-start.4
  5.0 0.0 copy-done.2
  5.0 0.5 %pack.1 = (f32[8,8,1,128]{3,2,1,0:T(1,128)S(1)}, f32[3,32,128]{2,1,0:T(8,128)S(1)}) custom-call(f32[8,8,32,128]{3,2,1,0:T(8,128)S(1)} %copy-done, f32[8,32,128]{2,1,0:T(8,128)S(1)} %copy-done.2), custom_call_target="tpu_custom_call" | custom-call | flops 1000000 | bytes 1048576 | tf_op jit(solution)/shard_map/pack/pallas_call | solution.py:391
  5.4 0.6 %collective-permute-start.2 = (f32[3,32,128]{2,1,0:T(8,128)S(1)}, f32[3,32,128]{2,1,0:T(8,128)S(1)}, u32[]{:S(2)}, u32[]{:S(2)}) collective-permute-start(f32[3,32,128]{2,1,0:T(8,128)S(1)} %get-tuple-element.14.own_ref), channel_id=1, source_target_pairs={{1,2},{5,6},{2,1},{6,5},{0,4},{4,0},{3,7},{7,3},{9,10},{13,14},{10... | collective-permute-start | bytes 147464 | tf_op jit(solution)/shard_map/turn1_gz_1/ppermute | solution.py:31
  6.0 2.6 %collective-permute-start.1 = (f32[3,32,128]{2,1,0:T(8,128)S(1)}, f32[3,32,128]{2,1,0:T(8,128)S(1)}, u32[]{:S(2)}, u32[]{:S(2)}) collective-permute-start(f32[3,32,128]{2,1,0:T(8,128)S(1)} %get-tuple-element.14.own_ref), channel_id=1, source_target_pairs={{0,1},{4,5},{1,0},{5,4},{2,3},{6,7},{3,2},{7,6},{8,9},{12,13},{9,8... | collective-permute-start | bytes 147464 | tf_op jit(solution)/shard_map/turn1_gz_0/ppermute | solution.py:31
  8.7 0.0 collective-permute-start
  8.7 1.2 %collective-permute-done.refs_0_.refs_2_ = f32[8,8,1,128]{3,2,1,0:T(1,128)S(1)} collective-permute-done((f32[8,8,1,128]{3,2,1,0:T(1,128)S(1)}, f32[8,8,1,128]{3,2,1,0:T(1,128)S(1)}, u32[]{:S(2)}, u32[]{:S(2)}) %collective-permute-start) | collective-permute-done | bytes 32800 | tf_op jit(solution)/shard_map/turn1_gy_0/ppermute | solution.py:25
  9.9 0.0 collective-permute-done.2.refs_2_
  9.9 0.9 %collective-permute-done.1.refs_1_ = f32[3,32,128]{2,1,0:T(8,128)S(1)} collective-permute-done((f32[3,32,128]{2,1,0:T(8,128)S(1)}, f32[3,32,128]{2,1,0:T(8,128)S(1)}, u32[]{:S(2)}, u32[]{:S(2)}) %collective-permute-start.1) | collective-permute-done | bytes 49184 | tf_op jit(solution)/shard_map/turn1_gz_0/ppermute | solution.py:31
  10.8 0.7 %inner1.1 = (f32[8,8,32,128]{3,2,1,0:T(8,128)S(1)}, f32[2,32,128]{2,1,0:T(8,128)S(1)}) custom-call(f32[8,8,32,128]{3,2,1,0:T(8,128)S(1)} %copy-done, f32[8,32,128]{2,1,0:T(8,128)S(1)} %copy-done.2, f32[3,32,128]{2,1,0:T(8,128)S(1)} %get-tuple-element.14.own_ref, f32[8,8,1,128]{3,2,1,0:T(1,128)S(1)} %collective-permute-done.refs_0_.refs_2_, ...), custom_call_target="tpu_custom_call" | custom-call | flops 20000000 | bytes 1048576 | tf_op jit(solution)/shard_map/inner1/pallas_call | solution.py:391
  11.5 0.0 collective-permute-done.3.refs_0_
  11.5 0.0 collective-permute-done.4.refs_1_
  11.6 0.3 outer1.1
  11.9 3.0 %collective-permute-start.6 = (f32[9,32,128]{2,1,0:T(8,128)S(1)}, f32[9,32,128]{2,1,0:T(8,128)S(1)}, u32[]{:S(2)}, u32[]{:S(2)}) collective-permute-start(f32[9,32,128]{2,1,0:T(8,128)S(1)} %get-tuple-element.22), channel_id=1, source_target_pairs={{0,8},{4,12},{8,0},{12,4},{16,24},{20,28},{24,16},{28,20},{1,9},{5... | collective-permute-start | bytes 442376 | tf_op jit(solution)/shard_map/turn2_gx_0/ppermute | solution.py:31
  14.8 0.0 collective-permute-start.7
  14.9 0.5 %collective-permute-start.5 = (f32[9,8,1,128]{3,2,1,0:T(1,128)S(1)}, f32[9,8,1,128]{3,2,1,0:T(1,128)S(1)}, u32[]{:S(2)}, u32[]{:S(2)}) collective-permute-start(f32[9,8,1,128]{3,2,1,0:T(1,128)S(1)} %get-tuple-element.21), channel_id=1, source_target_pairs={{0,4},{4,0},{1,5},{5,1},{2,6},{6,2},{3,7},{7,3},{8,12},{12,8},{9,1... | collective-permute-start | bytes 110600 | tf_op jit(solution)/shard_map/turn2_gy_0/ppermute | solution.py:25
  15.4 1.5 %early.1.early_ref = f32[8,128]{1,0:T(8,128)S(1)} custom-call(f32[8,8,32,128]{3,2,1,0:T(8,128)S(1)} %copy-done, f32[8,8,32,128]{3,2,1,0:T(8,128)S(1)} %get-tuple-element.20.u_ref), custom_call_target="tpu_custom_call" | custom-call | flops 15000000 | bytes 1048576 | tf_op jit(solution)/shard_map/early/pallas_call | solution.py:391
  16.9 0.0 collective-permute-done.5.refs_0_.refs_2_
  16.9 1.3 %inner2.1.sums_ref = f32[2,36,8,128]{3,2,1,0:T(8,128)S(1)} custom-call(f32[8,8,32,128]{3,2,1,0:T(8,128)S(1)} %get-tuple-element.20.u_ref, f32[8,32,128]{2,1,0:T(8,128)S(1)} %copy-done.2, f32[2,32,128]{2,1,0:T(8,128)S(1)} %get-tuple-element.17.ends_ref, f32[9,8,1,128]{3,2,1,0:T(1,128)S(1)} %collective-permute-done.5.refs_0_.refs_2_), custom_call_target="tpu_custom_call" | custom-call | flops 15000000 | bytes 1048576 | tf_op jit(solution)/shard_map/inner2/pallas_call | solution.py:391
  18.2 0.0 copy-start.1
  18.2 1.4 %collective-permute-done.6.refs_0_ = f32[9,32,128]{2,1,0:T(8,128)S(1)} collective-permute-done((f32[9,32,128]{2,1,0:T(8,128)S(1)}, f32[9,32,128]{2,1,0:T(8,128)S(1)}, u32[]{:S(2)}, u32[]{:S(2)}) %collective-permute-start.6) | collective-permute-done | bytes 147488 | tf_op jit(solution)/shard_map/turn2_gx_0/ppermute | solution.py:31
  19.6 0.0 collective-permute-done.7.refs_1_
  19.6 0.7 %outer2.1 = f32[32,8,128]{2,1,0:T(8,128)S(1)} custom-call(f32[8,8,32,128]{3,2,1,0:T(8,128)S(1)} %get-tuple-element.20.u_ref, f32[8,32,128]{2,1,0:T(8,128)S(1)} %copy-done.2, f32[2,32,128]{2,1,0:T(8,128)S(1)} %get-tuple-element.17.ends_ref, f32[2,36,8,128]{3,2,1,0:T(8,128)S(1)} %inner2.1.sums_ref, f32[8,128]{1,0:T(8,128)S(1)} %early.1.early_ref, ...), custom_call_target="tpu_custom_call" | custom-call | flops 1000000 | bytes 1048576 | tf_op jit(solution)/shard_map/outer2/pallas_call | solution.py:391
  20.3 14.0 %all_to_all.5.parts_ref = f32[32,8,128]{2,1,0:T(8,128)S(1)} all-to-all(f32[32,8,128]{2,1,0:T(8,128)S(1)} %outer2.1), channel_id=1, replica_groups=mesh['gx'=4,'gy'=2,'gz'=4] {'gx','gy','gz'}, dimensions={0} | all-to-all | bytes 262144 | tf_op jit(solution)/shard_map/all_to_all | solution.py:470
  34.3 0.0 copy-done.1
  34.3 3.2 %finish.1 = (f32[8,8,32,128]{3,2,1,0:T(8,128)}, f32[1,8]{1,0:T(1,128)}) custom-call(f32[32,8,128]{2,1,0:T(8,128)S(1)} %all_to_all.5.parts_ref, f32[8,8,32,128]{3,2,1,0:T(8,128)S(1)} %copy-done.1, f32[8,8,32,128]{3,2,1,0:T(8,128)S(1)} %get-tuple-element.20.u_ref), custom_call_target="tpu_custom_call" | custom-call | flops 1000000 | bytes 1048576 | tf_op jit(solution)/shard_map/finish/pallas_call | solution.py:391
Async XLA Ops:
  0.6 1.2 %copy-start = (f32[8,8,32,128]{3,2,1,0:T(8,128)S(1)}, f32[8,8,32,128]{3,2,1,0:T(8,128)}, u32[]{:S(2)}) copy-start(f32[8,8,32,128]{3,2,1,0:T(8,128)} %b_ref.3) | copy-start | bytes 3145732
  1.9 3.1 %copy-start.2 = (f32[8,32,128]{2,1,0:T(8,128)S(1)}, f32[8,32,128]{2,1,0:T(8,128)}, u32[]{:S(2)}) copy-start(f32[8,32,128]{2,1,0:T(8,128)} %shift_ref.9) | copy-start | bytes 393220
  1.9 9.6 %collective-permute-start.3 = (f32[8,32,128]{2,1,0:T(8,128)S(1)}, f32[8,32,128]{2,1,0:T(8,128)S(1)}, u32[]{:S(2)}, u32[]{:S(2)}) collective-permute-start(f32[8,32,128]{2,1,0:T(8,128)S(1)} %get-tuple-element.18), channel_id=1, source_target_pairs={{0,8},{4,12},{8,0},{12,4},{16,24},{20,28},{24,16},{28,20},{1,9},{5... | collective-permute-start | bytes 393224 | tf_op jit(solution)/shard_map/turn1_gx_0/ppermute | solution.py:31
  5.0 6.6 %collective-permute-start.4 = (f32[8,32,128]{2,1,0:T(8,128)S(1)}, f32[8,32,128]{2,1,0:T(8,128)S(1)}, u32[]{:S(2)}, u32[]{:S(2)}) collective-permute-start(f32[8,32,128]{2,1,0:T(8,128)S(1)} %get-tuple-element.19), channel_id=1, source_target_pairs={{8,16},{12,20},{16,8},{20,12},{0,4},{4,0},{24,28},{28,24},{9,17},{... | collective-permute-start | bytes 393224 | tf_op jit(solution)/shard_map/turn1_gx_1/ppermute | solution.py:31
  5.4 4.4 %collective-permute-start.2 = (f32[3,32,128]{2,1,0:T(8,128)S(1)}, f32[3,32,128]{2,1,0:T(8,128)S(1)}, u32[]{:S(2)}, u32[]{:S(2)}) collective-permute-start(f32[3,32,128]{2,1,0:T(8,128)S(1)} %get-tuple-element.14.own_ref), channel_id=1, source_target_pairs={{1,2},{5,6},{2,1},{6,5},{0,4},{4,0},{3,7},{7,3},{9,10},{13,14},{10... | collective-permute-start | bytes 147464 | tf_op jit(solution)/shard_map/turn1_gz_1/ppermute | solution.py:31
  6.0 4.8 %collective-permute-start.1 = (f32[3,32,128]{2,1,0:T(8,128)S(1)}, f32[3,32,128]{2,1,0:T(8,128)S(1)}, u32[]{:S(2)}, u32[]{:S(2)}) collective-permute-start(f32[3,32,128]{2,1,0:T(8,128)S(1)} %get-tuple-element.14.own_ref), channel_id=1, source_target_pairs={{0,1},{4,5},{1,0},{5,4},{2,3},{6,7},{3,2},{7,6},{8,9},{12,13},{9,8... | collective-permute-start | bytes 147464 | tf_op jit(solution)/shard_map/turn1_gz_0/ppermute | solution.py:31
  8.7 1.2 %collective-permute-start = (f32[8,8,1,128]{3,2,1,0:T(1,128)S(1)}, f32[8,8,1,128]{3,2,1,0:T(1,128)S(1)}, u32[]{:S(2)}, u32[]{:S(2)}) collective-permute-start(f32[8,8,1,128]{3,2,1,0:T(1,128)S(1)} %get-tuple-element.15), channel_id=1, source_target_pairs={{0,4},{4,0},{1,5},{5,1},{2,6},{6,2},{3,7},{7,3},{8,12},{12,8},{9,1... | collective-permute-start | bytes 98312 | tf_op jit(solution)/shard_map/turn1_gy_0/ppermute | solution.py:25
  11.9 7.7 %collective-permute-start.6 = (f32[9,32,128]{2,1,0:T(8,128)S(1)}, f32[9,32,128]{2,1,0:T(8,128)S(1)}, u32[]{:S(2)}, u32[]{:S(2)}) collective-permute-start(f32[9,32,128]{2,1,0:T(8,128)S(1)} %get-tuple-element.22), channel_id=1, source_target_pairs={{0,8},{4,12},{8,0},{12,4},{16,24},{20,28},{24,16},{28,20},{1,9},{5... | collective-permute-start | bytes 442376 | tf_op jit(solution)/shard_map/turn2_gx_0/ppermute | solution.py:31
  14.8 4.7 %collective-permute-start.7 = (f32[9,32,128]{2,1,0:T(8,128)S(1)}, f32[9,32,128]{2,1,0:T(8,128)S(1)}, u32[]{:S(2)}, u32[]{:S(2)}) collective-permute-start(f32[9,32,128]{2,1,0:T(8,128)S(1)} %get-tuple-element.23), channel_id=1, source_target_pairs={{8,16},{12,20},{16,8},{20,12},{0,4},{4,0},{24,28},{28,24},{9,17},{... | collective-permute-start | bytes 442376 | tf_op jit(solution)/shard_map/turn2_gx_1/ppermute | solution.py:31
  14.9 2.0 %collective-permute-start.5 = (f32[9,8,1,128]{3,2,1,0:T(1,128)S(1)}, f32[9,8,1,128]{3,2,1,0:T(1,128)S(1)}, u32[]{:S(2)}, u32[]{:S(2)}) collective-permute-start(f32[9,8,1,128]{3,2,1,0:T(1,128)S(1)} %get-tuple-element.21), channel_id=1, source_target_pairs={{0,4},{4,0},{1,5},{5,1},{2,6},{6,2},{3,7},{7,3},{8,12},{12,8},{9,1... | collective-permute-start | bytes 110600 | tf_op jit(solution)/shard_map/turn2_gy_0/ppermute | solution.py:25
  18.2 16.1 %copy-start.1 = (f32[8,8,32,128]{3,2,1,0:T(8,128)S(1)}, f32[8,8,32,128]{3,2,1,0:T(8,128)}, u32[]{:S(2)}) copy-start(f32[8,8,32,128]{3,2,1,0:T(8,128)} %b_ref.3) | copy-start | bytes 3145732

commit v8 on v7

--- a/solution.py
+++ b/solution.py
@@ -276,7 +276,8 @@
     for h, left in enumerate((u_ref, t_ref)):
         inner = [sums_ref[h, k] for k in range(len(pairs_of(width)))]
         payload = put_moment(width, moment_sums(0, nx, nx - 1, left, t_ref, inner), (3 + h) * width, payload)
-    out_ref[...] = jnp.broadcast_to(payload[None], out_ref.shape)
+    folded = payload[:4] + shift_lanes(payload, LANES // 2)[4:]
+    out_ref[...] = jnp.broadcast_to(folded[None], out_ref.shape)
 
 
 def lanes_of(matrix, j):
@@ -360,7 +361,8 @@
 def finish_kernel(parts_ref, b_ref, u_ref, out_ref, norms_ref, coeff_ref):
     width, nx, ny, _ = b_ref.shape
     n = width
-    total = jnp.sum(parts_ref[...], axis=0)
+    folded = jnp.sum(parts_ref[...], axis=0)
+    total = jnp.concatenate([folded, shift_lanes(folded, LANES // 2)], axis=0)
     on_b, on_u, squares = small_algebra(total)
     norms_ref[...] = jnp.sqrt(shift_lanes(squares, -n))[:, :n]
     for f in range(width):
@@ -382,7 +384,7 @@
                     out_ref[group * k + d, x, y : y + 8, :] = total
             return carry
 
-        return lax.fori_loop(0, nx, plane, carry)
+        return lax.fori_loop(0, nx, plane, carry, unroll=nx)
 
     lax.fori_loop(0, width // group, fields, 0)
 
@@ -462,7 +464,7 @@
     )
     copies = call(
         kernel(outer_late_kernel, nx_r, ny_r),
-        jax.ShapeDtypeStruct((devices, 8, LANES), F32),
+        jax.ShapeDtypeStruct((devices, 4, LANES), F32),
         [u, shift, ends, sums, early, *halo_x, *halo_y],
         scratch=[full],
         name="outer2",

time: 37.7 us -> 36.6 us (0.971)
  blocking collectives: 14 us -> 13.1 us
    all_to_all x1, blocking collectives: 14 us -> 13.1 us  [body(): parts = lax.all_to_all(copies, AXES, 0, 0, tiled=True)]
where the time goes in v8:
time: 36.6 us; the launch traced here: 36.4 us
  blocking collectives  13.1 us (36%)
  starting transfers between devices  9.74 us (27%)
  Pallas kernels  8.13 us (22%)
  waiting for transfers between devices  3.52 us (10%)
  local copies, waits for them, and re-layouts  1.23 us (3%)
  between operations  0.71 us (2%)
    all_to_all x1, blocking collectives, body(): parts = lax.all_to_all(copies, AXES, 0, 0, tiled=True)  13.1 us
    ppermute x6, starting transfers between devices, swap(): lax.ppermute(values, ('gx', 'gy') if axis == 'gx' else ('gy', 'gz'), joint)  9.23 us
    pallas_call x8, Pallas kernels, call(): pl.pallas_call(kernel, out_shape=out_shape, in_specs=[pl.BlockSpec(memory...  8.13 us
    ppermute x6, waiting for transfers between devices, swap(): lax.ppermute(values, ('gx', 'gy') if axis == 'gx' else ('gy', 'gz'), joint)  2.31 us
    unnamed x6, local copies, waits for them, and re-layouts  1.23 us
    ppermute x2, waiting for transfers between devices, swap(): return lax.ppermute(values, axis, pairs)  1.21 us
  transfers between devices with their start and end apart: 8, of which 3 were waited for; matrix products, arithmetic and copies ran while one was open for 0% of the time, Pallas kernels for 11%

profile of v8, /device:TPU:0, one launch (start us, length us, event | category | flops | bytes accessed | tf_op | source)
XLA Modules:
  0.0 36.4 jit_solution(9039221484450032821)
XLA Ops:
  0.6 0.0 copy-start
  0.6 1.2 %copy-done = f32[8,8,32,128]{3,2,1,0:T(8,128)S(1)} copy-done((f32[8,8,32,128]{3,2,1,0:T(8,128)S(1)}, f32[8,8,32,128]{3,2,1,0:T(8,128)}, u32[]{:S(2)}) %copy-start) | copy-done | bytes 1048600
  1.9 0.0 copy-start.2
  1.9 0.1 cut.1
  1.9 3.0 %collective-permute-start.3 = (f32[8,32,128]{2,1,0:T(8,128)S(1)}, f32[8,32,128]{2,1,0:T(8,128)S(1)}, u32[]{:S(2)}, u32[]{:S(2)}) collective-permute-start(f32[8,32,128]{2,1,0:T(8,128)S(1)} %get-tuple-element.18), channel_id=1, source_target_pairs={{0,8},{4,12},{8,0},{12,4},{16,24},{20,28},{24,16},{28,20},{1,9},{5... | collective-permute-start | bytes 393224 | tf_op jit(solution)/shard_map/turn1_gx_0/ppermute | solution.py:31
  5.0 0.0 collective-permute-start.4
  5.0 0.0 copy-done.2
  5.0 0.5 %pack.1 = (f32[8,8,1,128]{3,2,1,0:T(1,128)S(1)}, f32[3,32,128]{2,1,0:T(8,128)S(1)}) custom-call(f32[8,8,32,128]{3,2,1,0:T(8,128)S(1)} %copy-done, f32[8,32,128]{2,1,0:T(8,128)S(1)} %copy-done.2), custom_call_target="tpu_custom_call" | custom-call | flops 1000000 | bytes 1048576 | tf_op jit(solution)/shard_map/pack/pallas_call | solution.py:393
  5.4 0.6 %collective-permute-start.2 = (f32[3,32,128]{2,1,0:T(8,128)S(1)}, f32[3,32,128]{2,1,0:T(8,128)S(1)}, u32[]{:S(2)}, u32[]{:S(2)}) collective-permute-start(f32[3,32,128]{2,1,0:T(8,128)S(1)} %get-tuple-element.14.own_ref), channel_id=1, source_target_pairs={{1,2},{5,6},{2,1},{6,5},{0,4},{4,0},{3,7},{7,3},{9,10},{13,14},{10... | collective-permute-start | bytes 147464 | tf_op jit(solution)/shard_map/turn1_gz_1/ppermute | solution.py:31
  6.0 2.6 %collective-permute-start.1 = (f32[3,32,128]{2,1,0:T(8,128)S(1)}, f32[3,32,128]{2,1,0:T(8,128)S(1)}, u32[]{:S(2)}, u32[]{:S(2)}) collective-permute-start(f32[3,32,128]{2,1,0:T(8,128)S(1)} %get-tuple-element.14.own_ref), channel_id=1, source_target_pairs={{0,1},{4,5},{1,0},{5,4},{2,3},{6,7},{3,2},{7,6},{8,9},{12,13},{9,8... | collective-permute-start | bytes 147464 | tf_op jit(solution)/shard_map/turn1_gz_0/ppermute | solution.py:31
  8.7 0.0 collective-permute-start
  8.7 1.2 %collective-permute-done.refs_0_.refs_2_ = f32[8,8,1,128]{3,2,1,0:T(1,128)S(1)} collective-permute-done((f32[8,8,1,128]{3,2,1,0:T(1,128)S(1)}, f32[8,8,1,128]{3,2,1,0:T(1,128)S(1)}, u32[]{:S(2)}, u32[]{:S(2)}) %collective-permute-start) | collective-permute-done | bytes 32800 | tf_op jit(solution)/shard_map/turn1_gy_0/ppermute | solution.py:25
  9.9 0.0 collective-permute-done.2.refs_2_
  9.9 0.9 %collective-permute-done.1.refs_1_ = f32[3,32,128]{2,1,0:T(8,128)S(1)} collective-permute-done((f32[3,32,128]{2,1,0:T(8,128)S(1)}, f32[3,32,128]{2,1,0:T(8,128)S(1)}, u32[]{:S(2)}, u32[]{:S(2)}) %collective-permute-start.1) | collective-permute-done | bytes 49184 | tf_op jit(solution)/shard_map/turn1_gz_0/ppermute | solution.py:31
  10.8 0.7 %inner1.1 = (f32[8,8,32,128]{3,2,1,0:T(8,128)S(1)}, f32[2,32,128]{2,1,0:T(8,128)S(1)}) custom-call(f32[8,8,32,128]{3,2,1,0:T(8,128)S(1)} %copy-done, f32[8,32,128]{2,1,0:T(8,128)S(1)} %copy-done.2, f32[3,32,128]{2,1,0:T(8,128)S(1)} %get-tuple-element.14.own_ref, f32[8,8,1,128]{3,2,1,0:T(1,128)S(1)} %collective-permute-done.refs_0_.refs_2_, ...), custom_call_target="tpu_custom_call" | custom-call | flops 20000000 | bytes 1048576 | tf_op jit(solution)/shard_map/inner1/pallas_call | solution.py:393
  11.5 0.0 collective-permute-done.3.refs_0_
  11.5 0.0 collective-permute-done.4.refs_1_
  11.6 0.3 outer1.1
  11.9 3.0 %collective-permute-start.6 = (f32[9,32,128]{2,1,0:T(8,128)S(1)}, f32[9,32,128]{2,1,0:T(8,128)S(1)}, u32[]{:S(2)}, u32[]{:S(2)}) collective-permute-start(f32[9,32,128]{2,1,0:T(8,128)S(1)} %get-tuple-element.22), channel_id=1, source_target_pairs={{0,8},{4,12},{8,0},{12,4},{16,24},{20,28},{24,16},{28,20},{1,9},{5... | collective-permute-start | bytes 442376 | tf_op jit(solution)/shard_map/turn2_gx_0/ppermute | solution.py:31
  14.9 0.0 collective-permute-start.7
  14.9 0.5 %collective-permute-start.5 = (f32[9,8,1,128]{3,2,1,0:T(1,128)S(1)}, f32[9,8,1,128]{3,2,1,0:T(1,128)S(1)}, u32[]{:S(2)}, u32[]{:S(2)}) collective-permute-start(f32[9,8,1,128]{3,2,1,0:T(1,128)S(1)} %get-tuple-element.21), channel_id=1, source_target_pairs={{0,4},{4,0},{1,5},{5,1},{2,6},{6,2},{3,7},{7,3},{8,12},{12,8},{9,1... | collective-permute-start | bytes 110600 | tf_op jit(solution)/shard_map/turn2_gy_0/ppermute | solution.py:25
  15.4 1.5 %early.1.early_ref = f32[8,128]{1,0:T(8,128)S(1)} custom-call(f32[8,8,32,128]{3,2,1,0:T(8,128)S(1)} %copy-done, f32[8,8,32,128]{3,2,1,0:T(8,128)S(1)} %get-tuple-element.20.u_ref), custom_call_target="tpu_custom_call" | custom-call | flops 15000000 | bytes 1048576 | tf_op jit(solution)/shard_map/early/pallas_call | solution.py:393
  16.9 0.0 collective-permute-done.5.refs_0_.refs_2_
  16.9 1.3 %inner2.1.sums_ref = f32[2,36,8,128]{3,2,1,0:T(8,128)S(1)} custom-call(f32[8,8,32,128]{3,2,1,0:T(8,128)S(1)} %get-tuple-element.20.u_ref, f32[8,32,128]{2,1,0:T(8,128)S(1)} %copy-done.2, f32[2,32,128]{2,1,0:T(8,128)S(1)} %get-tuple-element.17.ends_ref, f32[9,8,1,128]{3,2,1,0:T(1,128)S(1)} %collective-permute-done.5.refs_0_.refs_2_), custom_call_target="tpu_custom_call" | custom-call | flops 15000000 | bytes 1048576 | tf_op jit(solution)/shard_map/inner2/pallas_call | solution.py:393
  18.2 0.0 copy-start.1
  18.2 1.4 %collective-permute-done.6.refs_0_ = f32[9,32,128]{2,1,0:T(8,128)S(1)} collective-permute-done((f32[9,32,128]{2,1,0:T(8,128)S(1)}, f32[9,32,128]{2,1,0:T(8,128)S(1)}, u32[]{:S(2)}, u32[]{:S(2)}) %collective-permute-start.6) | collective-permute-done | bytes 147488 | tf_op jit(solution)/shard_map/turn2_gx_0/ppermute | solution.py:31
  19.6 0.0 collective-permute-done.7.refs_1_
  19.6 0.8 %outer2.1 = f32[32,4,128]{2,1,0:T(4,128)S(1)} custom-call(f32[8,8,32,128]{3,2,1,0:T(8,128)S(1)} %get-tuple-element.20.u_ref, f32[8,32,128]{2,1,0:T(8,128)S(1)} %copy-done.2, f32[2,32,128]{2,1,0:T(8,128)S(1)} %get-tuple-element.17.ends_ref, f32[2,36,8,128]{3,2,1,0:T(8,128)S(1)} %inner2.1.sums_ref, f32[8,128]{1,0:T(8,128)S(1)} %early.1.early_ref, ...), custom_call_target="tpu_custom_call" | custom-call | flops 1000000 | bytes 1048576 | tf_op jit(solution)/shard_map/outer2/pallas_call | solution.py:393
  20.4 13.1 %all_to_all.5.parts_ref = f32[32,4,128]{2,1,0:T(4,128)S(1)} all-to-all(f32[32,4,128]{2,1,0:T(4,128)S(1)} %outer2.1), channel_id=1, replica_groups=mesh['gx'=4,'gy'=2,'gz'=4] {'gx','gy','gz'}, dimensions={0} | all-to-all | bytes 131072 | tf_op jit(solution)/shard_map/all_to_all | solution.py:472
  33.5 0.0 copy-done.1
  33.5 2.9 %finish.1 = (f32[8,8,32,128]{3,2,1,0:T(8,128)}, f32[1,8]{1,0:T(1,128)}) custom-call(f32[32,4,128]{2,1,0:T(4,128)S(1)} %all_to_all.5.parts_ref, f32[8,8,32,128]{3,2,1,0:T(8,128)S(1)} %copy-done.1, f32[8,8,32,128]{3,2,1,0:T(8,128)S(1)} %get-tuple-element.20.u_ref), custom_call_target="tpu_custom_call" | custom-call | flops 1000000 | bytes 1048576 | tf_op jit(solution)/shard_map/finish/pallas_call | solution.py:393
Async XLA Ops:
  0.6 1.2 %copy-start = (f32[8,8,32,128]{3,2,1,0:T(8,128)S(1)}, f32[8,8,32,128]{3,2,1,0:T(8,128)}, u32[]{:S(2)}) copy-start(f32[8,8,32,128]{3,2,1,0:T(8,128)} %b_ref.3) | copy-start | bytes 3145732
  1.9 3.1 %copy-start.2 = (f32[8,32,128]{2,1,0:T(8,128)S(1)}, f32[8,32,128]{2,1,0:T(8,128)}, u32[]{:S(2)}) copy-start(f32[8,32,128]{2,1,0:T(8,128)} %shift_ref.9) | copy-start | bytes 393220
  1.9 9.6 %collective-permute-start.3 = (f32[8,32,128]{2,1,0:T(8,128)S(1)}, f32[8,32,128]{2,1,0:T(8,128)S(1)}, u32[]{:S(2)}, u32[]{:S(2)}) collective-permute-start(f32[8,32,128]{2,1,0:T(8,128)S(1)} %get-tuple-element.18), channel_id=1, source_target_pairs={{0,8},{4,12},{8,0},{12,4},{16,24},{20,28},{24,16},{28,20},{1,9},{5... | collective-permute-start | bytes 393224 | tf_op jit(solution)/shard_map/turn1_gx_0/ppermute | solution.py:31
  5.0 6.6 %collective-permute-start.4 = (f32[8,32,128]{2,1,0:T(8,128)S(1)}, f32[8,32,128]{2,1,0:T(8,128)S(1)}, u32[]{:S(2)}, u32[]{:S(2)}) collective-permute-start(f32[8,32,128]{2,1,0:T(8,128)S(1)} %get-tuple-element.19), channel_id=1, source_target_pairs={{8,16},{12,20},{16,8},{20,12},{0,4},{4,0},{24,28},{28,24},{9,17},{... | collective-permute-start | bytes 393224 | tf_op jit(solution)/shard_map/turn1_gx_1/ppermute | solution.py:31
  5.4 4.4 %collective-permute-start.2 = (f32[3,32,128]{2,1,0:T(8,128)S(1)}, f32[3,32,128]{2,1,0:T(8,128)S(1)}, u32[]{:S(2)}, u32[]{:S(2)}) collective-permute-start(f32[3,32,128]{2,1,0:T(8,128)S(1)} %get-tuple-element.14.own_ref), channel_id=1, source_target_pairs={{1,2},{5,6},{2,1},{6,5},{0,4},{4,0},{3,7},{7,3},{9,10},{13,14},{10... | collective-permute-start | bytes 147464 | tf_op jit(solution)/shard_map/turn1_gz_1/ppermute | solution.py:31
  6.0 4.8 %collective-permute-start.1 = (f32[3,32,128]{2,1,0:T(8,128)S(1)}, f32[3,32,128]{2,1,0:T(8,128)S(1)}, u32[]{:S(2)}, u32[]{:S(2)}) collective-permute-start(f32[3,32,128]{2,1,0:T(8,128)S(1)} %get-tuple-element.14.own_ref), channel_id=1, source_target_pairs={{0,1},{4,5},{1,0},{5,4},{2,3},{6,7},{3,2},{7,6},{8,9},{12,13},{9,8... | collective-permute-start | bytes 147464 | tf_op jit(solution)/shard_map/turn1_gz_0/ppermute | solution.py:31
  8.7 1.2 %collective-permute-start = (f32[8,8,1,128]{3,2,1,0:T(1,128)S(1)}, f32[8,8,1,128]{3,2,1,0:T(1,128)S(1)}, u32[]{:S(2)}, u32[]{:S(2)}) collective-permute-start(f32[8,8,1,128]{3,2,1,0:T(1,128)S(1)} %get-tuple-element.15), channel_id=1, source_target_pairs={{0,4},{4,0},{1,5},{5,1},{2,6},{6,2},{3,7},{7,3},{8,12},{12,8},{9,1... | collective-permute-start | bytes 98312 | tf_op jit(solution)/shard_map/turn1_gy_0/ppermute | solution.py:25
  11.9 7.7 %collective-permute-start.6 = (f32[9,32,128]{2,1,0:T(8,128)S(1)}, f32[9,32,128]{2,1,0:T(8,128)S(1)}, u32[]{:S(2)}, u32[]{:S(2)}) collective-permute-start(f32[9,32,128]{2,1,0:T(8,128)S(1)} %get-tuple-element.22), channel_id=1, source_target_pairs={{0,8},{4,12},{8,0},{12,4},{16,24},{20,28},{24,16},{28,20},{1,9},{5... | collective-permute-start | bytes 442376 | tf_op jit(solution)/shard_map/turn2_gx_0/ppermute | solution.py:31
  14.9 4.7 %collective-permute-start.7 = (f32[9,32,128]{2,1,0:T(8,128)S(1)}, f32[9,32,128]{2,1,0:T(8,128)S(1)}, u32[]{:S(2)}, u32[]{:S(2)}) collective-permute-start(f32[9,32,128]{2,1,0:T(8,128)S(1)} %get-tuple-element.23), channel_id=1, source_target_pairs={{8,16},{12,20},{16,8},{20,12},{0,4},{4,0},{24,28},{28,24},{9,17},{... | collective-permute-start | bytes 442376 | tf_op jit(solution)/shard_map/turn2_gx_1/ppermute | solution.py:31
  14.9 2.0 %collective-permute-start.5 = (f32[9,8,1,128]{3,2,1,0:T(1,128)S(1)}, f32[9,8,1,128]{3,2,1,0:T(1,128)S(1)}, u32[]{:S(2)}, u32[]{:S(2)}) collective-permute-start(f32[9,8,1,128]{3,2,1,0:T(1,128)S(1)} %get-tuple-element.21), channel_id=1, source_target_pairs={{0,4},{4,0},{1,5},{5,1},{2,6},{6,2},{3,7},{7,3},{8,12},{12,8},{9,1... | collective-permute-start | bytes 110600 | tf_op jit(solution)/shard_map/turn2_gy_0/ppermute | solution.py:25
  18.2 15.3 %copy-start.1 = (f32[8,8,32,128]{3,2,1,0:T(8,128)S(1)}, f32[8,8,32,128]{3,2,1,0:T(8,128)}, u32[]{:S(2)}) copy-start(f32[8,8,32,128]{3,2,1,0:T(8,128)} %b_ref.3) | copy-start | bytes 3145732

commit v9 on v8

--- a/solution.py
+++ b/solution.py
@@ -44,14 +44,8 @@
 
 
 def cut_x_kernel(v_ref, *refs):
-    faces, sems = refs[:-1], refs[-1]
-    copies = [
-        pltpu.make_async_copy(v_ref.at[:, x_plane(k, v_ref.shape[1])], ref, sems.at[k]) for k, ref in enumerate(faces)
-    ]
-    for copy in copies:
-        copy.start()
-    for copy in copies:
-        copy.wait()
+    for k, ref in enumerate(refs):
+        ref[...] = v_ref[:, x_plane(k, v_ref.shape[1])].reshape(ref.shape)
 
 
 def write_y_faces(v_ref, y_refs):
@@ -127,6 +121,18 @@
     return lax.rem((lane + 1) // 2, nx)
 
 
+def fold_plane(ends, x, nx):
+    ny = ends.shape[0]
+    lane = lax.broadcasted_iota(jnp.int32, (8, LANES), 1)
+    mine = lane_x(lane, nx) == x
+    groups = [jnp.where(mine, ends[8 * r : 8 * r + 8], 0.0) for r in range(ny // 8)]
+    return sum(pltpu.roll(group, lax.rem(LANES + 2 * r - 2 * x, LANES), 1) for r, group in enumerate(groups))
+
+
+def unfold_plane(folded, x, ny):
+    return jnp.concatenate([shift_lanes(folded, 2 * x - 2 * r) for r in range(ny // 8)], axis=0)
+
+
 def operator_on_ends(nx, own, z_in):
     near, far, diagonal = (halo_ends(z_in, layer) for layer in range(3))
     ny = near.shape[0]
@@ -146,11 +152,16 @@
     low_y, high_y = pick("gy", y_in, lambda ref: ref[width, 0])
     beside = jnp.where(row == 0, low_y, 0.0) + jnp.where(row == ny - 1, high_y, 0.0)
     if x_in:
-        x, by = lane_x(lane, nx), 2 * (nx - 1)
-        low_x, high_x = pick("gx", x_in, lambda ref: ref[width])
-        beside += jnp.where(x == 0, pltpu.roll(low_x, LANES - by, 1), 0.0)
-        beside += jnp.where(x == nx - 1, pltpu.roll(high_x, by, 1), 0.0)
+        x = lane_x(lane, nx)
+        low_x, high_x = pick("gx", x_in, lambda ref: ref[ref.shape[0] - 1])
+        beside += jnp.where(x == 0, unfold_plane(low_x, 0, ny), 0.0)
+        beside += jnp.where(x == nx - 1, unfold_plane(high_x, nx - 1, ny), 0.0)
     return base - inside_grid(lane) * beside
+
+
+def face_of(ref, f, ny):
+    groups = ny // 8
+    return ref[pl.ds(f * groups, groups)].reshape(ny, LANES)
 
 
 def apply_operator(planes, v_ref, shift_ref, x_in, y_in, ends, out_ref):
@@ -158,7 +169,7 @@
     lane = lax.broadcasted_iota(jnp.int32, (ny, LANES), 1)
     row = lax.broadcasted_iota(jnp.int32, (ny, LANES), 0)
     def field(f, carry):
-        low_x, high_x = pick("gx", x_in, lambda ref: ref[f])
+        low_x, high_x = pick("gx", x_in, lambda ref: face_of(ref, f, ny))
         for x in planes:
             low_y, high_y = pick("gy", y_in, lambda ref: ref[f, x])
             v = v_ref[f, x]
@@ -204,8 +215,9 @@
     near = ends_ref[0]
     apply_operator(outer_planes(v_ref), v_ref, shift_ref, x_in, y_in, near, out_ref)
     for k, ref in enumerate(x_out):
-        ref[:width] = out_ref[:, x_plane(k, nx)]
-        ref[width] = near
+        plane, rows = x_plane(k, nx), width * ny // 8
+        ref[:rows] = out_ref[:, plane].reshape(rows, 8, LANES)
+        ref[rows] = fold_plane(near, plane, nx)
     write_y_faces(out_ref, [ref.at[:width] for ref in y_out])
     for k, ref in enumerate(y_out):
         high = jnp.logical_xor(parity("gy"), k == 0)
@@ -389,11 +401,11 @@
     lax.fori_loop(0, width // group, fields, 0)
 
 
-def call(kernel, out_shape, operands, scratch=(), flops=1_000_000, name=None, aliases=None, far=False):
+def call(kernel, out_shape, operands, scratch=(), flops=1_000_000, name=None, aliases=None):
     return pl.pallas_call(
         kernel,
         out_shape=out_shape,
-        in_specs=[pl.BlockSpec(memory_space=pl.ANY if far else pltpu.VMEM)] * len(operands),
+        in_specs=[pl.BlockSpec(memory_space=pltpu.VMEM)] * len(operands),
         out_specs=jax.tree.map(lambda _: pl.BlockSpec(memory_space=pltpu.VMEM), out_shape),
         scratch_shapes=list(scratch),
         input_output_aliases=aliases or {},
@@ -413,7 +425,7 @@
 
 def body(right_side, shift):
     width, nx, ny, nz = right_side.shape
-    assert width == 8 and nz == LANES and ny % 8 == 0 and nx > 2 and width * nx <= LANES // 2
+    assert width == 8 and nz == LANES and ny % 8 == 0 and nx > 2 and width * nx <= LANES // 2 and ny <= 8 * nx
     nx_r, ny_r, nz_r = rounds_of()
     devices = 1
     for axis in AXES:
@@ -423,8 +435,8 @@
     full = pltpu.VMEM(right_side.shape, F32)
     kernel = functools.partial
 
-    def x_faces(fields):
-        return [jax.ShapeDtypeStruct((fields, ny, nz), F32)] * nx_r
+    def x_faces(extra):
+        return [jax.ShapeDtypeStruct((width * ny // 8 + extra, 8, nz), F32)] * nx_r
 
     def y_faces(fields):
         return [jax.ShapeDtypeStruct((fields, nx, 1, nz), F32)] * ny_r
@@ -432,7 +444,7 @@
     def ends_of(layers):
         return jax.ShapeDtypeStruct((layers, ny, LANES), F32)
 
-    faces = call(cut_x_kernel, x_faces(width), [right_side], scratch=[pltpu.SemaphoreType.DMA((max(nx_r, 1),))], name="cut", far=True)
+    faces = call(cut_x_kernel, x_faces(0), [right_side], name="cut")
     halo_x = trade(1, "gx", faces)
     *faces, own = call(pack_kernel, [*y_faces(width), ends_of(3)], [right_side, shift], name="pack")
     halo_y = trade(1, "gy", faces)
@@ -446,7 +458,7 @@
     )
     u, *faces = call(
         kernel(outer_operator_kernel, nx_r, ny_r),
-        [block, *x_faces(width + 1), *y_faces(width + 1)],
+        [block, *x_faces(1), *y_faces(width + 1)],
         [right_side, shift, inner, ends, *halo_x, *halo_y],
         aliases={2: 0},
         name="outer1",

time: 36.6 us -> 36 us (0.984)
  no operation moved by 1% of the time
where the time goes in v9:
time: 36 us; the launch traced here: 35.9 us
  blocking collectives  12.8 us (36%)
  starting transfers between devices  9.75 us (27%)
  Pallas kernels  8.07 us (22%)
  waiting for transfers between devices  3.26 us (9%)
  local copies, waits for them, and re-layouts  1.23 us (3%)
  between operations  0.71 us (2%)
    all_to_all x1, blocking collectives, body(): parts = lax.all_to_all(copies, AXES, 0, 0, tiled=True)  12.8 us
    ppermute x6, starting transfers between devices, swap(): lax.ppermute(values, ('gx', 'gy') if axis == 'gx' else ('gy', 'gz'), joint)  9.24 us
    pallas_call x8, Pallas kernels, call(): pl.pallas_call(kernel, out_shape=out_shape, in_specs=[pl.BlockSpec(memory...  8.07 us
    ppermute x6, waiting for transfers between devices, swap(): lax.ppermute(values, ('gx', 'gy') if axis == 'gx' else ('gy', 'gz'), joint)  2.06 us
    unnamed x6, local copies, waits for them, and re-layouts  1.23 us
    ppermute x2, waiting for transfers between devices, swap(): return lax.ppermute(values, axis, pairs)  1.21 us
  transfers between devices with their start and end apart: 8, of which 3 were waited for; matrix products, arithmetic and copies ran while one was open for 0% of the time, Pallas kernels for 11%

profile of v9, /device:TPU:0, one launch (start us, length us, event | category | flops | bytes accessed | tf_op | source)
XLA Modules:
  0.0 35.9 jit_solution(6326547389081557315)
XLA Ops:
  0.6 0.0 copy-start
  0.6 1.2 %copy-done = f32[8,8,32,128]{3,2,1,0:T(8,128)S(1)} copy-done((f32[8,8,32,128]{3,2,1,0:T(8,128)S(1)}, f32[8,8,32,128]{3,2,1,0:T(8,128)}, u32[]{:S(2)}) %copy-start) | copy-done | bytes 1048600
  1.9 0.0 copy-start.2
  1.9 3.0 %collective-permute-start.3 = (f32[32,8,128]{2,1,0:T(8,128)S(1)}, f32[32,8,128]{2,1,0:T(8,128)S(1)}, u32[]{:S(2)}, u32[]{:S(2)}) collective-permute-start(f32[32,8,128]{2,1,0:T(8,128)S(1)} %get-tuple-element.18), channel_id=1, source_target_pairs={{0,8},{4,12},{8,0},{12,4},{16,24},{20,28},{24,16},{28,20},{1,9},{5... | collective-permute-start | bytes 393224 | tf_op jit(solution)/shard_map/turn1_gx_0/ppermute | solution.py:31
  4.9 0.0 collective-permute-start.4
  4.9 0.0 copy-done.2
  4.9 0.5 %pack.1 = (f32[8,8,1,128]{3,2,1,0:T(1,128)S(1)}, f32[3,32,128]{2,1,0:T(8,128)S(1)}) custom-call(f32[8,8,32,128]{3,2,1,0:T(8,128)S(1)} %copy-done, f32[8,32,128]{2,1,0:T(8,128)S(1)} %copy-done.2), custom_call_target="tpu_custom_call" | custom-call | flops 1000000 | bytes 1048576 | tf_op jit(solution)/shard_map/pack/pallas_call | solution.py:405
  5.4 0.6 %collective-permute-start.2 = (f32[3,32,128]{2,1,0:T(8,128)S(1)}, f32[3,32,128]{2,1,0:T(8,128)S(1)}, u32[]{:S(2)}, u32[]{:S(2)}) collective-permute-start(f32[3,32,128]{2,1,0:T(8,128)S(1)} %get-tuple-element.14.own_ref), channel_id=1, source_target_pairs={{1,2},{5,6},{2,1},{6,5},{0,4},{4,0},{3,7},{7,3},{9,10},{13,14},{10... | collective-permute-start | bytes 147464 | tf_op jit(solution)/shard_map/turn1_gz_1/ppermute | solution.py:31
  6.0 2.6 %collective-permute-start.1 = (f32[3,32,128]{2,1,0:T(8,128)S(1)}, f32[3,32,128]{2,1,0:T(8,128)S(1)}, u32[]{:S(2)}, u32[]{:S(2)}) collective-permute-start(f32[3,32,128]{2,1,0:T(8,128)S(1)} %get-tuple-element.14.own_ref), channel_id=1, source_target_pairs={{0,1},{4,5},{1,0},{5,4},{2,3},{6,7},{3,2},{7,6},{8,9},{12,13},{9,8... | collective-permute-start | bytes 147464 | tf_op jit(solution)/shard_map/turn1_gz_0/ppermute | solution.py:31
  8.6 0.0 collective-permute-start
  8.6 1.2 %collective-permute-done.refs_0_.refs_2_ = f32[8,8,1,128]{3,2,1,0:T(1,128)S(1)} collective-permute-done((f32[8,8,1,128]{3,2,1,0:T(1,128)S(1)}, f32[8,8,1,128]{3,2,1,0:T(1,128)S(1)}, u32[]{:S(2)}, u32[]{:S(2)}) %collective-permute-start) | collective-permute-done | bytes 32800 | tf_op jit(solution)/shard_map/turn1_gy_0/ppermute | solution.py:25
  9.8 0.0 collective-permute-done.2.refs_2_
  9.8 0.9 %collective-permute-done.1.refs_1_ = f32[3,32,128]{2,1,0:T(8,128)S(1)} collective-permute-done((f32[3,32,128]{2,1,0:T(8,128)S(1)}, f32[3,32,128]{2,1,0:T(8,128)S(1)}, u32[]{:S(2)}, u32[]{:S(2)}) %collective-permute-start.1) | collective-permute-done | bytes 49184 | tf_op jit(solution)/shard_map/turn1_gz_0/ppermute | solution.py:31
  10.7 0.7 %inner1.1 = (f32[8,8,32,128]{3,2,1,0:T(8,128)S(1)}, f32[2,32,128]{2,1,0:T(8,128)S(1)}) custom-call(f32[8,8,32,128]{3,2,1,0:T(8,128)S(1)} %copy-done, f32[8,32,128]{2,1,0:T(8,128)S(1)} %copy-done.2, f32[3,32,128]{2,1,0:T(8,128)S(1)} %get-tuple-element.14.own_ref, f32[8,8,1,128]{3,2,1,0:T(1,128)S(1)} %collective-permute-done.refs_0_.refs_2_, ...), custom_call_target="tpu_custom_call" | custom-call | flops 20000000 | bytes 1048576 | tf_op jit(solution)/shard_map/inner1/pallas_call | solution.py:405
  11.5 0.0 collective-permute-done.3.refs_0_
  11.5 0.0 collective-permute-done.4.refs_1_
  11.5 0.3 outer1.1
  11.8 3.0 %collective-permute-start.6 = (f32[33,8,128]{2,1,0:T(8,128)S(1)}, f32[33,8,128]{2,1,0:T(8,128)S(1)}, u32[]{:S(2)}, u32[]{:S(2)}) collective-permute-start(f32[33,8,128]{2,1,0:T(8,128)S(1)} %get-tuple-element.22), channel_id=1, source_target_pairs={{0,8},{4,12},{8,0},{12,4},{16,24},{20,28},{24,16},{28,20},{1,9},{5... | collective-permute-start | bytes 405512 | tf_op jit(solution)/shard_map/turn2_gx_0/ppermute | solution.py:31
  14.8 0.0 collective-permute-start.7
  14.8 0.5 %collective-permute-start.5 = (f32[9,8,1,128]{3,2,1,0:T(1,128)S(1)}, f32[9,8,1,128]{3,2,1,0:T(1,128)S(1)}, u32[]{:S(2)}, u32[]{:S(2)}) collective-permute-start(f32[9,8,1,128]{3,2,1,0:T(1,128)S(1)} %get-tuple-element.21), channel_id=1, source_target_pairs={{0,4},{4,0},{1,5},{5,1},{2,6},{6,2},{3,7},{7,3},{8,12},{12,8},{9,1... | collective-permute-start | bytes 110600 | tf_op jit(solution)/shard_map/turn2_gy_0/ppermute | solution.py:25
  15.3 1.5 %early.1.early_ref = f32[8,128]{1,0:T(8,128)S(1)} custom-call(f32[8,8,32,128]{3,2,1,0:T(8,128)S(1)} %copy-done, f32[8,8,32,128]{3,2,1,0:T(8,128)S(1)} %get-tuple-element.20.u_ref), custom_call_target="tpu_custom_call" | custom-call | flops 15000000 | bytes 1048576 | tf_op jit(solution)/shard_map/early/pallas_call | solution.py:405
  16.8 0.0 collective-permute-done.5.refs_0_.refs_2_
  16.8 1.3 %inner2.1.sums_ref = f32[2,36,8,128]{3,2,1,0:T(8,128)S(1)} custom-call(f32[8,8,32,128]{3,2,1,0:T(8,128)S(1)} %get-tuple-element.20.u_ref, f32[8,32,128]{2,1,0:T(8,128)S(1)} %copy-done.2, f32[2,32,128]{2,1,0:T(8,128)S(1)} %get-tuple-element.17.ends_ref, f32[9,8,1,128]{3,2,1,0:T(1,128)S(1)} %collective-permute-done.5.refs_0_.refs_2_), custom_call_target="tpu_custom_call" | custom-call | flops 15000000 | bytes 1048576 | tf_op jit(solution)/shard_map/inner2/pallas_call | solution.py:405
  18.1 0.0 copy-start.1
  18.1 1.1 %collective-permute-done.6.refs_0_ = f32[33,8,128]{2,1,0:T(8,128)S(1)} collective-permute-done((f32[33,8,128]{2,1,0:T(8,128)S(1)}, f32[33,8,128]{2,1,0:T(8,128)S(1)}, u32[]{:S(2)}, u32[]{:S(2)}) %collective-permute-start.6) | collective-permute-done | bytes 135200 | tf_op jit(solution)/shard_map/turn2_gx_0/ppermute | solution.py:31
  19.2 0.0 collective-permute-done.7.refs_1_
  19.2 0.8 %outer2.1 = f32[32,4,128]{2,1,0:T(4,128)S(1)} custom-call(f32[8,8,32,128]{3,2,1,0:T(8,128)S(1)} %get-tuple-element.20.u_ref, f32[8,32,128]{2,1,0:T(8,128)S(1)} %copy-done.2, f32[2,32,128]{2,1,0:T(8,128)S(1)} %get-tuple-element.17.ends_ref, f32[2,36,8,128]{3,2,1,0:T(8,128)S(1)} %inner2.1.sums_ref, f32[8,128]{1,0:T(8,128)S(1)} %early.1.early_ref, ...), custom_call_target="tpu_custom_call" | custom-call | flops 1000000 | bytes 1048576 | tf_op jit(solution)/shard_map/outer2/pallas_call | solution.py:405
  20.1 12.8 %all_to_all.5.parts_ref = f32[32,4,128]{2,1,0:T(4,128)S(1)} all-to-all(f32[32,4,128]{2,1,0:T(4,128)S(1)} %outer2.1), channel_id=1, replica_groups=mesh['gx'=4,'gy'=2,'gz'=4] {'gx','gy','gz'}, dimensions={0} | all-to-all | bytes 131072 | tf_op jit(solution)/shard_map/all_to_all | solution.py:484
  32.9 0.0 copy-done.1
  32.9 2.9 %finish.1 = (f32[8,8,32,128]{3,2,1,0:T(8,128)}, f32[1,8]{1,0:T(1,128)}) custom-call(f32[32,4,128]{2,1,0:T(4,128)S(1)} %all_to_all.5.parts_ref, f32[8,8,32,128]{3,2,1,0:T(8,128)S(1)} %copy-done.1, f32[8,8,32,128]{3,2,1,0:T(8,128)S(1)} %get-tuple-element.20.u_ref), custom_call_target="tpu_custom_call" | custom-call | flops 1000000 | bytes 1048576 | tf_op jit(solution)/shard_map/finish/pallas_call | solution.py:405
  (1 shorter events, 0.0 us)
Async XLA Ops:
  0.6 1.2 %copy-start = (f32[8,8,32,128]{3,2,1,0:T(8,128)S(1)}, f32[8,8,32,128]{3,2,1,0:T(8,128)}, u32[]{:S(2)}) copy-start(f32[8,8,32,128]{3,2,1,0:T(8,128)} %b_ref.3) | copy-start | bytes 3145732
  1.9 3.1 %copy-start.2 = (f32[8,32,128]{2,1,0:T(8,128)S(1)}, f32[8,32,128]{2,1,0:T(8,128)}, u32[]{:S(2)}) copy-start(f32[8,32,128]{2,1,0:T(8,128)} %shift_ref.9) | copy-start | bytes 393220
  1.9 9.6 %collective-permute-start.3 = (f32[32,8,128]{2,1,0:T(8,128)S(1)}, f32[32,8,128]{2,1,0:T(8,128)S(1)}, u32[]{:S(2)}, u32[]{:S(2)}) collective-permute-start(f32[32,8,128]{2,1,0:T(8,128)S(1)} %get-tuple-element.18), channel_id=1, source_target_pairs={{0,8},{4,12},{8,0},{12,4},{16,24},{20,28},{24,16},{28,20},{1,9},{5... | collective-permute-start | bytes 393224 | tf_op jit(solution)/shard_map/turn1_gx_0/ppermute | solution.py:31
  4.9 6.6 %collective-permute-start.4 = (f32[32,8,128]{2,1,0:T(8,128)S(1)}, f32[32,8,128]{2,1,0:T(8,128)S(1)}, u32[]{:S(2)}, u32[]{:S(2)}) collective-permute-start(f32[32,8,128]{2,1,0:T(8,128)S(1)} %get-tuple-element.19), channel_id=1, source_target_pairs={{8,16},{12,20},{16,8},{20,12},{0,4},{4,0},{24,28},{28,24},{9,17},{... | collective-permute-start | bytes 393224 | tf_op jit(solution)/shard_map/turn1_gx_1/ppermute | solution.py:31
  5.4 4.4 %collective-permute-start.2 = (f32[3,32,128]{2,1,0:T(8,128)S(1)}, f32[3,32,128]{2,1,0:T(8,128)S(1)}, u32[]{:S(2)}, u32[]{:S(2)}) collective-permute-start(f32[3,32,128]{2,1,0:T(8,128)S(1)} %get-tuple-element.14.own_ref), channel_id=1, source_target_pairs={{1,2},{5,6},{2,1},{6,5},{0,4},{4,0},{3,7},{7,3},{9,10},{13,14},{10... | collective-permute-start | bytes 147464 | tf_op jit(solution)/shard_map/turn1_gz_1/ppermute | solution.py:31
  6.0 4.8 %collective-permute-start.1 = (f32[3,32,128]{2,1,0:T(8,128)S(1)}, f32[3,32,128]{2,1,0:T(8,128)S(1)}, u32[]{:S(2)}, u32[]{:S(2)}) collective-permute-start(f32[3,32,128]{2,1,0:T(8,128)S(1)} %get-tuple-element.14.own_ref), channel_id=1, source_target_pairs={{0,1},{4,5},{1,0},{5,4},{2,3},{6,7},{3,2},{7,6},{8,9},{12,13},{9,8... | collective-permute-start | bytes 147464 | tf_op jit(solution)/shard_map/turn1_gz_0/ppermute | solution.py:31
  8.6 1.2 %collective-permute-start = (f32[8,8,1,128]{3,2,1,0:T(1,128)S(1)}, f32[8,8,1,128]{3,2,1,0:T(1,128)S(1)}, u32[]{:S(2)}, u32[]{:S(2)}) collective-permute-start(f32[8,8,1,128]{3,2,1,0:T(1,128)S(1)} %get-tuple-element.15), channel_id=1, source_target_pairs={{0,4},{4,0},{1,5},{5,1},{2,6},{6,2},{3,7},{7,3},{8,12},{12,8},{9,1... | collective-permute-start | bytes 98312 | tf_op jit(solution)/shard_map/turn1_gy_0/ppermute | solution.py:25
  11.8 7.4 %collective-permute-start.6 = (f32[33,8,128]{2,1,0:T(8,128)S(1)}, f32[33,8,128]{2,1,0:T(8,128)S(1)}, u32[]{:S(2)}, u32[]{:S(2)}) collective-permute-start(f32[33,8,128]{2,1,0:T(8,128)S(1)} %get-tuple-element.22), channel_id=1, source_target_pairs={{0,8},{4,12},{8,0},{12,4},{16,24},{20,28},{24,16},{28,20},{1,9},{5... | collective-permute-start | bytes 405512 | tf_op jit(solution)/shard_map/turn2_gx_0/ppermute | solution.py:31
  14.8 4.4 %collective-permute-start.7 = (f32[33,8,128]{2,1,0:T(8,128)S(1)}, f32[33,8,128]{2,1,0:T(8,128)S(1)}, u32[]{:S(2)}, u32[]{:S(2)}) collective-permute-start(f32[33,8,128]{2,1,0:T(8,128)S(1)} %get-tuple-element.23), channel_id=1, source_target_pairs={{8,16},{12,20},{16,8},{20,12},{0,4},{4,0},{24,28},{28,24},{9,17},{... | collective-permute-start | bytes 405512 | tf_op jit(solution)/shard_map/turn2_gx_1/ppermute | solution.py:31
  14.8 2.0 %collective-permute-start.5 = (f32[9,8,1,128]{3,2,1,0:T(1,128)S(1)}, f32[9,8,1,128]{3,2,1,0:T(1,128)S(1)}, u32[]{:S(2)}, u32[]{:S(2)}) collective-permute-start(f32[9,8,1,128]{3,2,1,0:T(1,128)S(1)} %get-tuple-element.21), channel_id=1, source_target_pairs={{0,4},{4,0},{1,5},{5,1},{2,6},{6,2},{3,7},{7,3},{8,12},{12,8},{9,1... | collective-permute-start | bytes 110600 | tf_op jit(solution)/shard_map/turn2_gy_0/ppermute | solution.py:25
  18.1 14.8 %copy-start.1 = (f32[8,8,32,128]{3,2,1,0:T(8,128)S(1)}, f32[8,8,32,128]{3,2,1,0:T(8,128)}, u32[]{:S(2)}) copy-start(f32[8,8,32,128]{3,2,1,0:T(8,128)} %b_ref.3) | copy-start | bytes 3145732

commit v10 on v9

--- a/solution.py
+++ b/solution.py
@@ -67,9 +67,10 @@
     return near, jnp.where(at(1) | at(-2), turned, far)
 
 
-def pack_kernel(v_ref, shift_ref, *refs):
+def pack_kernel(ny_r, v_ref, shift_ref, *refs):
     width, nx, ny, _ = v_ref.shape
-    write_y_faces(v_ref, refs[:-1])
+    y_refs, (near_ref, *z_refs) = refs[:ny_r], refs[ny_r:]
+    write_y_faces(v_ref, y_refs)
     lane = lax.broadcasted_iota(jnp.int32, (ny, LANES), 1)
     nothing = jnp.zeros((ny, LANES), F32)
 
@@ -82,13 +83,13 @@
     diagonal = nothing
     for x in range(nx):
         diagonal = packed_ends((6.0 - CENTRE) + shift_ref[x], x, lane, diagonal)
-    copies = 1
-    while copies < width:
-        diagonal = diagonal + pltpu.roll(diagonal, 2 * nx * copies, 1)
-        copies *= 2
-    refs[-1][0] = near
-    refs[-1][1] = far
-    refs[-1][2] = diagonal
+    groups = ny // 8
+    folded = sum(shift_lanes(diagonal[8 * r : 8 * r + 8], 2 * nx * r) for r in range(groups))
+    near_ref[...] = near
+    for k, ref in enumerate(z_refs):
+        first = jnp.where(jnp.logical_xor(parity("gz"), k == 0), 1, 0)
+        ref[:groups] = jnp.where(lax.rem(lane, 2) == first, near, far).reshape(groups, 8, LANES)
+        ref[groups] = folded
 
 
 def pick(axis, refs, load):
@@ -102,13 +103,23 @@
     return low, high
 
 
-def halo_ends(z_in, layer):
-    low, high = pick("gz", z_in, lambda ref: ref[layer])
-    if not z_in:
-        return None
+def by_side(low, high, by):
     lane = lax.broadcasted_iota(jnp.int32, low.shape, 1)
-    by = 2 if layer == 1 else 1
-    return jnp.where(lax.rem(lane, 2) == 0, pltpu.roll(low, by, 1), pltpu.roll(high, LANES - by, 1))
+    return jnp.where(lax.rem(lane, 2) == 0, shift_lanes(low, by), shift_lanes(high, -by))
+
+
+def halo_ends(z_in, nx, width):
+    groups = z_in[0].shape[0] - 1
+    low, high = pick("gz", z_in, lambda ref: ref[:groups].reshape(8 * groups, LANES))
+    folded = by_side(*pick("gz", z_in, lambda ref: ref[groups]), 1)
+    lane = lax.broadcasted_iota(jnp.int32, folded.shape, 1)
+    mine = lax.rem(lane + 1, LANES) < 2 * nx
+    rows = [jnp.where(mine, shift_lanes(folded, -2 * nx * r), 0.0) for r in range(groups)]
+    diagonal, copies = jnp.concatenate(rows, axis=0), 1
+    while copies < width:
+        diagonal = diagonal + shift_lanes(diagonal, 2 * nx * copies)
+        copies *= 2
+    return by_side(low, high, 1), by_side(low, high, 2), diagonal
 
 
 def inside_grid(lane):
@@ -133,8 +144,8 @@
     return jnp.concatenate([shift_lanes(folded, 2 * x - 2 * r) for r in range(ny // 8)], axis=0)
 
 
-def operator_on_ends(nx, own, z_in):
-    near, far, diagonal = (halo_ends(z_in, layer) for layer in range(3))
+def operator_on_ends(nx, width, own, z_in):
+    near, far, diagonal = halo_ends(z_in, nx, width)
     ny = near.shape[0]
     lane = lax.broadcasted_iota(jnp.int32, near.shape, 1)
     row = lax.broadcasted_iota(jnp.int32, near.shape, 0)
@@ -203,7 +214,7 @@
 
 def inner_operator_kernel(ny_r, nz_r, v_ref, shift_ref, own_ref, *refs):
     y_in, z_in, (out_ref, ends_ref) = split(refs, ny_r, nz_r)
-    near, base = operator_on_ends(v_ref.shape[1], own_ref[0], z_in)
+    near, base = operator_on_ends(v_ref.shape[1], v_ref.shape[0], own_ref[...], z_in)
     ends_ref[0] = near
     ends_ref[1] = base
     apply_operator(inner_planes(v_ref), v_ref, shift_ref, (), y_in, near, out_ref)
@@ -425,7 +436,7 @@
 
 def body(right_side, shift):
     width, nx, ny, nz = right_side.shape
-    assert width == 8 and nz == LANES and ny % 8 == 0 and nx > 2 and width * nx <= LANES // 2 and ny <= 8 * nx
+    assert width == 8 and nz == LANES and ny % 8 == 0 and nx > 2 and width * nx <= LANES // 2 and ny <= 8 * nx and ny * nx <= 4 * LANES
     nx_r, ny_r, nz_r = rounds_of()
     devices = 1
     for axis in AXES:
@@ -446,9 +457,14 @@
 
     faces = call(cut_x_kernel, x_faces(0), [right_side], name="cut")
     halo_x = trade(1, "gx", faces)
-    *faces, own = call(pack_kernel, [*y_faces(width), ends_of(3)], [right_side, shift], name="pack")
-    halo_y = trade(1, "gy", faces)
-    halo_z = trade(1, "gz", [own] * nz_r)
+    packed = call(
+        kernel(pack_kernel, ny_r),
+        [*y_faces(width), jax.ShapeDtypeStruct((ny, LANES), F32), *[jax.ShapeDtypeStruct((ny // 8 + 1, 8, LANES), F32)] * nz_r],
+        [right_side, shift],
+        name="pack",
+    )
+    halo_y, own = trade(1, "gy", packed[:ny_r]), packed[ny_r]
+    halo_z = trade(1, "gz", packed[ny_r + 1 :])
     inner, ends = call(
         kernel(inner_operator_kernel, ny_r, nz_r),
         [block, ends_of(2)],

time: 36 us -> 36 us (level)
  blocking collectives: 12.8 us -> 13.6 us
  starting transfers between devices: 9.75 us -> 9.21 us
    ppermute x2, waiting for transfers between devices: 1.21 us -> 0.01 us  [swap(): return lax.ppermute(values, axis, pairs)]
    ppermute x6, starting transfers between devices: 9.24 us -> 8.13 us  [swap(): lax.ppermute(values, ('gx', 'gy') if axis == 'gx' else ('gy', 'gz'), joint)]
    ppermute x6, waiting for transfers between devices: 2.06 us -> 3.08 us  [swap(): lax.ppermute(values, ('gx', 'gy') if axis == 'gx' else ('gy', 'gz'), joint)]
    all_to_all x1, blocking collectives: 12.8 us -> 13.6 us  [body(): parts = lax.all_to_all(copies, AXES, 0, 0, tiled=True)]
    ppermute x2, starting transfers between devices: 0.51 us -> 1.08 us  [swap(): return lax.ppermute(values, axis, pairs)]
  transfers between devices with their start and end apart: 8 -> 8, of which waited for: 3 -> 2; matrix products, arithmetic and copies ran while one was open for 0% -> 0% of each run, Pallas kernels for 11% -> 11%
where the time goes in v10:
time: 36 us; the launch traced here: 35.9 us
  blocking collectives  13.6 us (38%)
  starting transfers between devices  9.21 us (26%)
  Pallas kernels  8.02 us (22%)
  waiting for transfers between devices  3.09 us (9%)
  local copies, waits for them, and re-layouts  1.23 us (3%)
  between operations  0.71 us (2%)
    all_to_all x1, blocking collectives, body(): parts = lax.all_to_all(copies, AXES, 0, 0, tiled=True)  13.6 us
    ppermute x6, starting transfers between devices, swap(): lax.ppermute(values, ('gx', 'gy') if axis == 'gx' else ('gy', 'gz'), joint)  8.13 us
    pallas_call x8, Pallas kernels, call(): pl.pallas_call(kernel, out_shape=out_shape, in_specs=[pl.BlockSpec(memory...  8.02 us
    ppermute x6, waiting for transfers between devices, swap(): lax.ppermute(values, ('gx', 'gy') if axis == 'gx' else ('gy', 'gz'), joint)  3.08 us
    unnamed x6, local copies, waits for them, and re-layouts  1.23 us
    ppermute x2, starting transfers between devices, swap(): return lax.ppermute(values, axis, pairs)  1.08 us
  transfers between devices with their start and end apart: 8, of which 2 were waited for; matrix products, arithmetic and copies ran while one was open for 0% of the time, Pallas kernels for 11%

profile of v10, /device:TPU:0, one launch (start us, length us, event | category | flops | bytes accessed | tf_op | source)
XLA Modules:
  0.0 35.9 jit_solution(2303856781094285477)
XLA Ops:
  0.6 0.0 copy-start
  0.6 1.2 %copy-done = f32[8,8,32,128]{3,2,1,0:T(8,128)S(1)} copy-done((f32[8,8,32,128]{3,2,1,0:T(8,128)S(1)}, f32[8,8,32,128]{3,2,1,0:T(8,128)}, u32[]{:S(2)}) %copy-start) | copy-done | bytes 1048600
  1.9 0.0 copy-start.2
  1.9 3.0 %collective-permute-start.3 = (f32[32,8,128]{2,1,0:T(8,128)S(1)}, f32[32,8,128]{2,1,0:T(8,128)S(1)}, u32[]{:S(2)}, u32[]{:S(2)}) collective-permute-start(f32[32,8,128]{2,1,0:T(8,128)S(1)} %get-tuple-element.22), channel_id=1, source_target_pairs={{0,8},{4,12},{8,0},{12,4},{16,24},{20,28},{24,16},{28,20},{1,9},{5... | collective-permute-start | bytes 393224 | tf_op jit(solution)/shard_map/turn1_gx_0/ppermute | solution.py:31
  4.9 0.0 collective-permute-start.4
  4.9 0.0 copy-done.2
  4.9 0.4 %pack.1 = (f32[8,8,1,128]{3,2,1,0:T(1,128)S(1)}, f32[32,128]{1,0:T(8,128)S(1)}, f32[5,8,128]{2,1,0:T(8,128)S(1)}, f32[5,8,128]{2,1,0:T(8,128)S(1)}) custom-call(f32[8,8,32,128]{3,2,1,0:T(8,128)S(1)} %copy-done, f32[8,32,128]{2,1,0:T(8,128)S(1)} %copy-done.2), custom_call_target="tpu_custom_call" | custom-call | flops 1000000 | bytes 1048576 | tf_op jit(solution)/shard_map/pack/pallas_call | solution.py:416
  5.3 0.6 %collective-permute-start = (f32[8,8,1,128]{3,2,1,0:T(1,128)S(1)}, f32[8,8,1,128]{3,2,1,0:T(1,128)S(1)}, u32[]{:S(2)}, u32[]{:S(2)}) collective-permute-start(f32[8,8,1,128]{3,2,1,0:T(1,128)S(1)} %get-tuple-element.17), channel_id=1, source_target_pairs={{0,4},{4,0},{1,5},{5,1},{2,6},{6,2},{3,7},{7,3},{8,12},{12,8},{9,1... | collective-permute-start | bytes 98312 | tf_op jit(solution)/shard_map/turn1_gy_0/ppermute | solution.py:25
  5.9 1.6 %collective-permute-start.1 = (f32[5,8,128]{2,1,0:T(8,128)S(1)}, f32[5,8,128]{2,1,0:T(8,128)S(1)}, u32[]{:S(2)}, u32[]{:S(2)}) collective-permute-start(f32[5,8,128]{2,1,0:T(8,128)S(1)} %get-tuple-element.18), channel_id=1, source_target_pairs={{0,1},{4,5},{1,0},{5,4},{2,3},{6,7},{3,2},{7,6},{8,9},{12,13},{9,8... | collective-permute-start | bytes 61448 | tf_op jit(solution)/shard_map/turn1_gz_0/ppermute | solution.py:31
  7.5 0.0 collective-permute-start.2
  7.5 2.2 %collective-permute-done.1.refs_1_ = f32[5,8,128]{2,1,0:T(8,128)S(1)} collective-permute-done((f32[5,8,128]{2,1,0:T(8,128)S(1)}, f32[5,8,128]{2,1,0:T(8,128)S(1)}, u32[]{:S(2)}, u32[]{:S(2)}) %collective-permute-start.1) | collective-permute-done | bytes 20512 | tf_op jit(solution)/shard_map/turn1_gz_0/ppermute | solution.py:31
  9.7 0.0 collective-permute-done.2.refs_2_
  9.7 0.0 collective-permute-done.refs_0_.refs_2_
  9.7 0.7 %inner1.1 = (f32[8,8,32,128]{3,2,1,0:T(8,128)S(1)}, f32[2,32,128]{2,1,0:T(8,128)S(1)}) custom-call(f32[8,8,32,128]{3,2,1,0:T(8,128)S(1)} %copy-done, f32[8,32,128]{2,1,0:T(8,128)S(1)} %copy-done.2, f32[32,128]{1,0:T(8,128)S(1)} %get-tuple-element.16.own_ref, f32[8,8,1,128]{3,2,1,0:T(1,128)S(1)} %collective-permute-done.refs_0_.refs_2_, ...), custom_call_target="tpu_custom_call" | custom-call | flops 20000000 | bytes 1048576 | tf_op jit(solution)/shard_map/inner1/pallas_call | solution.py:416
  10.4 0.0 collective-permute-done.3.refs_0_
  10.5 0.0 collective-permute-done.4.refs_1_
  10.5 0.3 outer1.1
  10.8 3.5 %collective-permute-start.6 = (f32[33,8,128]{2,1,0:T(8,128)S(1)}, f32[33,8,128]{2,1,0:T(8,128)S(1)}, u32[]{:S(2)}, u32[]{:S(2)}) collective-permute-start(f32[33,8,128]{2,1,0:T(8,128)S(1)} %get-tuple-element.26), channel_id=1, source_target_pairs={{0,8},{4,12},{8,0},{12,4},{16,24},{20,28},{24,16},{28,20},{1,9},{5... | collective-permute-start | bytes 405512 | tf_op jit(solution)/shard_map/turn2_gx_0/ppermute | solution.py:31
  14.3 0.0 collective-permute-start.7
  14.3 0.5 %collective-permute-start.5 = (f32[9,8,1,128]{3,2,1,0:T(1,128)S(1)}, f32[9,8,1,128]{3,2,1,0:T(1,128)S(1)}, u32[]{:S(2)}, u32[]{:S(2)}) collective-permute-start(f32[9,8,1,128]{3,2,1,0:T(1,128)S(1)} %get-tuple-element.25), channel_id=1, source_target_pairs={{0,4},{4,0},{1,5},{5,1},{2,6},{6,2},{3,7},{7,3},{8,12},{12,8},{9,1... | collective-permute-start | bytes 110600 | tf_op jit(solution)/shard_map/turn2_gy_0/ppermute | solution.py:25
  14.8 1.5 %early.1.early_ref = f32[8,128]{1,0:T(8,128)S(1)} custom-call(f32[8,8,32,128]{3,2,1,0:T(8,128)S(1)} %copy-done, f32[8,8,32,128]{3,2,1,0:T(8,128)S(1)} %get-tuple-element.24.u_ref), custom_call_target="tpu_custom_call" | custom-call | flops 15000000 | bytes 1048576 | tf_op jit(solution)/shard_map/early/pallas_call | solution.py:416
  16.3 0.0 collective-permute-done.5.refs_0_.refs_2_
  16.3 1.3 %inner2.1.sums_ref = f32[2,36,8,128]{3,2,1,0:T(8,128)S(1)} custom-call(f32[8,8,32,128]{3,2,1,0:T(8,128)S(1)} %get-tuple-element.24.u_ref, f32[8,32,128]{2,1,0:T(8,128)S(1)} %copy-done.2, f32[2,32,128]{2,1,0:T(8,128)S(1)} %get-tuple-element.21.ends_ref, f32[9,8,1,128]{3,2,1,0:T(1,128)S(1)} %collective-permute-done.5.refs_0_.refs_2_), custom_call_target="tpu_custom_call" | custom-call | flops 15000000 | bytes 1048576 | tf_op jit(solution)/shard_map/inner2/pallas_call | solution.py:416
  17.6 0.0 copy-start.1
  17.6 0.9 %collective-permute-done.6.refs_0_ = f32[33,8,128]{2,1,0:T(8,128)S(1)} collective-permute-done((f32[33,8,128]{2,1,0:T(8,128)S(1)}, f32[33,8,128]{2,1,0:T(8,128)S(1)}, u32[]{:S(2)}, u32[]{:S(2)}) %collective-permute-start.6) | collective-permute-done | bytes 135200 | tf_op jit(solution)/shard_map/turn2_gx_0/ppermute | solution.py:31
  18.5 0.0 collective-permute-done.7.refs_1_
  18.5 0.8 %outer2.1 = f32[32,4,128]{2,1,0:T(4,128)S(1)} custom-call(f32[8,8,32,128]{3,2,1,0:T(8,128)S(1)} %get-tuple-element.24.u_ref, f32[8,32,128]{2,1,0:T(8,128)S(1)} %copy-done.2, f32[2,32,128]{2,1,0:T(8,128)S(1)} %get-tuple-element.21.ends_ref, f32[2,36,8,128]{3,2,1,0:T(8,128)S(1)} %inner2.1.sums_ref, f32[8,128]{1,0:T(8,128)S(1)} %early.1.early_ref, ...), custom_call_target="tpu_custom_call" | custom-call | flops 1000000 | bytes 1048576 | tf_op jit(solution)/shard_map/outer2/pallas_call | solution.py:416
  19.3 13.6 %all_to_all.5.parts_ref = f32[32,4,128]{2,1,0:T(4,128)S(1)} all-to-all(f32[32,4,128]{2,1,0:T(4,128)S(1)} %outer2.1), channel_id=1, replica_groups=mesh['gx'=4,'gy'=2,'gz'=4] {'gx','gy','gz'}, dimensions={0} | all-to-all | bytes 131072 | tf_op jit(solution)/shard_map/all_to_all | solution.py:500
  32.9 0.0 copy-done.1
  32.9 2.9 %finish.1 = (f32[8,8,32,128]{3,2,1,0:T(8,128)}, f32[1,8]{1,0:T(1,128)}) custom-call(f32[32,4,128]{2,1,0:T(4,128)S(1)} %all_to_all.5.parts_ref, f32[8,8,32,128]{3,2,1,0:T(8,128)S(1)} %copy-done.1, f32[8,8,32,128]{3,2,1,0:T(8,128)S(1)} %get-tuple-element.24.u_ref), custom_call_target="tpu_custom_call" | custom-call | flops 1000000 | bytes 1048576 | tf_op jit(solution)/shard_map/finish/pallas_call | solution.py:416
  (1 shorter events, 0.0 us)
Async XLA Ops:
  0.6 1.2 %copy-start = (f32[8,8,32,128]{3,2,1,0:T(8,128)S(1)}, f32[8,8,32,128]{3,2,1,0:T(8,128)}, u32[]{:S(2)}) copy-start(f32[8,8,32,128]{3,2,1,0:T(8,128)} %b_ref.3) | copy-start | bytes 3145732
  1.9 3.1 %copy-start.2 = (f32[8,32,128]{2,1,0:T(8,128)S(1)}, f32[8,32,128]{2,1,0:T(8,128)}, u32[]{:S(2)}) copy-start(f32[8,32,128]{2,1,0:T(8,128)} %shift_ref.9) | copy-start | bytes 393220
  1.9 8.6 %collective-permute-start.3 = (f32[32,8,128]{2,1,0:T(8,128)S(1)}, f32[32,8,128]{2,1,0:T(8,128)S(1)}, u32[]{:S(2)}, u32[]{:S(2)}) collective-permute-start(f32[32,8,128]{2,1,0:T(8,128)S(1)} %get-tuple-element.22), channel_id=1, source_target_pairs={{0,8},{4,12},{8,0},{12,4},{16,24},{20,28},{24,16},{28,20},{1,9},{5... | collective-permute-start | bytes 393224 | tf_op jit(solution)/shard_map/turn1_gx_0/ppermute | solution.py:31
  4.9 5.5 %collective-permute-start.4 = (f32[32,8,128]{2,1,0:T(8,128)S(1)}, f32[32,8,128]{2,1,0:T(8,128)S(1)}, u32[]{:S(2)}, u32[]{:S(2)}) collective-permute-start(f32[32,8,128]{2,1,0:T(8,128)S(1)} %get-tuple-element.23), channel_id=1, source_target_pairs={{8,16},{12,20},{16,8},{20,12},{0,4},{4,0},{24,28},{28,24},{9,17},{... | collective-permute-start | bytes 393224 | tf_op jit(solution)/shard_map/turn1_gx_1/ppermute | solution.py:31
  5.3 4.4 %collective-permute-start = (f32[8,8,1,128]{3,2,1,0:T(1,128)S(1)}, f32[8,8,1,128]{3,2,1,0:T(1,128)S(1)}, u32[]{:S(2)}, u32[]{:S(2)}) collective-permute-start(f32[8,8,1,128]{3,2,1,0:T(1,128)S(1)} %get-tuple-element.17), channel_id=1, source_target_pairs={{0,4},{4,0},{1,5},{5,1},{2,6},{6,2},{3,7},{7,3},{8,12},{12,8},{9,1... | collective-permute-start | bytes 98312 | tf_op jit(solution)/shard_map/turn1_gy_0/ppermute | solution.py:25
  5.9 3.8 %collective-permute-start.1 = (f32[5,8,128]{2,1,0:T(8,128)S(1)}, f32[5,8,128]{2,1,0:T(8,128)S(1)}, u32[]{:S(2)}, u32[]{:S(2)}) collective-permute-start(f32[5,8,128]{2,1,0:T(8,128)S(1)} %get-tuple-element.18), channel_id=1, source_target_pairs={{0,1},{4,5},{1,0},{5,4},{2,3},{6,7},{3,2},{7,6},{8,9},{12,13},{9,8... | collective-permute-start | bytes 61448 | tf_op jit(solution)/shard_map/turn1_gz_0/ppermute | solution.py:31
  7.5 2.2 %collective-permute-start.2 = (f32[5,8,128]{2,1,0:T(8,128)S(1)}, f32[5,8,128]{2,1,0:T(8,128)S(1)}, u32[]{:S(2)}, u32[]{:S(2)}) collective-permute-start(f32[5,8,128]{2,1,0:T(8,128)S(1)} %get-tuple-element.19), channel_id=1, source_target_pairs={{1,2},{5,6},{2,1},{6,5},{0,4},{4,0},{3,7},{7,3},{9,10},{13,14},{10... | collective-permute-start | bytes 61448 | tf_op jit(solution)/shard_map/turn1_gz_1/ppermute | solution.py:31
  10.8 7.7 %collective-permute-start.6 = (f32[33,8,128]{2,1,0:T(8,128)S(1)}, f32[33,8,128]{2,1,0:T(8,128)S(1)}, u32[]{:S(2)}, u32[]{:S(2)}) collective-permute-start(f32[33,8,128]{2,1,0:T(8,128)S(1)} %get-tuple-element.26), channel_id=1, source_target_pairs={{0,8},{4,12},{8,0},{12,4},{16,24},{20,28},{24,16},{28,20},{1,9},{5... | collective-permute-start | bytes 405512 | tf_op jit(solution)/shard_map/turn2_gx_0/ppermute | solution.py:31
  14.3 4.2 %collective-permute-start.7 = (f32[33,8,128]{2,1,0:T(8,128)S(1)}, f32[33,8,128]{2,1,0:T(8,128)S(1)}, u32[]{:S(2)}, u32[]{:S(2)}) collective-permute-start(f32[33,8,128]{2,1,0:T(8,128)S(1)} %get-tuple-element.27), channel_id=1, source_target_pairs={{8,16},{12,20},{16,8},{20,12},{0,4},{4,0},{24,28},{28,24},{9,17},{... | collective-permute-start | bytes 405512 | tf_op jit(solution)/shard_map/turn2_gx_1/ppermute | solution.py:31
  14.3 2.0 %collective-permute-start.5 = (f32[9,8,1,128]{3,2,1,0:T(1,128)S(1)}, f32[9,8,1,128]{3,2,1,0:T(1,128)S(1)}, u32[]{:S(2)}, u32[]{:S(2)}) collective-permute-start(f32[9,8,1,128]{3,2,1,0:T(1,128)S(1)} %get-tuple-element.25), channel_id=1, source_target_pairs={{0,4},{4,0},{1,5},{5,1},{2,6},{6,2},{3,7},{7,3},{8,12},{12,8},{9,1... | collective-permute-start | bytes 110600 | tf_op jit(solution)/shard_map/turn2_gy_0/ppermute | solution.py:25
  17.6 15.3 %copy-start.1 = (f32[8,8,32,128]{3,2,1,0:T(8,128)S(1)}, f32[8,8,32,128]{3,2,1,0:T(8,128)}, u32[]{:S(2)}) copy-start(f32[8,8,32,128]{3,2,1,0:T(8,128)} %b_ref.3) | copy-start | bytes 3145732

commit v11 on v10

--- a/solution.py
+++ b/solution.py
@@ -8,7 +8,7 @@
 from jax.sharding import PartitionSpec as P
 
 AXES = ("gx", "gy", "gz")
-CENTRE = 7.0
+CENTRE = 4.0
 LANES = 128
 F32 = jnp.float32
 

time: 36 us -> 36 us (level)
  no operation moved by 1% of the time
where the time goes in v11:
time: 36 us; the launch traced here: 35.9 us
  blocking collectives  13.6 us (38%)
  starting transfers between devices  9.21 us (26%)
  Pallas kernels  8.02 us (22%)
  waiting for transfers between devices  3.09 us (9%)
  local copies, waits for them, and re-layouts  1.23 us (3%)
  between operations  0.71 us (2%)
    all_to_all x1, blocking collectives, body(): parts = lax.all_to_all(copies, AXES, 0, 0, tiled=True)  13.6 us
    ppermute x6, starting transfers between devices, swap(): lax.ppermute(values, ('gx', 'gy') if axis == 'gx' else ('gy', 'gz'), joint)  8.13 us
    pallas_call x8, Pallas kernels, call(): pl.pallas_call(kernel, out_shape=out_shape, in_specs=[pl.BlockSpec(memory...  8.02 us
    ppermute x6, waiting for transfers between devices, swap(): lax.ppermute(values, ('gx', 'gy') if axis == 'gx' else ('gy', 'gz'), joint)  3.08 us
    unnamed x6, local copies, waits for them, and re-layouts  1.23 us
    ppermute x2, starting transfers between devices, swap(): return lax.ppermute(values, axis, pairs)  1.08 us
  transfers between devices with their start and end apart: 8, of which 2 were waited for; matrix products, arithmetic and copies ran while one was open for 0% of the time, Pallas kernels for 11%

profile of v11, /device:TPU:0, one launch (start us, length us, event | category | flops | bytes accessed | tf_op | source)
XLA Modules:
  0.0 35.9 jit_solution(15424137986453899382)
XLA Ops:
  0.6 0.0 copy-start
  0.6 1.2 %copy-done = f32[8,8,32,128]{3,2,1,0:T(8,128)S(1)} copy-done((f32[8,8,32,128]{3,2,1,0:T(8,128)S(1)}, f32[8,8,32,128]{3,2,1,0:T(8,128)}, u32[]{:S(2)}) %copy-start) | copy-done | bytes 1048600
  1.9 0.0 copy-start.2
  1.9 3.0 %collective-permute-start.3 = (f32[32,8,128]{2,1,0:T(8,128)S(1)}, f32[32,8,128]{2,1,0:T(8,128)S(1)}, u32[]{:S(2)}, u32[]{:S(2)}) collective-permute-start(f32[32,8,128]{2,1,0:T(8,128)S(1)} %get-tuple-element.22), channel_id=1, source_target_pairs={{0,8},{4,12},{8,0},{12,4},{16,24},{20,28},{24,16},{28,20},{1,9},{5... | collective-permute-start | bytes 393224 | tf_op jit(solution)/shard_map/turn1_gx_0/ppermute | solution.py:31
  4.9 0.0 collective-permute-start.4
  4.9 0.0 copy-done.2
  4.9 0.4 %pack.1 = (f32[8,8,1,128]{3,2,1,0:T(1,128)S(1)}, f32[32,128]{1,0:T(8,128)S(1)}, f32[5,8,128]{2,1,0:T(8,128)S(1)}, f32[5,8,128]{2,1,0:T(8,128)S(1)}) custom-call(f32[8,8,32,128]{3,2,1,0:T(8,128)S(1)} %copy-done, f32[8,32,128]{2,1,0:T(8,128)S(1)} %copy-done.2), custom_call_target="tpu_custom_call" | custom-call | flops 1000000 | bytes 1048576 | tf_op jit(solution)/shard_map/pack/pallas_call | solution.py:416
  5.3 0.6 %collective-permute-start = (f32[8,8,1,128]{3,2,1,0:T(1,128)S(1)}, f32[8,8,1,128]{3,2,1,0:T(1,128)S(1)}, u32[]{:S(2)}, u32[]{:S(2)}) collective-permute-start(f32[8,8,1,128]{3,2,1,0:T(1,128)S(1)} %get-tuple-element.17), channel_id=1, source_target_pairs={{0,4},{4,0},{1,5},{5,1},{2,6},{6,2},{3,7},{7,3},{8,12},{12,8},{9,1... | collective-permute-start | bytes 98312 | tf_op jit(solution)/shard_map/turn1_gy_0/ppermute | solution.py:25
  5.9 1.6 %collective-permute-start.1 = (f32[5,8,128]{2,1,0:T(8,128)S(1)}, f32[5,8,128]{2,1,0:T(8,128)S(1)}, u32[]{:S(2)}, u32[]{:S(2)}) collective-permute-start(f32[5,8,128]{2,1,0:T(8,128)S(1)} %get-tuple-element.18), channel_id=1, source_target_pairs={{0,1},{4,5},{1,0},{5,4},{2,3},{6,7},{3,2},{7,6},{8,9},{12,13},{9,8... | collective-permute-start | bytes 61448 | tf_op jit(solution)/shard_map/turn1_gz_0/ppermute | solution.py:31
  7.5 0.0 collective-permute-start.2
  7.5 2.2 %collective-permute-done.1.refs_1_ = f32[5,8,128]{2,1,0:T(8,128)S(1)} collective-permute-done((f32[5,8,128]{2,1,0:T(8,128)S(1)}, f32[5,8,128]{2,1,0:T(8,128)S(1)}, u32[]{:S(2)}, u32[]{:S(2)}) %collective-permute-start.1) | collective-permute-done | bytes 20512 | tf_op jit(solution)/shard_map/turn1_gz_0/ppermute | solution.py:31
  9.7 0.0 collective-permute-done.2.refs_2_
  9.7 0.0 collective-permute-done.refs_0_.refs_2_
  9.7 0.7 %inner1.1 = (f32[8,8,32,128]{3,2,1,0:T(8,128)S(1)}, f32[2,32,128]{2,1,0:T(8,128)S(1)}) custom-call(f32[8,8,32,128]{3,2,1,0:T(8,128)S(1)} %copy-done, f32[8,32,128]{2,1,0:T(8,128)S(1)} %copy-done.2, f32[32,128]{1,0:T(8,128)S(1)} %get-tuple-element.16.own_ref, f32[8,8,1,128]{3,2,1,0:T(1,128)S(1)} %collective-permute-done.refs_0_.refs_2_, ...), custom_call_target="tpu_custom_call" | custom-call | flops 20000000 | bytes 1048576 | tf_op jit(solution)/shard_map/inner1/pallas_call | solution.py:416
  10.4 0.0 collective-permute-done.3.refs_0_
  10.5 0.0 collective-permute-done.4.refs_1_
  10.5 0.3 outer1.1
  10.8 3.5 %collective-permute-start.6 = (f32[33,8,128]{2,1,0:T(8,128)S(1)}, f32[33,8,128]{2,1,0:T(8,128)S(1)}, u32[]{:S(2)}, u32[]{:S(2)}) collective-permute-start(f32[33,8,128]{2,1,0:T(8,128)S(1)} %get-tuple-element.26), channel_id=1, source_target_pairs={{0,8},{4,12},{8,0},{12,4},{16,24},{20,28},{24,16},{28,20},{1,9},{5... | collective-permute-start | bytes 405512 | tf_op jit(solution)/shard_map/turn2_gx_0/ppermute | solution.py:31
  14.3 0.0 collective-permute-start.7
  14.3 0.5 %collective-permute-start.5 = (f32[9,8,1,128]{3,2,1,0:T(1,128)S(1)}, f32[9,8,1,128]{3,2,1,0:T(1,128)S(1)}, u32[]{:S(2)}, u32[]{:S(2)}) collective-permute-start(f32[9,8,1,128]{3,2,1,0:T(1,128)S(1)} %get-tuple-element.25), channel_id=1, source_target_pairs={{0,4},{4,0},{1,5},{5,1},{2,6},{6,2},{3,7},{7,3},{8,12},{12,8},{9,1... | collective-permute-start | bytes 110600 | tf_op jit(solution)/shard_map/turn2_gy_0/ppermute | solution.py:25
  14.8 1.5 %early.1.early_ref = f32[8,128]{1,0:T(8,128)S(1)} custom-call(f32[8,8,32,128]{3,2,1,0:T(8,128)S(1)} %copy-done, f32[8,8,32,128]{3,2,1,0:T(8,128)S(1)} %get-tuple-element.24.u_ref), custom_call_target="tpu_custom_call" | custom-call | flops 15000000 | bytes 1048576 | tf_op jit(solution)/shard_map/early/pallas_call | solution.py:416
  16.3 0.0 collective-permute-done.5.refs_0_.refs_2_
  16.3 1.3 %inner2.1.sums_ref = f32[2,36,8,128]{3,2,1,0:T(8,128)S(1)} custom-call(f32[8,8,32,128]{3,2,1,0:T(8,128)S(1)} %get-tuple-element.24.u_ref, f32[8,32,128]{2,1,0:T(8,128)S(1)} %copy-done.2, f32[2,32,128]{2,1,0:T(8,128)S(1)} %get-tuple-element.21.ends_ref, f32[9,8,1,128]{3,2,1,0:T(1,128)S(1)} %collective-permute-done.5.refs_0_.refs_2_), custom_call_target="tpu_custom_call" | custom-call | flops 15000000 | bytes 1048576 | tf_op jit(solution)/shard_map/inner2/pallas_call | solution.py:416
  17.6 0.0 copy-start.1
  17.6 0.9 %collective-permute-done.6.refs_0_ = f32[33,8,128]{2,1,0:T(8,128)S(1)} collective-permute-done((f32[33,8,128]{2,1,0:T(8,128)S(1)}, f32[33,8,128]{2,1,0:T(8,128)S(1)}, u32[]{:S(2)}, u32[]{:S(2)}) %collective-permute-start.6) | collective-permute-done | bytes 135200 | tf_op jit(solution)/shard_map/turn2_gx_0/ppermute | solution.py:31
  18.5 0.0 collective-permute-done.7.refs_1_
  18.5 0.8 %outer2.1 = f32[32,4,128]{2,1,0:T(4,128)S(1)} custom-call(f32[8,8,32,128]{3,2,1,0:T(8,128)S(1)} %get-tuple-element.24.u_ref, f32[8,32,128]{2,1,0:T(8,128)S(1)} %copy-done.2, f32[2,32,128]{2,1,0:T(8,128)S(1)} %get-tuple-element.21.ends_ref, f32[2,36,8,128]{3,2,1,0:T(8,128)S(1)} %inner2.1.sums_ref, f32[8,128]{1,0:T(8,128)S(1)} %early.1.early_ref, ...), custom_call_target="tpu_custom_call" | custom-call | flops 1000000 | bytes 1048576 | tf_op jit(solution)/shard_map/outer2/pallas_call | solution.py:416
  19.3 13.6 %all_to_all.5.parts_ref = f32[32,4,128]{2,1,0:T(4,128)S(1)} all-to-all(f32[32,4,128]{2,1,0:T(4,128)S(1)} %outer2.1), channel_id=1, replica_groups=mesh['gx'=4,'gy'=2,'gz'=4] {'gx','gy','gz'}, dimensions={0} | all-to-all | bytes 131072 | tf_op jit(solution)/shard_map/all_to_all | solution.py:500
  32.9 0.0 copy-done.1
  32.9 2.9 %finish.1 = (f32[8,8,32,128]{3,2,1,0:T(8,128)}, f32[1,8]{1,0:T(1,128)}) custom-call(f32[32,4,128]{2,1,0:T(4,128)S(1)} %all_to_all.5.parts_ref, f32[8,8,32,128]{3,2,1,0:T(8,128)S(1)} %copy-done.1, f32[8,8,32,128]{3,2,1,0:T(8,128)S(1)} %get-tuple-element.24.u_ref), custom_call_target="tpu_custom_call" | custom-call | flops 1000000 | bytes 1048576 | tf_op jit(solution)/shard_map/finish/pallas_call | solution.py:416
  (1 shorter events, 0.0 us)
Async XLA Ops:
  0.6 1.2 %copy-start = (f32[8,8,32,128]{3,2,1,0:T(8,128)S(1)}, f32[8,8,32,128]{3,2,1,0:T(8,128)}, u32[]{:S(2)}) copy-start(f32[8,8,32,128]{3,2,1,0:T(8,128)} %b_ref.3) | copy-start | bytes 3145732
  1.9 3.1 %copy-start.2 = (f32[8,32,128]{2,1,0:T(8,128)S(1)}, f32[8,32,128]{2,1,0:T(8,128)}, u32[]{:S(2)}) copy-start(f32[8,32,128]{2,1,0:T(8,128)} %shift_ref.9) | copy-start | bytes 393220
  1.9 8.6 %collective-permute-start.3 = (f32[32,8,128]{2,1,0:T(8,128)S(1)}, f32[32,8,128]{2,1,0:T(8,128)S(1)}, u32[]{:S(2)}, u32[]{:S(2)}) collective-permute-start(f32[32,8,128]{2,1,0:T(8,128)S(1)} %get-tuple-element.22), channel_id=1, source_target_pairs={{0,8},{4,12},{8,0},{12,4},{16,24},{20,28},{24,16},{28,20},{1,9},{5... | collective-permute-start | bytes 393224 | tf_op jit(solution)/shard_map/turn1_gx_0/ppermute | solution.py:31
  4.9 5.5 %collective-permute-start.4 = (f32[32,8,128]{2,1,0:T(8,128)S(1)}, f32[32,8,128]{2,1,0:T(8,128)S(1)}, u32[]{:S(2)}, u32[]{:S(2)}) collective-permute-start(f32[32,8,128]{2,1,0:T(8,128)S(1)} %get-tuple-element.23), channel_id=1, source_target_pairs={{8,16},{12,20},{16,8},{20,12},{0,4},{4,0},{24,28},{28,24},{9,17},{... | collective-permute-start | bytes 393224 | tf_op jit(solution)/shard_map/turn1_gx_1/ppermute | solution.py:31
  5.3 4.4 %collective-permute-start = (f32[8,8,1,128]{3,2,1,0:T(1,128)S(1)}, f32[8,8,1,128]{3,2,1,0:T(1,128)S(1)}, u32[]{:S(2)}, u32[]{:S(2)}) collective-permute-start(f32[8,8,1,128]{3,2,1,0:T(1,128)S(1)} %get-tuple-element.17), channel_id=1, source_target_pairs={{0,4},{4,0},{1,5},{5,1},{2,6},{6,2},{3,7},{7,3},{8,12},{12,8},{9,1... | collective-permute-start | bytes 98312 | tf_op jit(solution)/shard_map/turn1_gy_0/ppermute | solution.py:25
  5.9 3.8 %collective-permute-start.1 = (f32[5,8,128]{2,1,0:T(8,128)S(1)}, f32[5,8,128]{2,1,0:T(8,128)S(1)}, u32[]{:S(2)}, u32[]{:S(2)}) collective-permute-start(f32[5,8,128]{2,1,0:T(8,128)S(1)} %get-tuple-element.18), channel_id=1, source_target_pairs={{0,1},{4,5},{1,0},{5,4},{2,3},{6,7},{3,2},{7,6},{8,9},{12,13},{9,8... | collective-permute-start | bytes 61448 | tf_op jit(solution)/shard_map/turn1_gz_0/ppermute | solution.py:31
  7.5 2.2 %collective-permute-start.2 = (f32[5,8,128]{2,1,0:T(8,128)S(1)}, f32[5,8,128]{2,1,0:T(8,128)S(1)}, u32[]{:S(2)}, u32[]{:S(2)}) collective-permute-start(f32[5,8,128]{2,1,0:T(8,128)S(1)} %get-tuple-element.19), channel_id=1, source_target_pairs={{1,2},{5,6},{2,1},{6,5},{0,4},{4,0},{3,7},{7,3},{9,10},{13,14},{10... | collective-permute-start | bytes 61448 | tf_op jit(solution)/shard_map/turn1_gz_1/ppermute | solution.py:31
  10.8 7.7 %collective-permute-start.6 = (f32[33,8,128]{2,1,0:T(8,128)S(1)}, f32[33,8,128]{2,1,0:T(8,128)S(1)}, u32[]{:S(2)}, u32[]{:S(2)}) collective-permute-start(f32[33,8,128]{2,1,0:T(8,128)S(1)} %get-tuple-element.26), channel_id=1, source_target_pairs={{0,8},{4,12},{8,0},{12,4},{16,24},{20,28},{24,16},{28,20},{1,9},{5... | collective-permute-start | bytes 405512 | tf_op jit(solution)/shard_map/turn2_gx_0/ppermute | solution.py:31
  14.3 4.2 %collective-permute-start.7 = (f32[33,8,128]{2,1,0:T(8,128)S(1)}, f32[33,8,128]{2,1,0:T(8,128)S(1)}, u32[]{:S(2)}, u32[]{:S(2)}) collective-permute-start(f32[33,8,128]{2,1,0:T(8,128)S(1)} %get-tuple-element.27), channel_id=1, source_target_pairs={{8,16},{12,20},{16,8},{20,12},{0,4},{4,0},{24,28},{28,24},{9,17},{... | collective-permute-start | bytes 405512 | tf_op jit(solution)/shard_map/turn2_gx_1/ppermute | solution.py:31
  14.3 2.0 %collective-permute-start.5 = (f32[9,8,1,128]{3,2,1,0:T(1,128)S(1)}, f32[9,8,1,128]{3,2,1,0:T(1,128)S(1)}, u32[]{:S(2)}, u32[]{:S(2)}) collective-permute-start(f32[9,8,1,128]{3,2,1,0:T(1,128)S(1)} %get-tuple-element.25), channel_id=1, source_target_pairs={{0,4},{4,0},{1,5},{5,1},{2,6},{6,2},{3,7},{7,3},{8,12},{12,8},{9,1... | collective-permute-start | bytes 110600 | tf_op jit(solution)/shard_map/turn2_gy_0/ppermute | solution.py:25
  17.6 15.3 %copy-start.1 = (f32[8,8,32,128]{3,2,1,0:T(8,128)S(1)}, f32[8,8,32,128]{3,2,1,0:T(8,128)}, u32[]{:S(2)}) copy-start(f32[8,8,32,128]{3,2,1,0:T(8,128)} %b_ref.3) | copy-start | bytes 3145732

commit v12 on v11

--- a/solution.py
+++ b/solution.py
@@ -254,7 +254,7 @@
                 sums[k] = sums[k] + a[i] * b[j]
         return tuple(sums)
 
-    return lax.fori_loop(0, -((first - last) // step), plane, tuple(sums))
+    return lax.fori_loop(0, -((first - last) // step), plane, tuple(sums), unroll=2)
 
 
 def no_sums(width):

time: 36 us -> 35.9 us (level)
  transfers between devices with their start and end apart: 8 -> 8, of which waited for: 2 -> 2; matrix products, arithmetic and copies ran while one was open for 0% -> 0% of each run, Pallas kernels for 11% -> 10%
where the time goes in v12:
time: 35.9 us; the launch traced here: 35.7 us
  blocking collectives  13.6 us (38%)
  starting transfers between devices  9.21 us (26%)
  Pallas kernels  7.68 us (21%)
  waiting for transfers between devices  3.27 us (9%)
  local copies, waits for them, and re-layouts  1.23 us (3%)
  between operations  0.71 us (2%)
    all_to_all x1, blocking collectives, body(): parts = lax.all_to_all(copies, AXES, 0, 0, tiled=True)  13.6 us
    ppermute x6, starting transfers between devices, swap(): lax.ppermute(values, ('gx', 'gy') if axis == 'gx' else ('gy', 'gz'), joint)  8.13 us
    pallas_call x8, Pallas kernels, call(): pl.pallas_call(kernel, out_shape=out_shape, in_specs=[pl.BlockSpec(memory...  7.68 us
    ppermute x6, waiting for transfers between devices, swap(): lax.ppermute(values, ('gx', 'gy') if axis == 'gx' else ('gy', 'gz'), joint)  3.27 us
    unnamed x6, local copies, waits for them, and re-layouts  1.23 us
    ppermute x2, starting transfers between devices, swap(): return lax.ppermute(values, axis, pairs)  1.08 us
  transfers between devices with their start and end apart: 8, of which 2 were waited for; matrix products, arithmetic and copies ran while one was open for 0% of the time, Pallas kernels for 10%

profile of v12, /device:TPU:0, one launch (start us, length us, event | category | flops | bytes accessed | tf_op | source)
XLA Modules:
  0.0 35.7 jit_solution(5615355621467704093)
XLA Ops:
  0.6 0.0 copy-start
  0.6 1.2 %copy-done = f32[8,8,32,128]{3,2,1,0:T(8,128)S(1)} copy-done((f32[8,8,32,128]{3,2,1,0:T(8,128)S(1)}, f32[8,8,32,128]{3,2,1,0:T(8,128)}, u32[]{:S(2)}) %copy-start) | copy-done | bytes 1048600
  1.9 0.0 copy-start.2
  1.9 3.0 %collective-permute-start.3 = (f32[32,8,128]{2,1,0:T(8,128)S(1)}, f32[32,8,128]{2,1,0:T(8,128)S(1)}, u32[]{:S(2)}, u32[]{:S(2)}) collective-permute-start(f32[32,8,128]{2,1,0:T(8,128)S(1)} %get-tuple-element.22), channel_id=1, source_target_pairs={{0,8},{4,12},{8,0},{12,4},{16,24},{20,28},{24,16},{28,20},{1,9},{5... | collective-permute-start | bytes 393224 | tf_op jit(solution)/shard_map/turn1_gx_0/ppermute | solution.py:31
  4.9 0.0 collective-permute-start.4
  4.9 0.0 copy-done.2
  4.9 0.4 %pack.1 = (f32[8,8,1,128]{3,2,1,0:T(1,128)S(1)}, f32[32,128]{1,0:T(8,128)S(1)}, f32[5,8,128]{2,1,0:T(8,128)S(1)}, f32[5,8,128]{2,1,0:T(8,128)S(1)}) custom-call(f32[8,8,32,128]{3,2,1,0:T(8,128)S(1)} %copy-done, f32[8,32,128]{2,1,0:T(8,128)S(1)} %copy-done.2), custom_call_target="tpu_custom_call" | custom-call | flops 1000000 | bytes 1048576 | tf_op jit(solution)/shard_map/pack/pallas_call | solution.py:416
  5.3 0.6 %collective-permute-start = (f32[8,8,1,128]{3,2,1,0:T(1,128)S(1)}, f32[8,8,1,128]{3,2,1,0:T(1,128)S(1)}, u32[]{:S(2)}, u32[]{:S(2)}) collective-permute-start(f32[8,8,1,128]{3,2,1,0:T(1,128)S(1)} %get-tuple-element.17), channel_id=1, source_target_pairs={{0,4},{4,0},{1,5},{5,1},{2,6},{6,2},{3,7},{7,3},{8,12},{12,8},{9,1... | collective-permute-start | bytes 98312 | tf_op jit(solution)/shard_map/turn1_gy_0/ppermute | solution.py:25
  5.9 1.6 %collective-permute-start.1 = (f32[5,8,128]{2,1,0:T(8,128)S(1)}, f32[5,8,128]{2,1,0:T(8,128)S(1)}, u32[]{:S(2)}, u32[]{:S(2)}) collective-permute-start(f32[5,8,128]{2,1,0:T(8,128)S(1)} %get-tuple-element.18), channel_id=1, source_target_pairs={{0,1},{4,5},{1,0},{5,4},{2,3},{6,7},{3,2},{7,6},{8,9},{12,13},{9,8... | collective-permute-start | bytes 61448 | tf_op jit(solution)/shard_map/turn1_gz_0/ppermute | solution.py:31
  7.5 0.0 collective-permute-start.2
  7.5 2.2 %collective-permute-done.1.refs_1_ = f32[5,8,128]{2,1,0:T(8,128)S(1)} collective-permute-done((f32[5,8,128]{2,1,0:T(8,128)S(1)}, f32[5,8,128]{2,1,0:T(8,128)S(1)}, u32[]{:S(2)}, u32[]{:S(2)}) %collective-permute-start.1) | collective-permute-done | bytes 20512 | tf_op jit(solution)/shard_map/turn1_gz_0/ppermute | solution.py:31
  9.7 0.0 collective-permute-done.2.refs_2_
  9.7 0.0 collective-permute-done.refs_0_.refs_2_
  9.7 0.7 %inner1.1 = (f32[8,8,32,128]{3,2,1,0:T(8,128)S(1)}, f32[2,32,128]{2,1,0:T(8,128)S(1)}) custom-call(f32[8,8,32,128]{3,2,1,0:T(8,128)S(1)} %copy-done, f32[8,32,128]{2,1,0:T(8,128)S(1)} %copy-done.2, f32[32,128]{1,0:T(8,128)S(1)} %get-tuple-element.16.own_ref, f32[8,8,1,128]{3,2,1,0:T(1,128)S(1)} %collective-permute-done.refs_0_.refs_2_, ...), custom_call_target="tpu_custom_call" | custom-call | flops 20000000 | bytes 1048576 | tf_op jit(solution)/shard_map/inner1/pallas_call | solution.py:416
  10.4 0.0 collective-permute-done.3.refs_0_
  10.5 0.0 collective-permute-done.4.refs_1_
  10.5 0.3 outer1.1
  10.8 3.5 %collective-permute-start.6 = (f32[33,8,128]{2,1,0:T(8,128)S(1)}, f32[33,8,128]{2,1,0:T(8,128)S(1)}, u32[]{:S(2)}, u32[]{:S(2)}) collective-permute-start(f32[33,8,128]{2,1,0:T(8,128)S(1)} %get-tuple-element.26), channel_id=1, source_target_pairs={{0,8},{4,12},{8,0},{12,4},{16,24},{20,28},{24,16},{28,20},{1,9},{5... | collective-permute-start | bytes 405512 | tf_op jit(solution)/shard_map/turn2_gx_0/ppermute | solution.py:31
  14.3 0.0 collective-permute-start.7
  14.3 0.5 %collective-permute-start.5 = (f32[9,8,1,128]{3,2,1,0:T(1,128)S(1)}, f32[9,8,1,128]{3,2,1,0:T(1,128)S(1)}, u32[]{:S(2)}, u32[]{:S(2)}) collective-permute-start(f32[9,8,1,128]{3,2,1,0:T(1,128)S(1)} %get-tuple-element.25), channel_id=1, source_target_pairs={{0,4},{4,0},{1,5},{5,1},{2,6},{6,2},{3,7},{7,3},{8,12},{12,8},{9,1... | collective-permute-start | bytes 110600 | tf_op jit(solution)/shard_map/turn2_gy_0/ppermute | solution.py:25
  14.8 1.4 %early.1.early_ref = f32[8,128]{1,0:T(8,128)S(1)} custom-call(f32[8,8,32,128]{3,2,1,0:T(8,128)S(1)} %copy-done, f32[8,8,32,128]{3,2,1,0:T(8,128)S(1)} %get-tuple-element.24.u_ref), custom_call_target="tpu_custom_call" | custom-call | flops 15000000 | bytes 1048576 | tf_op jit(solution)/shard_map/early/pallas_call | solution.py:416
  16.2 0.0 collective-permute-done.5.refs_0_.refs_2_
  16.2 1.2 %inner2.1.sums_ref = f32[2,36,8,128]{3,2,1,0:T(8,128)S(1)} custom-call(f32[8,8,32,128]{3,2,1,0:T(8,128)S(1)} %get-tuple-element.24.u_ref, f32[8,32,128]{2,1,0:T(8,128)S(1)} %copy-done.2, f32[2,32,128]{2,1,0:T(8,128)S(1)} %get-tuple-element.21.ends_ref, f32[9,8,1,128]{3,2,1,0:T(1,128)S(1)} %collective-permute-done.5.refs_0_.refs_2_), custom_call_target="tpu_custom_call" | custom-call | flops 15000000 | bytes 1048576 | tf_op jit(solution)/shard_map/inner2/pallas_call | solution.py:416
  17.4 0.0 copy-start.1
  17.4 1.1 %collective-permute-done.6.refs_0_ = f32[33,8,128]{2,1,0:T(8,128)S(1)} collective-permute-done((f32[33,8,128]{2,1,0:T(8,128)S(1)}, f32[33,8,128]{2,1,0:T(8,128)S(1)}, u32[]{:S(2)}, u32[]{:S(2)}) %collective-permute-start.6) | collective-permute-done | bytes 135200 | tf_op jit(solution)/shard_map/turn2_gx_0/ppermute | solution.py:31
  18.5 0.0 collective-permute-done.7.refs_1_
  18.5 0.7 %outer2.1 = f32[32,4,128]{2,1,0:T(4,128)S(1)} custom-call(f32[8,8,32,128]{3,2,1,0:T(8,128)S(1)} %get-tuple-element.24.u_ref, f32[8,32,128]{2,1,0:T(8,128)S(1)} %copy-done.2, f32[2,32,128]{2,1,0:T(8,128)S(1)} %get-tuple-element.21.ends_ref, f32[2,36,8,128]{3,2,1,0:T(8,128)S(1)} %inner2.1.sums_ref, f32[8,128]{1,0:T(8,128)S(1)} %early.1.early_ref, ...), custom_call_target="tpu_custom_call" | custom-call | flops 1000000 | bytes 1048576 | tf_op jit(solution)/shard_map/outer2/pallas_call | solution.py:416
  19.1 13.6 %all_to_all.5.parts_ref = f32[32,4,128]{2,1,0:T(4,128)S(1)} all-to-all(f32[32,4,128]{2,1,0:T(4,128)S(1)} %outer2.1), channel_id=1, replica_groups=mesh['gx'=4,'gy'=2,'gz'=4] {'gx','gy','gz'}, dimensions={0} | all-to-all | bytes 131072 | tf_op jit(solution)/shard_map/all_to_all | solution.py:500
  32.8 0.0 copy-done.1
  32.8 2.9 %finish.1 = (f32[8,8,32,128]{3,2,1,0:T(8,128)}, f32[1,8]{1,0:T(1,128)}) custom-call(f32[32,4,128]{2,1,0:T(4,128)S(1)} %all_to_all.5.parts_ref, f32[8,8,32,128]{3,2,1,0:T(8,128)S(1)} %copy-done.1, f32[8,8,32,128]{3,2,1,0:T(8,128)S(1)} %get-tuple-element.24.u_ref), custom_call_target="tpu_custom_call" | custom-call | flops 1000000 | bytes 1048576 | tf_op jit(solution)/shard_map/finish/pallas_call | solution.py:416
  (1 shorter events, 0.0 us)
Async XLA Ops:
  0.6 1.2 %copy-start = (f32[8,8,32,128]{3,2,1,0:T(8,128)S(1)}, f32[8,8,32,128]{3,2,1,0:T(8,128)}, u32[]{:S(2)}) copy-start(f32[8,8,32,128]{3,2,1,0:T(8,128)} %b_ref.3) | copy-start | bytes 3145732
  1.9 3.1 %copy-start.2 = (f32[8,32,128]{2,1,0:T(8,128)S(1)}, f32[8,32,128]{2,1,0:T(8,128)}, u32[]{:S(2)}) copy-start(f32[8,32,128]{2,1,0:T(8,128)} %shift_ref.9) | copy-start | bytes 393220
  1.9 8.6 %collective-permute-start.3 = (f32[32,8,128]{2,1,0:T(8,128)S(1)}, f32[32,8,128]{2,1,0:T(8,128)S(1)}, u32[]{:S(2)}, u32[]{:S(2)}) collective-permute-start(f32[32,8,128]{2,1,0:T(8,128)S(1)} %get-tuple-element.22), channel_id=1, source_target_pairs={{0,8},{4,12},{8,0},{12,4},{16,24},{20,28},{24,16},{28,20},{1,9},{5... | collective-permute-start | bytes 393224 | tf_op jit(solution)/shard_map/turn1_gx_0/ppermute | solution.py:31
  4.9 5.5 %collective-permute-start.4 = (f32[32,8,128]{2,1,0:T(8,128)S(1)}, f32[32,8,128]{2,1,0:T(8,128)S(1)}, u32[]{:S(2)}, u32[]{:S(2)}) collective-permute-start(f32[32,8,128]{2,1,0:T(8,128)S(1)} %get-tuple-element.23), channel_id=1, source_target_pairs={{8,16},{12,20},{16,8},{20,12},{0,4},{4,0},{24,28},{28,24},{9,17},{... | collective-permute-start | bytes 393224 | tf_op jit(solution)/shard_map/turn1_gx_1/ppermute | solution.py:31
  5.3 4.4 %collective-permute-start = (f32[8,8,1,128]{3,2,1,0:T(1,128)S(1)}, f32[8,8,1,128]{3,2,1,0:T(1,128)S(1)}, u32[]{:S(2)}, u32[]{:S(2)}) collective-permute-start(f32[8,8,1,128]{3,2,1,0:T(1,128)S(1)} %get-tuple-element.17), channel_id=1, source_target_pairs={{0,4},{4,0},{1,5},{5,1},{2,6},{6,2},{3,7},{7,3},{8,12},{12,8},{9,1... | collective-permute-start | bytes 98312 | tf_op jit(solution)/shard_map/turn1_gy_0/ppermute | solution.py:25
  5.9 3.8 %collective-permute-start.1 = (f32[5,8,128]{2,1,0:T(8,128)S(1)}, f32[5,8,128]{2,1,0:T(8,128)S(1)}, u32[]{:S(2)}, u32[]{:S(2)}) collective-permute-start(f32[5,8,128]{2,1,0:T(8,128)S(1)} %get-tuple-element.18), channel_id=1, source_target_pairs={{0,1},{4,5},{1,0},{5,4},{2,3},{6,7},{3,2},{7,6},{8,9},{12,13},{9,8... | collective-permute-start | bytes 61448 | tf_op jit(solution)/shard_map/turn1_gz_0/ppermute | solution.py:31
  7.5 2.2 %collective-permute-start.2 = (f32[5,8,128]{2,1,0:T(8,128)S(1)}, f32[5,8,128]{2,1,0:T(8,128)S(1)}, u32[]{:S(2)}, u32[]{:S(2)}) collective-permute-start(f32[5,8,128]{2,1,0:T(8,128)S(1)} %get-tuple-element.19), channel_id=1, source_target_pairs={{1,2},{5,6},{2,1},{6,5},{0,4},{4,0},{3,7},{7,3},{9,10},{13,14},{10... | collective-permute-start | bytes 61448 | tf_op jit(solution)/shard_map/turn1_gz_1/ppermute | solution.py:31
  10.8 7.7 %collective-permute-start.6 = (f32[33,8,128]{2,1,0:T(8,128)S(1)}, f32[33,8,128]{2,1,0:T(8,128)S(1)}, u32[]{:S(2)}, u32[]{:S(2)}) collective-permute-start(f32[33,8,128]{2,1,0:T(8,128)S(1)} %get-tuple-element.26), channel_id=1, source_target_pairs={{0,8},{4,12},{8,0},{12,4},{16,24},{20,28},{24,16},{28,20},{1,9},{5... | collective-permute-start | bytes 405512 | tf_op jit(solution)/shard_map/turn2_gx_0/ppermute | solution.py:31
  14.3 4.2 %collective-permute-start.7 = (f32[33,8,128]{2,1,0:T(8,128)S(1)}, f32[33,8,128]{2,1,0:T(8,128)S(1)}, u32[]{:S(2)}, u32[]{:S(2)}) collective-permute-start(f32[33,8,128]{2,1,0:T(8,128)S(1)} %get-tuple-element.27), channel_id=1, source_target_pairs={{8,16},{12,20},{16,8},{20,12},{0,4},{4,0},{24,28},{28,24},{9,17},{... | collective-permute-start | bytes 405512 | tf_op jit(solution)/shard_map/turn2_gx_1/ppermute | solution.py:31
  14.3 1.9 %collective-permute-start.5 = (f32[9,8,1,128]{3,2,1,0:T(1,128)S(1)}, f32[9,8,1,128]{3,2,1,0:T(1,128)S(1)}, u32[]{:S(2)}, u32[]{:S(2)}) collective-permute-start(f32[9,8,1,128]{3,2,1,0:T(1,128)S(1)} %get-tuple-element.25), channel_id=1, source_target_pairs={{0,4},{4,0},{1,5},{5,1},{2,6},{6,2},{3,7},{7,3},{8,12},{12,8},{9,1... | collective-permute-start | bytes 110600 | tf_op jit(solution)/shard_map/turn2_gy_0/ppermute | solution.py:25
  17.4 15.3 %copy-start.1 = (f32[8,8,32,128]{3,2,1,0:T(8,128)S(1)}, f32[8,8,32,128]{3,2,1,0:T(8,128)}, u32[]{:S(2)}) copy-start(f32[8,8,32,128]{3,2,1,0:T(8,128)} %b_ref.3) | copy-start | bytes 3145732

commit v13 on v12

--- a/solution.py
+++ b/solution.py
@@ -212,23 +212,24 @@
     return (0, ref.shape[1] - 1)
 
 
-def inner_operator_kernel(ny_r, nz_r, v_ref, shift_ref, own_ref, *refs):
-    y_in, z_in, (out_ref, ends_ref) = split(refs, ny_r, nz_r)
-    near, base = operator_on_ends(v_ref.shape[1], v_ref.shape[0], own_ref[...], z_in)
+def outer_operator_kernel(nx_r, ny_r, nz_r, v_ref, shift_ref, own_ref, *refs):
+    x_in, y_in, z_in, (out_ref, ends_ref), x_out = split(refs, nx_r, ny_r, nz_r, 2)
+    width, nx, ny, _ = v_ref.shape
+    near, base = operator_on_ends(nx, width, own_ref[...], z_in)
     ends_ref[0] = near
     ends_ref[1] = base
-    apply_operator(inner_planes(v_ref), v_ref, shift_ref, (), y_in, near, out_ref)
-
-
-def outer_operator_kernel(nx_r, ny_r, v_ref, shift_ref, inner_ref, ends_ref, *refs):
-    x_in, y_in, (out_ref,), x_out, y_out = split(refs, nx_r, ny_r, 1, nx_r)
-    width, nx, ny, _ = v_ref.shape
-    near = ends_ref[0]
     apply_operator(outer_planes(v_ref), v_ref, shift_ref, x_in, y_in, near, out_ref)
     for k, ref in enumerate(x_out):
         plane, rows = x_plane(k, nx), width * ny // 8
         ref[:rows] = out_ref[:, plane].reshape(rows, 8, LANES)
         ref[rows] = fold_plane(near, plane, nx)
+
+
+def inner_operator_kernel(ny_r, v_ref, shift_ref, outer_ref, ends_ref, *refs):
+    y_in, (out_ref,), y_out = split(refs, ny_r, 1)
+    width, nx, ny, _ = v_ref.shape
+    near = ends_ref[0]
+    apply_operator(inner_planes(v_ref), v_ref, shift_ref, (), y_in, near, out_ref)
     write_y_faces(out_ref, [ref.at[:width] for ref in y_out])
     for k, ref in enumerate(y_out):
         high = jnp.logical_xor(parity("gy"), k == 0)
@@ -465,22 +466,22 @@
     )
     halo_y, own = trade(1, "gy", packed[:ny_r]), packed[ny_r]
     halo_z = trade(1, "gz", packed[ny_r + 1 :])
-    inner, ends = call(
-        kernel(inner_operator_kernel, ny_r, nz_r),
-        [block, ends_of(2)],
-        [right_side, shift, own, *halo_y, *halo_z],
+    outer, ends, *faces = call(
+        kernel(outer_operator_kernel, nx_r, ny_r, nz_r),
+        [block, ends_of(2), *x_faces(1)],
+        [right_side, shift, own, *halo_x, *halo_y, *halo_z],
+        name="outer1",
+    )
+    halo_x = trade(2, "gx", faces)
+    u, *faces = call(
+        kernel(inner_operator_kernel, ny_r),
+        [block, *y_faces(width + 1)],
+        [right_side, shift, outer, ends, *halo_y],
+        aliases={2: 0},
         flops=20_000_000,
         name="inner1",
     )
-    u, *faces = call(
-        kernel(outer_operator_kernel, nx_r, ny_r),
-        [block, *x_faces(1), *y_faces(width + 1)],
-        [right_side, shift, inner, ends, *halo_x, *halo_y],
-        aliases={2: 0},
-        name="outer1",
-    )
-    halo_x = trade(2, "gx", faces[:nx_r])
-    halo_y = trade(2, "gy", faces[nx_r:])
+    halo_y = trade(2, "gy", faces)
     early = call(early_moments_kernel, jax.ShapeDtypeStruct((8, LANES), F32), [right_side, u], flops=15_000_000, name="early")
     sums = call(
         kernel(inner_late_kernel, ny_r),

time: 35.9 us -> 36 us (level)
  waiting for transfers between devices: 3.27 us -> 2.45 us
  starting transfers between devices: 9.21 us -> 10 us
    ppermute x6, waiting for transfers between devices: 3.27 us -> 2.44 us  [swap(): lax.ppermute(values, ('gx', 'gy') if axis == 'gx' else ('gy', 'gz'), joint)]
    ppermute x6, starting transfers between devices: 8.13 us -> 8.87 us  [swap(): lax.ppermute(values, ('gx', 'gy') if axis == 'gx' else ('gy', 'gz'), joint)]
where the time goes in v13:
time: 36 us; the launch traced here: 35.8 us
  blocking collectives  13.6 us (38%)
  starting transfers between devices  10 us (28%)
  Pallas kernels  7.77 us (22%)
  waiting for transfers between devices  2.45 us (7%)
  local copies, waits for them, and re-layouts  1.23 us (3%)
  between operations  0.7 us (2%)
    all_to_all x1, blocking collectives, body(): parts = lax.all_to_all(copies, AXES, 0, 0, tiled=True)  13.6 us
    ppermute x6, starting transfers between devices, swap(): lax.ppermute(values, ('gx', 'gy') if axis == 'gx' else ('gy', 'gz'), joint)  8.87 us
    pallas_call x8, Pallas kernels, call(): pl.pallas_call(kernel, out_shape=out_shape, in_specs=[pl.BlockSpec(memory...  7.77 us
    ppermute x6, waiting for transfers between devices, swap(): lax.ppermute(values, ('gx', 'gy') if axis == 'gx' else ('gy', 'gz'), joint)  2.44 us
    unnamed x6, local copies, waits for them, and re-layouts  1.23 us
    ppermute x2, starting transfers between devices, swap(): return lax.ppermute(values, axis, pairs)  1.14 us
  transfers between devices with their start and end apart: 8, of which 2 were waited for; matrix products, arithmetic and copies ran while one was open for 0% of the time, Pallas kernels for 10%

profile of v13, /device:TPU:0, one launch (start us, length us, event | category | flops | bytes accessed | tf_op | source)
XLA Modules:
  0.0 35.8 jit_solution(2108294466938941448)
XLA Ops:
  0.6 0.0 copy-start
  0.6 1.2 %copy-done = f32[8,8,32,128]{3,2,1,0:T(8,128)S(1)} copy-done((f32[8,8,32,128]{3,2,1,0:T(8,128)S(1)}, f32[8,8,32,128]{3,2,1,0:T(8,128)}, u32[]{:S(2)}) %copy-start) | copy-done | bytes 1048600
  1.9 0.0 copy-start.2
  1.9 3.0 %collective-permute-start = (f32[32,8,128]{2,1,0:T(8,128)S(1)}, f32[32,8,128]{2,1,0:T(8,128)S(1)}, u32[]{:S(2)}, u32[]{:S(2)}) collective-permute-start(f32[32,8,128]{2,1,0:T(8,128)S(1)} %get-tuple-element.17), channel_id=1, source_target_pairs={{0,8},{4,12},{8,0},{12,4},{16,24},{20,28},{24,16},{28,20},{1,9},{5... | collective-permute-start | bytes 393224 | tf_op jit(solution)/shard_map/turn1_gx_0/ppermute | solution.py:31
  4.9 0.0 collective-permute-start.1
  4.9 0.0 copy-done.2
  4.9 0.4 %pack.1 = (f32[8,8,1,128]{3,2,1,0:T(1,128)S(1)}, f32[32,128]{1,0:T(8,128)S(1)}, f32[5,8,128]{2,1,0:T(8,128)S(1)}, f32[5,8,128]{2,1,0:T(8,128)S(1)}) custom-call(f32[8,8,32,128]{3,2,1,0:T(8,128)S(1)} %copy-done, f32[8,32,128]{2,1,0:T(8,128)S(1)} %copy-done.2), custom_call_target="tpu_custom_call" | custom-call | flops 1000000 | bytes 1048576 | tf_op jit(solution)/shard_map/pack/pallas_call | solution.py:417
  5.3 0.6 %collective-permute-start.2 = (f32[8,8,1,128]{3,2,1,0:T(1,128)S(1)}, f32[8,8,1,128]{3,2,1,0:T(1,128)S(1)}, u32[]{:S(2)}, u32[]{:S(2)}) collective-permute-start(f32[8,8,1,128]{3,2,1,0:T(1,128)S(1)} %get-tuple-element.19), channel_id=1, source_target_pairs={{0,4},{4,0},{1,5},{5,1},{2,6},{6,2},{3,7},{7,3},{8,12},{12,8},{9,1... | collective-permute-start | bytes 98312 | tf_op jit(solution)/shard_map/turn1_gy_0/ppermute | solution.py:25
  5.9 1.6 %collective-permute-start.3 = (f32[5,8,128]{2,1,0:T(8,128)S(1)}, f32[5,8,128]{2,1,0:T(8,128)S(1)}, u32[]{:S(2)}, u32[]{:S(2)}) collective-permute-start(f32[5,8,128]{2,1,0:T(8,128)S(1)} %get-tuple-element.20), channel_id=1, source_target_pairs={{0,1},{4,5},{1,0},{5,4},{2,3},{6,7},{3,2},{7,6},{8,9},{12,13},{9,8... | collective-permute-start | bytes 61448 | tf_op jit(solution)/shard_map/turn1_gz_0/ppermute | solution.py:31
  7.5 0.0 collective-permute-start.4
  7.5 2.2 %collective-permute-done.3.refs_3_ = f32[5,8,128]{2,1,0:T(8,128)S(1)} collective-permute-done((f32[5,8,128]{2,1,0:T(8,128)S(1)}, f32[5,8,128]{2,1,0:T(8,128)S(1)}, u32[]{:S(2)}, u32[]{:S(2)}) %collective-permute-start.3) | collective-permute-done | bytes 20512 | tf_op jit(solution)/shard_map/turn1_gz_0/ppermute | solution.py:31
  9.7 0.0 collective-permute-done.4.refs_4_
  9.7 0.0 collective-permute-done.2.refs_2_.refs_0_
  9.7 0.0 collective-permute-done.refs_0_
  9.7 0.0 collective-permute-done.1.refs_1_
  9.7 0.4 %outer1.1 = (f32[8,8,32,128]{3,2,1,0:T(8,128)S(1)}, f32[2,32,128]{2,1,0:T(8,128)S(1)}, f32[33,8,128]{2,1,0:T(8,128)S(1)}, f32[33,8,128]{2,1,0:T(8,128)S(1)}) custom-call(f32[8,8,32,128]{3,2,1,0:T(8,128)S(1)} %copy-done, f32[8,32,128]{2,1,0:T(8,128)S(1)} %copy-done.2, f32[32,128]{1,0:T(8,128)S(1)} %get-tuple-element.16.own_ref, ...), custom_call_target="tpu_custom_call" | custom-call | flops 1000000 | bytes 1048576 | tf_op jit(solution)/shard_map/outer1/pallas_call | solution.py:417
  10.1 4.2 %collective-permute-start.6 = (f32[33,8,128]{2,1,0:T(8,128)S(1)}, f32[33,8,128]{2,1,0:T(8,128)S(1)}, u32[]{:S(2)}, u32[]{:S(2)}) collective-permute-start(f32[33,8,128]{2,1,0:T(8,128)S(1)} %get-tuple-element.26), channel_id=1, source_target_pairs={{0,8},{4,12},{8,0},{12,4},{16,24},{20,28},{24,16},{28,20},{1,9},{5... | collective-permute-start | bytes 405512 | tf_op jit(solution)/shard_map/turn2_gx_0/ppermute | solution.py:31
  14.4 0.0 collective-permute-start.7
  14.4 0.8 %inner1.1 = (f32[8,8,32,128]{3,2,1,0:T(8,128)S(1)}, f32[9,8,1,128]{3,2,1,0:T(1,128)S(1)}) custom-call(f32[8,8,32,128]{3,2,1,0:T(8,128)S(1)} %copy-done, f32[8,32,128]{2,1,0:T(8,128)S(1)} %copy-done.2, f32[8,8,32,128]{3,2,1,0:T(8,128)S(1)} %get-tuple-element.22.outer_ref, ...), custom_call_target="tpu_custom_call", output_to_operand_aliasing={{0}: (2, {})} | custom-call | flops 20000000 | bytes 1048576 | tf_op jit(solution)/shard_map/inner1/pallas_call | solution.py:417
  15.1 0.6 %collective-permute-start.5 = (f32[9,8,1,128]{3,2,1,0:T(1,128)S(1)}, f32[9,8,1,128]{3,2,1,0:T(1,128)S(1)}, u32[]{:S(2)}, u32[]{:S(2)}) collective-permute-start(f32[9,8,1,128]{3,2,1,0:T(1,128)S(1)} %get-tuple-element.25), channel_id=1, source_target_pairs={{0,4},{4,0},{1,5},{5,1},{2,6},{6,2},{3,7},{7,3},{8,12},{12,8},{9,1... | collective-permute-start | bytes 110600 | tf_op jit(solution)/shard_map/turn2_gy_0/ppermute | solution.py:25
  15.7 1.4 %early.1.early_ref = f32[8,128]{1,0:T(8,128)S(1)} custom-call(f32[8,8,32,128]{3,2,1,0:T(8,128)S(1)} %copy-done, f32[8,8,32,128]{3,2,1,0:T(8,128)S(1)} %get-tuple-element.24.u_ref), custom_call_target="tpu_custom_call" | custom-call | flops 15000000 | bytes 1048576 | tf_op jit(solution)/shard_map/early/pallas_call | solution.py:417
  17.1 0.0 collective-permute-done.5.refs_0_.refs_2_
  17.1 1.2 %inner2.1.sums_ref = f32[2,36,8,128]{3,2,1,0:T(8,128)S(1)} custom-call(f32[8,8,32,128]{3,2,1,0:T(8,128)S(1)} %get-tuple-element.24.u_ref, f32[8,32,128]{2,1,0:T(8,128)S(1)} %copy-done.2, f32[2,32,128]{2,1,0:T(8,128)S(1)} %get-tuple-element.23.ends_ref, f32[9,8,1,128]{3,2,1,0:T(1,128)S(1)} %collective-permute-done.5.refs_0_.refs_2_), custom_call_target="tpu_custom_call" | custom-call | flops 15000000 | bytes 1048576 | tf_op jit(solution)/shard_map/inner2/pallas_call | solution.py:417
  18.3 0.0 copy-start.1
  18.3 0.2 collective-permute-done.6.refs_0_
  18.5 0.0 collective-permute-done.7.refs_1_
  18.5 0.7 %outer2.1 = f32[32,4,128]{2,1,0:T(4,128)S(1)} custom-call(f32[8,8,32,128]{3,2,1,0:T(8,128)S(1)} %get-tuple-element.24.u_ref, f32[8,32,128]{2,1,0:T(8,128)S(1)} %copy-done.2, f32[2,32,128]{2,1,0:T(8,128)S(1)} %get-tuple-element.23.ends_ref, f32[2,36,8,128]{3,2,1,0:T(8,128)S(1)} %inner2.1.sums_ref, f32[8,128]{1,0:T(8,128)S(1)} %early.1.early_ref, ...), custom_call_target="tpu_custom_call" | custom-call | flops 1000000 | bytes 1048576 | tf_op jit(solution)/shard_map/outer2/pallas_call | solution.py:417
  19.2 13.6 %all_to_all.5.parts_ref = f32[32,4,128]{2,1,0:T(4,128)S(1)} all-to-all(f32[32,4,128]{2,1,0:T(4,128)S(1)} %outer2.1), channel_id=1, replica_groups=mesh['gx'=4,'gy'=2,'gz'=4] {'gx','gy','gz'}, dimensions={0} | all-to-all | bytes 131072 | tf_op jit(solution)/shard_map/all_to_all | solution.py:501
  32.8 0.0 copy-done.1
  32.8 2.9 %finish.1 = (f32[8,8,32,128]{3,2,1,0:T(8,128)}, f32[1,8]{1,0:T(1,128)}) custom-call(f32[32,4,128]{2,1,0:T(4,128)S(1)} %all_to_all.5.parts_ref, f32[8,8,32,128]{3,2,1,0:T(8,128)S(1)} %copy-done.1, f32[8,8,32,128]{3,2,1,0:T(8,128)S(1)} %get-tuple-element.24.u_ref), custom_call_target="tpu_custom_call" | custom-call | flops 1000000 | bytes 1048576 | tf_op jit(solution)/shard_map/finish/pallas_call | solution.py:417
  (1 shorter events, 0.0 us)
Async XLA Ops:
  0.6 1.2 %copy-start = (f32[8,8,32,128]{3,2,1,0:T(8,128)S(1)}, f32[8,8,32,128]{3,2,1,0:T(8,128)}, u32[]{:S(2)}) copy-start(f32[8,8,32,128]{3,2,1,0:T(8,128)} %b_ref.3) | copy-start | bytes 3145732
  1.9 3.1 %copy-start.2 = (f32[8,32,128]{2,1,0:T(8,128)S(1)}, f32[8,32,128]{2,1,0:T(8,128)}, u32[]{:S(2)}) copy-start(f32[8,32,128]{2,1,0:T(8,128)} %shift_ref.9) | copy-start | bytes 393220
  1.9 7.8 %collective-permute-start = (f32[32,8,128]{2,1,0:T(8,128)S(1)}, f32[32,8,128]{2,1,0:T(8,128)S(1)}, u32[]{:S(2)}, u32[]{:S(2)}) collective-permute-start(f32[32,8,128]{2,1,0:T(8,128)S(1)} %get-tuple-element.17), channel_id=1, source_target_pairs={{0,8},{4,12},{8,0},{12,4},{16,24},{20,28},{24,16},{28,20},{1,9},{5... | collective-permute-start | bytes 393224 | tf_op jit(solution)/shard_map/turn1_gx_0/ppermute | solution.py:31
  4.9 4.8 %collective-permute-start.1 = (f32[32,8,128]{2,1,0:T(8,128)S(1)}, f32[32,8,128]{2,1,0:T(8,128)S(1)}, u32[]{:S(2)}, u32[]{:S(2)}) collective-permute-start(f32[32,8,128]{2,1,0:T(8,128)S(1)} %get-tuple-element.18), channel_id=1, source_target_pairs={{8,16},{12,20},{16,8},{20,12},{0,4},{4,0},{24,28},{28,24},{9,17},{... | collective-permute-start | bytes 393224 | tf_op jit(solution)/shard_map/turn1_gx_1/ppermute | solution.py:31
  5.3 4.4 %collective-permute-start.2 = (f32[8,8,1,128]{3,2,1,0:T(1,128)S(1)}, f32[8,8,1,128]{3,2,1,0:T(1,128)S(1)}, u32[]{:S(2)}, u32[]{:S(2)}) collective-permute-start(f32[8,8,1,128]{3,2,1,0:T(1,128)S(1)} %get-tuple-element.19), channel_id=1, source_target_pairs={{0,4},{4,0},{1,5},{5,1},{2,6},{6,2},{3,7},{7,3},{8,12},{12,8},{9,1... | collective-permute-start | bytes 98312 | tf_op jit(solution)/shard_map/turn1_gy_0/ppermute | solution.py:25
  5.9 3.8 %collective-permute-start.3 = (f32[5,8,128]{2,1,0:T(8,128)S(1)}, f32[5,8,128]{2,1,0:T(8,128)S(1)}, u32[]{:S(2)}, u32[]{:S(2)}) collective-permute-start(f32[5,8,128]{2,1,0:T(8,128)S(1)} %get-tuple-element.20), channel_id=1, source_target_pairs={{0,1},{4,5},{1,0},{5,4},{2,3},{6,7},{3,2},{7,6},{8,9},{12,13},{9,8... | collective-permute-start | bytes 61448 | tf_op jit(solution)/shard_map/turn1_gz_0/ppermute | solution.py:31
  7.5 2.2 %collective-permute-start.4 = (f32[5,8,128]{2,1,0:T(8,128)S(1)}, f32[5,8,128]{2,1,0:T(8,128)S(1)}, u32[]{:S(2)}, u32[]{:S(2)}) collective-permute-start(f32[5,8,128]{2,1,0:T(8,128)S(1)} %get-tuple-element.21), channel_id=1, source_target_pairs={{1,2},{5,6},{2,1},{6,5},{0,4},{4,0},{3,7},{7,3},{9,10},{13,14},{10... | collective-permute-start | bytes 61448 | tf_op jit(solution)/shard_map/turn1_gz_1/ppermute | solution.py:31
  10.1 8.4 %collective-permute-start.6 = (f32[33,8,128]{2,1,0:T(8,128)S(1)}, f32[33,8,128]{2,1,0:T(8,128)S(1)}, u32[]{:S(2)}, u32[]{:S(2)}) collective-permute-start(f32[33,8,128]{2,1,0:T(8,128)S(1)} %get-tuple-element.26), channel_id=1, source_target_pairs={{0,8},{4,12},{8,0},{12,4},{16,24},{20,28},{24,16},{28,20},{1,9},{5... | collective-permute-start | bytes 405512 | tf_op jit(solution)/shard_map/turn2_gx_0/ppermute | solution.py:31
  14.4 4.2 %collective-permute-start.7 = (f32[33,8,128]{2,1,0:T(8,128)S(1)}, f32[33,8,128]{2,1,0:T(8,128)S(1)}, u32[]{:S(2)}, u32[]{:S(2)}) collective-permute-start(f32[33,8,128]{2,1,0:T(8,128)S(1)} %get-tuple-element.27), channel_id=1, source_target_pairs={{8,16},{12,20},{16,8},{20,12},{0,4},{4,0},{24,28},{28,24},{9,17},{... | collective-permute-start | bytes 405512 | tf_op jit(solution)/shard_map/turn2_gx_1/ppermute | solution.py:31
  15.1 1.9 %collective-permute-start.5 = (f32[9,8,1,128]{3,2,1,0:T(1,128)S(1)}, f32[9,8,1,128]{3,2,1,0:T(1,128)S(1)}, u32[]{:S(2)}, u32[]{:S(2)}) collective-permute-start(f32[9,8,1,128]{3,2,1,0:T(1,128)S(1)} %get-tuple-element.25), channel_id=1, source_target_pairs={{0,4},{4,0},{1,5},{5,1},{2,6},{6,2},{3,7},{7,3},{8,12},{12,8},{9,1... | collective-permute-start | bytes 110600 | tf_op jit(solution)/shard_map/turn2_gy_0/ppermute | solution.py:25
  18.3 14.5 %copy-start.1 = (f32[8,8,32,128]{3,2,1,0:T(8,128)S(1)}, f32[8,8,32,128]{3,2,1,0:T(8,128)}, u32[]{:S(2)}) copy-start(f32[8,8,32,128]{3,2,1,0:T(8,128)} %b_ref.3) | copy-start | bytes 3145732

commit v14 on v12

--- a/solution.py
+++ b/solution.py
@@ -409,7 +409,7 @@
 
         return lax.fori_loop(0, nx, plane, carry, unroll=nx)
 
-    lax.fori_loop(0, width // group, fields, 0)
+    lax.fori_loop(0, width // group, fields, 0, unroll=2)
 
 
 def call(kernel, out_shape, operands, scratch=(), flops=1_000_000, name=None, aliases=None):

time: 35.9 us -> 35.8 us (level)
  no operation moved by 1% of the time
where the time goes in v14:
time: 35.8 us; the launch traced here: 35.7 us
  blocking collectives  13.6 us (38%)
  starting transfers between devices  9.21 us (26%)
  Pallas kernels  7.65 us (21%)
  waiting for transfers between devices  3.27 us (9%)
  local copies, waits for them, and re-layouts  1.23 us (3%)
  between operations  0.71 us (2%)
    all_to_all x1, blocking collectives, body(): parts = lax.all_to_all(copies, AXES, 0, 0, tiled=True)  13.6 us
    ppermute x6, starting transfers between devices, swap(): lax.ppermute(values, ('gx', 'gy') if axis == 'gx' else ('gy', 'gz'), joint)  8.13 us
    pallas_call x8, Pallas kernels, call(): pl.pallas_call(kernel, out_shape=out_shape, in_specs=[pl.BlockSpec(memory...  7.65 us
    ppermute x6, waiting for transfers between devices, swap(): lax.ppermute(values, ('gx', 'gy') if axis == 'gx' else ('gy', 'gz'), joint)  3.27 us
    unnamed x6, local copies, waits for them, and re-layouts  1.23 us
    ppermute x2, starting transfers between devices, swap(): return lax.ppermute(values, axis, pairs)  1.08 us
  transfers between devices with their start and end apart: 8, of which 2 were waited for; matrix products, arithmetic and copies ran while one was open for 0% of the time, Pallas kernels for 10%

profile of v14, /device:TPU:0, one launch (start us, length us, event | category | flops | bytes accessed | tf_op | source)
XLA Modules:
  0.0 35.7 jit_solution(9949512688303051231)
XLA Ops:
  0.6 0.0 copy-start
  0.6 1.2 %copy-done = f32[8,8,32,128]{3,2,1,0:T(8,128)S(1)} copy-done((f32[8,8,32,128]{3,2,1,0:T(8,128)S(1)}, f32[8,8,32,128]{3,2,1,0:T(8,128)}, u32[]{:S(2)}) %copy-start) | copy-done | bytes 1048600
  1.9 0.0 copy-start.2
  1.9 3.0 %collective-permute-start.3 = (f32[32,8,128]{2,1,0:T(8,128)S(1)}, f32[32,8,128]{2,1,0:T(8,128)S(1)}, u32[]{:S(2)}, u32[]{:S(2)}) collective-permute-start(f32[32,8,128]{2,1,0:T(8,128)S(1)} %get-tuple-element.22), channel_id=1, source_target_pairs={{0,8},{4,12},{8,0},{12,4},{16,24},{20,28},{24,16},{28,20},{1,9},{5... | collective-permute-start | bytes 393224 | tf_op jit(solution)/shard_map/turn1_gx_0/ppermute | solution.py:31
  4.9 0.0 collective-permute-start.4
  4.9 0.0 copy-done.2
  4.9 0.4 %pack.1 = (f32[8,8,1,128]{3,2,1,0:T(1,128)S(1)}, f32[32,128]{1,0:T(8,128)S(1)}, f32[5,8,128]{2,1,0:T(8,128)S(1)}, f32[5,8,128]{2,1,0:T(8,128)S(1)}) custom-call(f32[8,8,32,128]{3,2,1,0:T(8,128)S(1)} %copy-done, f32[8,32,128]{2,1,0:T(8,128)S(1)} %copy-done.2), custom_call_target="tpu_custom_call" | custom-call | flops 1000000 | bytes 1048576 | tf_op jit(solution)/shard_map/pack/pallas_call | solution.py:416
  5.3 0.6 %collective-permute-start = (f32[8,8,1,128]{3,2,1,0:T(1,128)S(1)}, f32[8,8,1,128]{3,2,1,0:T(1,128)S(1)}, u32[]{:S(2)}, u32[]{:S(2)}) collective-permute-start(f32[8,8,1,128]{3,2,1,0:T(1,128)S(1)} %get-tuple-element.17), channel_id=1, source_target_pairs={{0,4},{4,0},{1,5},{5,1},{2,6},{6,2},{3,7},{7,3},{8,12},{12,8},{9,1... | collective-permute-start | bytes 98312 | tf_op jit(solution)/shard_map/turn1_gy_0/ppermute | solution.py:25
  5.9 1.6 %collective-permute-start.1 = (f32[5,8,128]{2,1,0:T(8,128)S(1)}, f32[5,8,128]{2,1,0:T(8,128)S(1)}, u32[]{:S(2)}, u32[]{:S(2)}) collective-permute-start(f32[5,8,128]{2,1,0:T(8,128)S(1)} %get-tuple-element.18), channel_id=1, source_target_pairs={{0,1},{4,5},{1,0},{5,4},{2,3},{6,7},{3,2},{7,6},{8,9},{12,13},{9,8... | collective-permute-start | bytes 61448 | tf_op jit(solution)/shard_map/turn1_gz_0/ppermute | solution.py:31
  7.5 0.0 collective-permute-start.2
  7.5 2.2 %collective-permute-done.1.refs_1_ = f32[5,8,128]{2,1,0:T(8,128)S(1)} collective-permute-done((f32[5,8,128]{2,1,0:T(8,128)S(1)}, f32[5,8,128]{2,1,0:T(8,128)S(1)}, u32[]{:S(2)}, u32[]{:S(2)}) %collective-permute-start.1) | collective-permute-done | bytes 20512 | tf_op jit(solution)/shard_map/turn1_gz_0/ppermute | solution.py:31
  9.7 0.0 collective-permute-done.2.refs_2_
  9.7 0.0 collective-permute-done.refs_0_.refs_2_
  9.7 0.7 %inner1.1 = (f32[8,8,32,128]{3,2,1,0:T(8,128)S(1)}, f32[2,32,128]{2,1,0:T(8,128)S(1)}) custom-call(f32[8,8,32,128]{3,2,1,0:T(8,128)S(1)} %copy-done, f32[8,32,128]{2,1,0:T(8,128)S(1)} %copy-done.2, f32[32,128]{1,0:T(8,128)S(1)} %get-tuple-element.16.own_ref, f32[8,8,1,128]{3,2,1,0:T(1,128)S(1)} %collective-permute-done.refs_0_.refs_2_, ...), custom_call_target="tpu_custom_call" | custom-call | flops 20000000 | bytes 1048576 | tf_op jit(solution)/shard_map/inner1/pallas_call | solution.py:416
  10.4 0.0 collective-permute-done.3.refs_0_
  10.5 0.0 collective-permute-done.4.refs_1_
  10.5 0.3 outer1.1
  10.8 3.5 %collective-permute-start.6 = (f32[33,8,128]{2,1,0:T(8,128)S(1)}, f32[33,8,128]{2,1,0:T(8,128)S(1)}, u32[]{:S(2)}, u32[]{:S(2)}) collective-permute-start(f32[33,8,128]{2,1,0:T(8,128)S(1)} %get-tuple-element.26), channel_id=1, source_target_pairs={{0,8},{4,12},{8,0},{12,4},{16,24},{20,28},{24,16},{28,20},{1,9},{5... | collective-permute-start | bytes 405512 | tf_op jit(solution)/shard_map/turn2_gx_0/ppermute | solution.py:31
  14.3 0.0 collective-permute-start.7
  14.3 0.5 %collective-permute-start.5 = (f32[9,8,1,128]{3,2,1,0:T(1,128)S(1)}, f32[9,8,1,128]{3,2,1,0:T(1,128)S(1)}, u32[]{:S(2)}, u32[]{:S(2)}) collective-permute-start(f32[9,8,1,128]{3,2,1,0:T(1,128)S(1)} %get-tuple-element.25), channel_id=1, source_target_pairs={{0,4},{4,0},{1,5},{5,1},{2,6},{6,2},{3,7},{7,3},{8,12},{12,8},{9,1... | collective-permute-start | bytes 110600 | tf_op jit(solution)/shard_map/turn2_gy_0/ppermute | solution.py:25
  14.8 1.4 %early.1.early_ref = f32[8,128]{1,0:T(8,128)S(1)} custom-call(f32[8,8,32,128]{3,2,1,0:T(8,128)S(1)} %copy-done, f32[8,8,32,128]{3,2,1,0:T(8,128)S(1)} %get-tuple-element.24.u_ref), custom_call_target="tpu_custom_call" | custom-call | flops 15000000 | bytes 1048576 | tf_op jit(solution)/shard_map/early/pallas_call | solution.py:416
  16.2 0.0 collective-permute-done.5.refs_0_.refs_2_
  16.2 1.2 %inner2.1.sums_ref = f32[2,36,8,128]{3,2,1,0:T(8,128)S(1)} custom-call(f32[8,8,32,128]{3,2,1,0:T(8,128)S(1)} %get-tuple-element.24.u_ref, f32[8,32,128]{2,1,0:T(8,128)S(1)} %copy-done.2, f32[2,32,128]{2,1,0:T(8,128)S(1)} %get-tuple-element.21.ends_ref, f32[9,8,1,128]{3,2,1,0:T(1,128)S(1)} %collective-permute-done.5.refs_0_.refs_2_), custom_call_target="tpu_custom_call" | custom-call | flops 15000000 | bytes 1048576 | tf_op jit(solution)/shard_map/inner2/pallas_call | solution.py:416
  17.4 0.0 copy-start.1
  17.4 1.1 %collective-permute-done.6.refs_0_ = f32[33,8,128]{2,1,0:T(8,128)S(1)} collective-permute-done((f32[33,8,128]{2,1,0:T(8,128)S(1)}, f32[33,8,128]{2,1,0:T(8,128)S(1)}, u32[]{:S(2)}, u32[]{:S(2)}) %collective-permute-start.6) | collective-permute-done | bytes 135200 | tf_op jit(solution)/shard_map/turn2_gx_0/ppermute | solution.py:31
  18.5 0.0 collective-permute-done.7.refs_1_
  18.5 0.7 %outer2.1 = f32[32,4,128]{2,1,0:T(4,128)S(1)} custom-call(f32[8,8,32,128]{3,2,1,0:T(8,128)S(1)} %get-tuple-element.24.u_ref, f32[8,32,128]{2,1,0:T(8,128)S(1)} %copy-done.2, f32[2,32,128]{2,1,0:T(8,128)S(1)} %get-tuple-element.21.ends_ref, f32[2,36,8,128]{3,2,1,0:T(8,128)S(1)} %inner2.1.sums_ref, f32[8,128]{1,0:T(8,128)S(1)} %early.1.early_ref, ...), custom_call_target="tpu_custom_call" | custom-call | flops 1000000 | bytes 1048576 | tf_op jit(solution)/shard_map/outer2/pallas_call | solution.py:416
  19.1 13.6 %all_to_all.5.parts_ref = f32[32,4,128]{2,1,0:T(4,128)S(1)} all-to-all(f32[32,4,128]{2,1,0:T(4,128)S(1)} %outer2.1), channel_id=1, replica_groups=mesh['gx'=4,'gy'=2,'gz'=4] {'gx','gy','gz'}, dimensions={0} | all-to-all | bytes 131072 | tf_op jit(solution)/shard_map/all_to_all | solution.py:500
  32.8 0.0 copy-done.1
  32.8 2.9 %finish.1 = (f32[8,8,32,128]{3,2,1,0:T(8,128)}, f32[1,8]{1,0:T(1,128)}) custom-call(f32[32,4,128]{2,1,0:T(4,128)S(1)} %all_to_all.5.parts_ref, f32[8,8,32,128]{3,2,1,0:T(8,128)S(1)} %copy-done.1, f32[8,8,32,128]{3,2,1,0:T(8,128)S(1)} %get-tuple-element.24.u_ref), custom_call_target="tpu_custom_call" | custom-call | flops 1000000 | bytes 1048576 | tf_op jit(solution)/shard_map/finish/pallas_call | solution.py:416
  (1 shorter events, 0.0 us)
Async XLA Ops:
  0.6 1.2 %copy-start = (f32[8,8,32,128]{3,2,1,0:T(8,128)S(1)}, f32[8,8,32,128]{3,2,1,0:T(8,128)}, u32[]{:S(2)}) copy-start(f32[8,8,32,128]{3,2,1,0:T(8,128)} %b_ref.3) | copy-start | bytes 3145732
  1.9 3.1 %copy-start.2 = (f32[8,32,128]{2,1,0:T(8,128)S(1)}, f32[8,32,128]{2,1,0:T(8,128)}, u32[]{:S(2)}) copy-start(f32[8,32,128]{2,1,0:T(8,128)} %shift_ref.9) | copy-start | bytes 393220
  1.9 8.6 %collective-permute-start.3 = (f32[32,8,128]{2,1,0:T(8,128)S(1)}, f32[32,8,128]{2,1,0:T(8,128)S(1)}, u32[]{:S(2)}, u32[]{:S(2)}) collective-permute-start(f32[32,8,128]{2,1,0:T(8,128)S(1)} %get-tuple-element.22), channel_id=1, source_target_pairs={{0,8},{4,12},{8,0},{12,4},{16,24},{20,28},{24,16},{28,20},{1,9},{5... | collective-permute-start | bytes 393224 | tf_op jit(solution)/shard_map/turn1_gx_0/ppermute | solution.py:31
  4.9 5.5 %collective-permute-start.4 = (f32[32,8,128]{2,1,0:T(8,128)S(1)}, f32[32,8,128]{2,1,0:T(8,128)S(1)}, u32[]{:S(2)}, u32[]{:S(2)}) collective-permute-start(f32[32,8,128]{2,1,0:T(8,128)S(1)} %get-tuple-element.23), channel_id=1, source_target_pairs={{8,16},{12,20},{16,8},{20,12},{0,4},{4,0},{24,28},{28,24},{9,17},{... | collective-permute-start | bytes 393224 | tf_op jit(solution)/shard_map/turn1_gx_1/ppermute | solution.py:31
  5.3 4.4 %collective-permute-start = (f32[8,8,1,128]{3,2,1,0:T(1,128)S(1)}, f32[8,8,1,128]{3,2,1,0:T(1,128)S(1)}, u32[]{:S(2)}, u32[]{:S(2)}) collective-permute-start(f32[8,8,1,128]{3,2,1,0:T(1,128)S(1)} %get-tuple-element.17), channel_id=1, source_target_pairs={{0,4},{4,0},{1,5},{5,1},{2,6},{6,2},{3,7},{7,3},{8,12},{12,8},{9,1... | collective-permute-start | bytes 98312 | tf_op jit(solution)/shard_map/turn1_gy_0/ppermute | solution.py:25
  5.9 3.8 %collective-permute-start.1 = (f32[5,8,128]{2,1,0:T(8,128)S(1)}, f32[5,8,128]{2,1,0:T(8,128)S(1)}, u32[]{:S(2)}, u32[]{:S(2)}) collective-permute-start(f32[5,8,128]{2,1,0:T(8,128)S(1)} %get-tuple-element.18), channel_id=1, source_target_pairs={{0,1},{4,5},{1,0},{5,4},{2,3},{6,7},{3,2},{7,6},{8,9},{12,13},{9,8... | collective-permute-start | bytes 61448 | tf_op jit(solution)/shard_map/turn1_gz_0/ppermute | solution.py:31
  7.5 2.2 %collective-permute-start.2 = (f32[5,8,128]{2,1,0:T(8,128)S(1)}, f32[5,8,128]{2,1,0:T(8,128)S(1)}, u32[]{:S(2)}, u32[]{:S(2)}) collective-permute-start(f32[5,8,128]{2,1,0:T(8,128)S(1)} %get-tuple-element.19), channel_id=1, source_target_pairs={{1,2},{5,6},{2,1},{6,5},{0,4},{4,0},{3,7},{7,3},{9,10},{13,14},{10... | collective-permute-start | bytes 61448 | tf_op jit(solution)/shard_map/turn1_gz_1/ppermute | solution.py:31
  10.8 7.7 %collective-permute-start.6 = (f32[33,8,128]{2,1,0:T(8,128)S(1)}, f32[33,8,128]{2,1,0:T(8,128)S(1)}, u32[]{:S(2)}, u32[]{:S(2)}) collective-permute-start(f32[33,8,128]{2,1,0:T(8,128)S(1)} %get-tuple-element.26), channel_id=1, source_target_pairs={{0,8},{4,12},{8,0},{12,4},{16,24},{20,28},{24,16},{28,20},{1,9},{5... | collective-permute-start | bytes 405512 | tf_op jit(solution)/shard_map/turn2_gx_0/ppermute | solution.py:31
  14.3 4.2 %collective-permute-start.7 = (f32[33,8,128]{2,1,0:T(8,128)S(1)}, f32[33,8,128]{2,1,0:T(8,128)S(1)}, u32[]{:S(2)}, u32[]{:S(2)}) collective-permute-start(f32[33,8,128]{2,1,0:T(8,128)S(1)} %get-tuple-element.27), channel_id=1, source_target_pairs={{8,16},{12,20},{16,8},{20,12},{0,4},{4,0},{24,28},{28,24},{9,17},{... | collective-permute-start | bytes 405512 | tf_op jit(solution)/shard_map/turn2_gx_1/ppermute | solution.py:31
  14.3 1.9 %collective-permute-start.5 = (f32[9,8,1,128]{3,2,1,0:T(1,128)S(1)}, f32[9,8,1,128]{3,2,1,0:T(1,128)S(1)}, u32[]{:S(2)}, u32[]{:S(2)}) collective-permute-start(f32[9,8,1,128]{3,2,1,0:T(1,128)S(1)} %get-tuple-element.25), channel_id=1, source_target_pairs={{0,4},{4,0},{1,5},{5,1},{2,6},{6,2},{3,7},{7,3},{8,12},{12,8},{9,1... | collective-permute-start | bytes 110600 | tf_op jit(solution)/shard_map/turn2_gy_0/ppermute | solution.py:25
  17.4 15.3 %copy-start.1 = (f32[8,8,32,128]{3,2,1,0:T(8,128)S(1)}, f32[8,8,32,128]{3,2,1,0:T(8,128)}, u32[]{:S(2)}) copy-start(f32[8,8,32,128]{3,2,1,0:T(8,128)} %b_ref.3) | copy-start | bytes 3145732
